TPU v7x, 256 devices: a whole 4x4x8 slice. The times are simulated.
256 devices in a mesh: img: 16 (over y, x_hi, core), ori: 8 (over z), slab: 2 (over x_lo).
Axes of the slice: x: 4 (x_hi: 2, x_lo: 2; x = x_hi * 2 + x_lo), y: 4, z: 8, core: 2. Of those that a mesh axis runs over, the one named last changes fastest.
Arguments:
- images: bfloat16 [3072, 160, 256], P('img', 'slab'), may hold values from -6 to 6
- noise_weight: float32 [160, 128], P('slab'), may hold values from 0.5 to 200
- prior_mask: int32 [3072, 1536], P('img', 'ori'), may hold values from 0 to 1, as said below
- volume: bfloat16 [128, 4, 256], P(None, 'slab'), may hold values from -0.046875 to 0.046875
- interp_weights: bfloat16 [1536, 96, 512], P(('ori', 'img'), None, 'slab'), may hold values from -1.5 to 1.5
- row_first: int32 [1536, 2], P(('ori', 'img'), 'slab'), may hold values from 0 to 112, as said below
- row_count: int32 [1536, 2], P(('ori', 'img'), 'slab'), may hold values from 48 to 96, as said below
Outputs:
- log_evidence: float32 [3072], P('img')
- inserted: float32 [128, 4, 256], P(('img', 'ori'), 'slab')
Inputs may be any that keep to these rules, and one draw needn't show every extreme that they name: `prior_mask`: every image allows at least one orientation. row_first + row_count <= 160. `row_count`: the first slice reaches 96 rows on every slab.
All inputs are finite; a program needn't handle non-finite values.
Results may differ from a plain program's by a relative error of at most 0.013.
Values may be sent and summed in bfloat16 or wider, within the bound.
No kernel may reach another device: no remote copies, remote signals or barrier semaphores. Data moves between devices by JAX's collectives and lax.ppermute only.
A program may use at most 128 MiB of HBM per device.

v0:
```python
from functools import partial

import jax
import jax.numpy as jnp
from jax import lax
from jax.sharding import Mesh
from jax.sharding import PartitionSpec as P

IMG = ("img_0", "img_1", "img_2")
IMG_ORI = ("img_0", "img_1", "img_2", "ori")
ORI_IMG = ("ori", "img_0", "img_1", "img_2")


def cut_along(shard, dim, peers):
    before, after = (shard.shape[:dim], shard.shape[dim + 1 :])
    return jnp.moveaxis(shard.reshape(*before, peers, -1, *after), dim, 0)


def sum_at_owner(shard, axis, dim):
    blocks = cut_along(shard, dim, lax.axis_size(axis))
    arrived = lax.all_to_all(blocks, axis, split_axis=0, concat_axis=0, tiled=True)
    return arrived.sum(axis=0)


def copy_for_each(shard, axis):
    copies = jnp.broadcast_to(shard, (lax.axis_size(axis), *shard.shape))
    return lax.all_to_all(copies, axis, split_axis=0, concat_axis=0, tiled=True)


def of_everyone(shard, axis):
    return copy_for_each(shard, axis).sum(axis=0)


def all_in_one(shard, axis):
    leaves = jax.tree.leaves(shard)
    sequence = sorted(range(len(leaves)), key=lambda k: -leaves[k].size)
    width = (1, *leaves[sequence[0]].shape)[-1]
    lines = [
        jnp.pad(leaves[k].reshape(-1), (0, -leaves[k].size % width)).reshape(-1, width)
        for k in sequence
    ]
    both, at, found = (copy_for_each(jnp.concatenate(lines), axis), 0, {})
    for k, line in zip(sequence, lines):
        share = both[:, at : at + len(line)].reshape(len(both), -1)
        found[k] = share[:, : leaves[k].size].reshape(-1, *leaves[k].shape)
        at += len(line)
    numbers = iter(range(len(leaves)))
    return jax.tree.map(lambda _: found[next(numbers)], shard)


def folded_in_pairs(pieces, combine):
    while len(jax.tree.leaves(pieces)[0]) > 1:
        pieces = jax.vmap(combine)(
            *(jax.tree.map(lambda part: part[side::2], pieces) for side in (0, 1))
        )
    return jax.tree.map(lambda part: part[0], pieces)


def combined_all(shard, axis, combine):
    pieces = all_in_one(shard, axis)
    return folded_in_pairs(pieces, combine)


def sum_at_owner_2(shard, axis, dim):
    blocks = cut_along(shard, dim, lax.axis_size(axis))
    arrived = lax.all_to_all(blocks, axis, split_axis=0, concat_axis=0, tiled=True)
    return arrived.astype(jnp.float32).sum(axis=0)


def summed_rows(shard, axes, dim):
    far, near = axes
    own = sum_at_owner_2(cut_along(shard, dim, lax.axis_size(far)), near, dim + 1)
    return jnp.sum(
        lax.all_to_all(own.astype(jnp.bfloat16), far, 0, 0, tiled=True).astype(jnp.float32), axis=0
    )


def laid_out(blocks, dim):
    blocks = jnp.moveaxis(blocks, 0, dim)
    lengths = blocks.shape
    return blocks.reshape(*lengths[:dim], lengths[dim] * lengths[dim + 1], *lengths[dim + 2 :])


def gathered_copies(shard, axis, dim):
    return laid_out(copy_for_each(shard, axis), dim)


def sum_in_two_steps(shard, axes, dim):
    far, near = axes
    blocks = cut_along(shard, dim, lax.axis_size(far))
    nearer = sum_at_owner(blocks, near, dim + 1)
    arrived = lax.all_to_all(nearer, far, split_axis=0, concat_axis=0, tiled=True)
    return arrived.sum(axis=0)


def place_rows(rows_all, block, row_start):
    padded = jnp.zeros((rows_all + block.shape[0], block.shape[1]), jnp.float32)
    updated = lax.dynamic_update_slice(padded, block, (row_start, jnp.int32(0)))
    return updated[:rows_all]


def pick_rows(reach_rows, source, row_start):
    return lax.dynamic_slice_in_dim(source, row_start, reach_rows, 0)


def combine_mass(first_pair, second_pair):
    highest = jnp.maximum(first_pair[0], second_pair[0])
    summed = first_pair[1] * jnp.exp(first_pair[0] - highest) + second_pair[1] * jnp.exp(
        second_pair[0] - highest
    )
    return (highest, summed)


def local(images, noise_weight, prior_mask, volume, interp_weights, row_first, row_count):
    owned, reach_rows, line_span = interp_weights.shape
    planes = volume.shape[1]
    width = volume.shape[2]
    half_rows = images.shape[1]
    rows_all = half_rows * lax.axis_size("slab")
    vol_lines = volume.reshape(line_span, width)
    kept_rows = lax.broadcasted_iota(jnp.int32, (owned, reach_rows), 1) < row_count
    blocks = jnp.einsum(
        "kjl,lc->kjc", interp_weights, vol_lines, preferred_element_type=jnp.float32
    )
    blocks = blocks * kept_rows[:, :, None].astype(jnp.float32)
    placed = jax.vmap(partial(place_rows, rows_all), out_axes=1)(blocks, row_first[:, 0])

    def share(offset, amount):
        return placed

    own_rows = sum_at_owner(share(jnp.int32(0), half_rows * lax.axis_size("slab")), "slab", 0)
    own_rows = own_rows.astype(jnp.bfloat16)
    noise_both = jnp.concatenate([noise_weight, noise_weight], axis=1)
    seg_float = lax.all_gather(own_rows, IMG, axis=1, tiled=True).astype(jnp.float32)
    weighted = (noise_both[:, None, :] * seg_float).astype(jnp.bfloat16)
    inner_prod = jnp.einsum("nrc,rkc->nk", images, weighted, preferred_element_type=jnp.float32)
    quadratic = 0.5 * jnp.sum(noise_both[:, None, :] * seg_float * seg_float, axis=(0, 2))
    partial_scores = inner_prod - quadratic[None, :]
    scores = of_everyone(partial_scores, "slab")
    allowed = prior_mask > 0
    masked = jnp.where(allowed, scores, -1e30)
    local_top = jnp.max(masked, axis=1)
    local_mass = jnp.sum(jnp.where(allowed, jnp.exp(scores - local_top[:, None]), 0.0), axis=1)
    highest, total_mass = combined_all((local_top, local_mass), "ori", combine_mass)
    exp_scores = jnp.where(allowed, jnp.exp(scores - highest[:, None]), 0.0)
    log_evidence = highest + jnp.log(total_mass)
    posterior = (exp_scores / total_mass[:, None]).astype(jnp.bfloat16)
    columns = posterior
    image_sums = summed_rows(
        jnp.einsum("nk,nrc->krc", columns, images, preferred_element_type=jnp.float32).astype(
            jnp.bfloat16
        ),
        (("img_0", "img_1"), "img_2"),
        0,
    ).astype(jnp.bfloat16)
    full_rows = gathered_copies(image_sums, "slab", 1)
    padded = jnp.pad(full_rows, ((0, 0), (0, reach_rows), (0, 0)))
    picked = jax.vmap(partial(pick_rows, reach_rows))(padded, row_first[:, 0])
    picked = picked * kept_rows[:, :, None].astype(jnp.bfloat16)
    rows_out = volume.shape[0] // (lax.axis_size(IMG) * lax.axis_size("ori"))
    columns = interp_weights
    accumulated = jnp.einsum("kjl,kjc->lc", columns, picked, preferred_element_type=jnp.float32)
    inserted = sum_in_two_steps(
        accumulated.reshape(rows_out * lax.axis_size(IMG_ORI), planes, width),
        (("img_0", "img_1"), ("img_2", "ori")),
        0,
    )
    return (log_evidence, inserted)


def solution(mesh):
    torus = Mesh(
        mesh.devices.reshape(4, 2, 2, mesh.shape["ori"], mesh.shape["slab"]),
        ("img_0", "img_1", "img_2", "ori", "slab"),
    )
    in_specs = (
        P(IMG, "slab", None),
        P("slab", None),
        P(IMG, "ori"),
        P(None, "slab", None),
        P(ORI_IMG, None, "slab"),
        P(ORI_IMG, "slab"),
        P(ORI_IMG, "slab"),
    )
    out_specs = (P(IMG), P(IMG_ORI, "slab", None))
    return jax.shard_map(local, mesh=torus, in_specs=in_specs, out_specs=out_specs, check_vma=False)
```

profile of v0, /device:TPU:32, one launch (start us, length us, event | category | flops | bytes accessed | tf_op | source)
XLA Modules:
  0.0 429.5 jit_solution(4320711514885184938)
XLA Ops:
  12.7 113.2 %while.1 = (s32[]{:T(128)}, f32[12,256,256]{2,1,0:T(8,128)}, s32[12,3]{0,1:T(4,128)S(1)}, f32[12,96,256]{2,1,0:T(8,128)S(1)}, s32[]{:T(128)}, /*index=5*/s32[3]{0:T(128)}, s32[]{:T(128)}) while((s32[]{:T(128)}, f32[12,256,256]{2,1,0:T(8,128)}, s32[12,3]{0,1:T(4,128)S(1)}, f32[12,96,256]{2,1,0:T(8,128)S(1)}, s32[]{:T(128)}, /*index=5*/s32[3]{0:T(128)}, ...), condition=%wide.while_cond, body=%wide.while_body.sunk | while | flops 24595 | bytes 491691 | solution.py:98
  13.3 3.3 and_reduce_fusion.2
  16.6 2.8 dynamic-slice_select_fusion.2
  19.3 2.8 dynamic-update-slice.3
  22.7 3.3 and_reduce_fusion.2
  28.8 2.8 dynamic-update-slice.3
  32.2 3.3 and_reduce_fusion.2
  38.2 2.8 dynamic-update-slice.3
  41.6 3.3 and_reduce_fusion.2
  44.8 2.8 dynamic-slice_select_fusion.2
  47.6 2.8 dynamic-update-slice.3
  51.0 3.3 and_reduce_fusion.2
  57.0 2.8 dynamic-update-slice.3
  60.4 3.3 and_reduce_fusion.2
  66.5 2.8 dynamic-update-slice.3
  69.9 3.3 and_reduce_fusion.2
  73.1 2.8 dynamic-slice_select_fusion.2
  75.9 2.8 dynamic-update-slice.3
  79.3 3.3 and_reduce_fusion.2
  82.6 2.8 dynamic-slice_select_fusion.2
  85.3 2.8 dynamic-update-slice.3
  88.7 3.3 and_reduce_fusion.2
  94.8 2.8 dynamic-update-slice.3
  98.2 3.3 and_reduce_fusion.2
  104.2 2.8 dynamic-update-slice.3
  107.6 3.3 and_reduce_fusion.2
  113.6 2.8 dynamic-update-slice.3
  117.1 3.3 and_reduce_fusion.2
  123.1 2.8 dynamic-update-slice.3
  127.7 26.2 %all_to_all.40 = f32[2,80,12,256]{3,1,2,0:T(8,128)S(1)} all-to-all(f32[2,80,12,256]{3,1,2,0:T(8,128)S(1)} %copy.51), channel_id=1, replica_groups=mesh['img_0'=4,'img_1'=2,'img_2'=2,'ori'=8,'slab'=2] {'slab'}, dimensions={0} | all-to-all | bytes 3932160 | tf_op jit(solution)/shard_map/all_to_all | solution.py:21
  155.0 78.2 %all-gather.2.cloned.1.call-done = bf16[80,192,256]{2,0,1:T(8,128)(2,1)} async-done(((bf16[80,12,256]{2,0,1:T(8,128)(2,1)}), bf16[80,192,256]{2,0,1:T(8,128)(2,1)}) %all-gather.2.cloned.1.call-update) | async-done | bytes 7864336 | tf_op jit(solution)/shard_map/all_gather | solution.py:134
  233.3 9.4 %fusion = (f32[192]{0:T(256)S(1)}, bf16[80,192,256]{2,0,1:T(8,128)(2,1)}) fusion(bf16[80,192,256]{2,0,1:T(8,128)(2,1)} %all-gather.2.cloned.1.call-done, f32[80,256]{1,0:T(8,128)S(1)} %pad_maximum_fusion), kind=kLoop, calls=%fused_computation.6 | loop fusion | flops 19660608 | bytes 15811328 | tf_op jit(solution)/shard_map/reduce_sum | solution.py:137
  242.7 13.9 %fusion.19 = f32[192,192]{0,1:T(8,128)S(1)} fusion(bf16[192,80,256]{2,1,0:T(8,128)(2,1)} %param.7, bf16[80,192,256]{2,0,1:T(8,128)(2,1)} %get-tuple-element.30, f32[192]{0:T(256)S(1)} %broadcast_multiply_fusion.1), kind=kOutput, calls=%fused_computation.17 | convolution fusion | flops 1509986304 | bytes 15876864 | tf_op jit(solution)/shard_map/nrc,rkc->nk/dot_general | solution.py:136
  256.7 9.7 %all_to_all.41 = f32[2,192,192]{2,1,0:T(8,128)S(1)} all-to-all(f32[2,192,192]{2,1,0:T(8,128)S(1)} %broadcast_in_dim.33), channel_id=1, replica_groups=mesh['img_0'=4,'img_1'=2,'img_2'=2,'ori'=8,'slab'=2] {'slab'}, dimensions={0} | all-to-all | bytes 589824 | tf_op jit(solution)/shard_map/all_to_all | solution.py:27
  266.8 13.6 %all_to_all.42 = f32[8,2,192]{2,1,0:T(2,128)S(1)} all-to-all(f32[8,2,192]{2,1,0:T(2,128)S(1)} %broadcast_in_dim.36), channel_id=1, replica_groups=mesh['img_0'=4,'img_1'=2,'img_2'=2,'ori'=8,'slab'=2] {'ori'}, dimensions={0} | all-to-all | bytes 24576 | tf_op jit(solution)/shard_map/all_to_all | solution.py:27
  280.7 6.6 %fusion.6 = bf16[192,80,256]{2,0,1:T(8,128)(2,1)S(1)} fusion(bf16[192,80,256]{2,1,0:T(8,128)(2,1)} %param.7, pred[192,192]{1,0:T(32,128)(4,1)S(1)} %get-tuple-element.25, f32[192,192]{1,0:T(8,128)S(1)} %reduce_sum.84, f32[192]{0:T(256)S(1)} %bitcast.63, f32[192]{0:T(256)S(1)} %bitcast.65), kind=kOutput, calls=%fused_computation.12 | convolution fusion | flops 1514029056 | bytes 15914496 | tf_op jit(solution)/shard_map/nk,nrc->krc/dot_general | solution.py:150
  287.3 7.7 %copy.59 = bf16[192,80,256]{2,1,0:T(8,128)(2,1)} copy(bf16[192,80,256]{2,0,1:T(8,128)(2,1)S(1)} %fusion.6) | data formatting | bytes 15728640 | tf_op jit(solution)/shard_map/convert_element_type | solution.py:150
  295.0 3.7 copy.60
  298.7 11.3 %all_to_all.43 = bf16[2,8,12,80,256]{4,3,2,1,0:T(8,128)(2,1)} all-to-all(bf16[2,8,12,80,256]{4,3,2,1,0:T(8,128)(2,1)S(1)} %copy.60), channel_id=1, replica_groups=mesh['img_0'=4,'img_1'=2,'img_2'=2,'ori'=8,'slab'=2] {'img_2'}, dimensions={0} | all-to-all | bytes 15728640 | tf_op jit(solution)/shard_map/all_to_all | solution.py:66
  310.0 7.8 %reduce_sum.86 = bf16[8,12,80,256]{3,2,1,0:T(8,128)(2,1)} reduce(bf16[2,8,12,80,256]{4,3,2,1,0:T(8,128)(2,1)} %all_to_all.43, bf16[]{:T(256)} %constant.6.clone.1), dimensions={0}, to_apply=%region_6.7 | reduce | flops 1966080 | bytes 11796482 | tf_op jit(solution)/shard_map/reduce_sum | solution.py:67
  317.8 53.2 %all_to_all.44 = bf16[8,12,80,256]{3,2,1,0:T(8,128)(2,1)} all-to-all(bf16[8,12,80,256]{3,2,1,0:T(8,128)(2,1)} %reduce_sum.86), channel_id=1, replica_groups=mesh['img_0'=4,'img_1'=2,'img_2'=2,'ori'=8,'slab'=2] {'img_0','img_1'}, dimensions={0} | all-to-all | bytes 7864320 | tf_op jit(solution)/shard_map/all_to_all | solution.py:74
  371.1 2.8 reduce_sum.87
  374.9 3.6 all-to-all-start.5
  378.6 12.6 %all-to-all-done.5 = bf16[2,12,80,256]{3,2,1,0:T(8,128)(2,1)S(1)} async-done(((bf16[2,12,80,256]{3,2,1,0:T(8,128)(2,1)}), bf16[2,12,80,256]{3,2,1,0:T(8,128)(2,1)S(1)}, u32[]{:S(2)}, u32[]{:S(2)}) %all-to-all-start.5) | async-done | bytes 983072 | tf_op jit(solution)/shard_map/all_to_all | solution.py:27
  391.7 2.9 gather_fusion
  395.6 14.8 %all_to_all.45 = f32[16,8,1,2,256]{4,3,1,2,0:T(2,128)S(1)} all-to-all(f32[16,8,1,2,256]{4,3,1,2,0:T(2,128)S(1)} %bitcast.61), channel_id=1, replica_groups=mesh['img_0'=4,'img_1'=2,'img_2'=2,'ori'=8,'slab'=2] {'img_2','ori'}, dimensions={0} | all-to-all | bytes 524288 | tf_op jit(solution)/shard_map/all_to_all | solution.py:21
  411.1 3.3 all-to-all-start.7
  415.0 7.1 %all-to-all-done.7 = f32[8,1,2,256]{3,2,1,0:T(2,128)S(1)} async-done(((f32[8,1,2,256]{3,2,1,0:T(2,128)}), f32[8,1,2,256]{3,2,1,0:T(2,128)S(1)}, u32[]{:S(2)}, u32[]{:S(2)}) %all-to-all-start.7) | async-done | bytes 16416 | tf_op jit(solution)/shard_map/all_to_all | solution.py:92
  (84 shorter events, 43.1 us)
Async XLA Ops:
  7.2 3.2 copy-start
  7.2 226.1 %all-gather.2.cloned.1.call-start = ((), (), s32[]{:S(2)}) async-start(), calls=%async_computation.8 | async-start | bytes 8355840 | tf_op jit(solution)/shard_map/all_gather | solution.py:134
  125.9 29.1 %copy-start.2 = (f32[80,128]{1,0:T(8,128)S(1)}, f32[80,128]{1,0:T(8,128)}, u32[]{:S(2)}) copy-start(f32[80,128]{1,0:T(8,128)} %param.8) | copy-start | bytes 122884
  242.7 23.7 %copy-start.1 = (s32[192,192]{1,0:T(8,128)S(1)}, s32[192,192]{1,0:T(8,128)}, u32[]{:S(2)}) copy-start(s32[192,192]{1,0:T(8,128)} %param.9) | copy-start | bytes 442372
  374.9 16.3 %all-to-all-start.5 = ((bf16[2,12,80,256]{3,2,1,0:T(8,128)(2,1)}), bf16[2,12,80,256]{3,2,1,0:T(8,128)(2,1)S(1)}, u32[]{:S(2)}, u32[]{:S(2)}) async-start(bf16[2,12,80,256]{3,2,1,0:T(8,128)(2,1)} %broadcast_in_dim.37), calls=%async_computation.5 | async-start | bytes 1966080 | tf_op jit(solution)/shard_map/all_to_all | solution.py:27
  411.1 11.0 %all-to-all-start.7 = ((f32[8,1,2,256]{3,2,1,0:T(2,128)}), f32[8,1,2,256]{3,2,1,0:T(2,128)S(1)}, u32[]{:S(2)}, u32[]{:S(2)}) async-start(f32[8,1,2,256]{3,2,1,0:T(2,128)} %bitcast.19), calls=%async_computation.7 | async-start | bytes 32768 | tf_op jit(solution)/shard_map/all_to_all | solution.py:92
Sparse Core Ops, SparseCore 0:
  155.1 78.0 all-gather.1
where the time goes:
time: 432 us; the launch traced here: 430 us
  blocking collectives  129 us (30%)
  other arithmetic  98.1 us (23%)
  waiting for transfers between devices  97.9 us (23%)
  local copies, waits for them, and re-layouts  62.2 us (14%)
  matrix products  21.3 us (5%)
  between operations  14.2 us (3%)
  starting transfers between devices  6.94 us (2%)
    all_gather x1, waiting for transfers between devices, local(): lax.all_gather(own_rows, IMG, axis=1, tiled=True).astype(jnp.float32)  78.2 us
    scatter x24, other arithmetic  72.3 us
    all_to_all x1, blocking collectives, summed_rows(): lax.all_to_all(own.astype(jnp.bfloat16), far, 0, 0, tiled=True)  53.2 us
    all_to_all x2, blocking collectives, sum_at_owner(): lax.all_to_all(blocks, axis, split_axis=0, concat_axis=0, tiled=True)  41 us
    scatter x36, local copies, waits for them, and re-layouts  40.8 us
    all_to_all x2, blocking collectives, copy_for_each(): return lax.all_to_all(copies, axis, split_axis=0, concat_axis=0, tiled=True)  23.3 us
    dot_general x1, matrix products, local(): jnp.einsum('nrc,rkc->nk', images, weighted, preferred_element_type=jnp.fl...  13.9 us
    all_to_all x1, waiting for transfers between devices, copy_for_each(): return lax.all_to_all(copies, axis, split_axis=0, concat_axis=0, tiled=True)  12.6 us
  transfers between devices with their start and end apart: 3, of which 3 were waited for; matrix products, arithmetic and copies ran while one was open for 0% of the time, Pallas kernels for 0%

commit v1 on v0

v1 whole, which is shorter than its diff:
```python
import jax
import jax.numpy as jnp
from jax import lax
from jax.experimental import pallas as pl
from jax.experimental.pallas import tpu as pltpu
from jax.sharding import Mesh
from jax.sharding import PartitionSpec as P

IMG = ("y", "xh", "core")
BF16 = jnp.bfloat16
F32 = jnp.float32
SOURCES = ((0, 0), (0, 1), (-1, 0), (1, 0), (-1, 1), (1, 1), (2, 0), (2, 1))


def shifted(x, axis, step):
    n = lax.axis_size(axis)
    return lax.ppermute(x, axis, [(i, (i + step) % n) for i in range(n)])


def gathered(near, far):
    beside = shifted(near, "xh", 1)
    up = shifted(near, "y", 1)
    down = shifted(near, "y", -1)
    far = shifted(far, "slab", 1)
    across = shifted(up, "y", 1)
    beside_down = shifted(beside, "y", -1)
    beside_up = shifted(beside, "y", 1)
    far_beside = shifted(far, "xh", 1)
    far_down = shifted(far, "y", -1)
    far_up = shifted(far, "y", 1)
    far_across = shifted(far_down, "y", -1)
    far_beside_down = shifted(far_beside, "y", -1)
    far_beside_up = shifted(far_beside, "y", 1)
    across_beside = shifted(across, "xh", 1)
    far_across_beside = shifted(far_across, "xh", 1)
    return (
        [near, beside, up, down, beside_up, beside_down, across, across_beside],
        [far, far_beside, far_up, far_down, far_beside_up, far_beside_down, far_across, far_across_beside],
    )


def placed_rows(weights, row_first, row_count, half, half_rows):
    owned, reach, _ = weights.shape
    row = lax.broadcasted_iota(jnp.int32, (owned, half_rows, reach), 1)
    entry = lax.broadcasted_iota(jnp.int32, (owned, half_rows, reach), 2)
    at = half * half_rows + row - row_first[:, :, None]
    chosen = (entry == at) & (entry < row_count[:, :, None])
    return jnp.einsum("orj,ojl->orl", chosen.astype(BF16), weights, preferred_element_type=BF16)


def column_choice(total, owned, core):
    my_y = lax.axis_index("y")
    my_x = lax.axis_index("xh")
    picks = []
    for dy, dx in SOURCES:
        chip = ((my_y + dy + 4) % 4) * 2 + (my_x + dx) % 2
        first = (chip * 2 + core) * owned
        picks.append(first + jnp.arange(owned))
    wanted = jnp.concatenate(picks)
    return (jnp.arange(total)[None, :] == wanted[:, None]).astype(BF16)


def weighted_kernel(*refs):
    chips = (len(refs) - 6) // 2
    near, far = refs[:chips], refs[chips : 2 * chips]
    lines, lines_far, noise, out, quad, wide = refs[2 * chips :]
    rows = out.shape[0]
    step = noise.shape[0]
    some = step // rows
    owned = near[0].shape[0] // rows
    for chip in range(chips):

        def project(i, carry, chip=chip):
            at = pl.multiple_of(i * step, step)
            slices = jnp.dot(near[chip][pl.ds(at, step), :], lines[...], preferred_element_type=F32)
            slices += jnp.dot(far[chip][pl.ds(at, step), :], lines_far[...], preferred_element_type=F32)
            slices = slices.astype(BF16).astype(F32)
            weighted = noise[...] * slices
            wide[0, pl.ds(pl.multiple_of(chip * owned * rows + i * step, step), step), :] = weighted[:, :128]
            wide[1, pl.ds(pl.multiple_of(chip * owned * rows + i * step, step), step), :] = weighted[:, 128:]
            square = weighted * slices
            square = square[:, :128] + square[:, 128:]
            quad[pl.ds(chip * owned + i * some, some)] = jnp.sum(
                square.reshape(some, rows // 8, 8, 128), axis=1
            )
            return carry

        lax.fori_loop(0, owned // some, project, 0)

    def turn(r, carry):
        for half in range(2):
            out[r, :, half * 128 : half * 128 + 128] = wide[
                half, pl.ds(r, chips * owned, stride=rows), :
            ].astype(BF16)
        return carry

    lax.fori_loop(0, rows, turn, 0, unroll=4)


def weighted_slices(near, far, lines, lines_far, noise, rows):
    chips = len(near)
    count = chips * near[0].shape[0] // rows
    width = lines.shape[1]
    return pl.pallas_call(
        weighted_kernel,
        out_shape=(
            jax.ShapeDtypeStruct((rows, count, width), BF16),
            jax.ShapeDtypeStruct((count, 8, 128), F32),
        ),
        scratch_shapes=[pltpu.VMEM((2, count * rows, 128), F32)],
        compiler_params=pltpu.CompilerParams(vmem_limit_bytes=40 << 20),
        name="weighted_slices",
    )(*near, *far, lines, lines_far, noise)


def score_kernel(first, second, quad_first, quad_second, own, beside, out, acc):
    step = pl.program_id(0)
    rows = own.shape[0]
    shots = own.shape[1]

    @pl.when(step == 0)
    def _():
        acc[...] = jnp.zeros_like(acc)

    slices = jnp.concatenate(
        [jnp.concatenate([first[r], second[r]], axis=0) for r in range(rows)], axis=1
    )
    for k, shot in enumerate((own, beside)):
        block = jnp.concatenate([shot[r] for r in range(rows)], axis=1)
        acc[k] += lax.dot_general(
            slices, block, (((1,), (1,)), ((), ())), preferred_element_type=F32
        )

    @pl.when(step == pl.num_programs(0) - 1)
    def _():
        quad = jnp.concatenate([jnp.sum(quad_first[...], axis=1), jnp.sum(quad_second[...], axis=1)], axis=0)
        half = 0.5 * jnp.sum(quad, axis=1, keepdims=True)
        out[:, :shots] = acc[0] - half
        out[:, shots:] = acc[1] - half


def partial_scores(first, second, quad_first, quad_second, own, beside, block=8):
    rows, shots, width = own.shape
    count = first.shape[1]
    slices_spec = pl.BlockSpec((block, count, width), lambda i: (i, 0, 0))
    quad_spec = pl.BlockSpec(quad_first.shape, lambda i: (0, 0, 0))
    shots_spec = pl.BlockSpec((block, shots, width), lambda i: (i, 0, 0))
    return pl.pallas_call(
        score_kernel,
        grid=(rows // block,),
        in_specs=[slices_spec, slices_spec, quad_spec, quad_spec, shots_spec, shots_spec],
        out_specs=pl.BlockSpec((2 * count, 2 * shots), lambda i: (0, 0)),
        out_shape=jax.ShapeDtypeStruct((2 * count, 2 * shots), F32),
        scratch_shapes=[pltpu.VMEM((2, 2 * count, shots), F32)],
        compiler_params=pltpu.CompilerParams(
            dimension_semantics=("arbitrary",), vmem_limit_bytes=40 << 20
        ),
        name="partial_scores",
    )(first, second, quad_first, quad_second, own, beside)


def rows_major_kernel(shots, out, wide):
    count, rows, _ = shots.shape

    def spread(n, carry):
        block = shots[n].astype(F32)
        at = pl.multiple_of(n * rows, rows)
        wide[0, pl.ds(at, rows), :] = block[:, :128]
        wide[1, pl.ds(at, rows), :] = block[:, 128:]
        return carry

    lax.fori_loop(0, count, spread, 0, unroll=4)

    def turn(r, carry):
        for half in range(2):
            out[r, :, half * 128 : half * 128 + 128] = wide[
                half, pl.ds(r, count, stride=rows), :
            ].astype(BF16)
        return carry

    lax.fori_loop(0, rows, turn, 0, unroll=8)


def rows_major(images, block=32):
    shots, rows, width = images.shape
    return pl.pallas_call(
        rows_major_kernel,
        grid=(shots // block,),
        in_specs=[pl.BlockSpec((block, rows, width), lambda i: (i, 0, 0))],
        out_specs=pl.BlockSpec((rows, block, width), lambda i: (0, i, 0)),
        out_shape=jax.ShapeDtypeStruct((rows, shots, width), BF16),
        scratch_shapes=[pltpu.VMEM((2, block * rows, 128), F32)],
        compiler_params=pltpu.CompilerParams(
            dimension_semantics=("arbitrary",), vmem_limit_bytes=20 << 20
        ),
        name="rows_major",
    )(images)


def turn_kernel(*refs):
    chunks, out, flat = refs[:-2], refs[-2], refs[-1]
    half = len(chunks) // 2
    size, lines = chunks[0].shape
    for side in range(2):
        for i in range(half):
            flat[side, i * size : (i + 1) * size, :] = chunks[side * half + i][...]
    for side in range(2):

        def turn(i, carry, side=side):
            at = pl.multiple_of(i * 128, 128)
            out[side * lines : (side + 1) * lines, pl.ds(at, 128)] = flat[side, pl.ds(at, 128), :].T
            return carry

        lax.fori_loop(0, half * size // 128, turn, 0, unroll=2)


def turned_weights(near, far):
    size, lines = near[0].shape
    span = len(near) * size
    return pl.pallas_call(
        turn_kernel,
        out_shape=jax.ShapeDtypeStruct((2 * lines, span), BF16),
        scratch_shapes=[pltpu.VMEM((2, span, lines), BF16)],
        compiler_params=pltpu.CompilerParams(vmem_limit_bytes=20 << 20),
        name="turned_weights",
    )(*near, *far)


def insert_kernel(
    slab, scores, allowed, stats, own, beside, turned, turned_too, out, post_own, post_beside, wide, flat, here, done
):
    step = pl.program_id(0)
    rows = own.shape[0]
    shots = own.shape[1]
    all_rows = rows * pl.num_programs(0)
    count = scores.shape[0]
    lines = out.shape[1]
    fetches = [
        pltpu.make_async_copy(turned, here.at[0], done.at[0]),
        pltpu.make_async_copy(turned_too, here.at[1], done.at[1]),
    ]

    @pl.when(step == 0)
    def _():
        for fetch in fetches:
            fetch.start()
        mass = jnp.exp(scores[...] - stats[0:1, :])
        post = jnp.where(allowed[...] > 0.5, mass, 0.0) / stats[1:2, :]
        post_own[...] = post[:, :shots].astype(BF16)
        post_beside[...] = post[:, shots:].astype(BF16)

    for r in range(rows):
        sums = jnp.dot(post_own[...], own[r], preferred_element_type=F32)
        sums += jnp.dot(post_beside[...], beside[r], preferred_element_type=F32)
        for half in range(2):
            wide[half, pl.ds(step * rows + r, count, stride=all_rows), :] = sums[
                :, half * 128 : half * 128 + 128
            ]

    @pl.when(step == pl.num_programs(0) - 1)
    def _():
        span = 640

        def narrow(i, carry):
            at = pl.multiple_of(i * span, span)
            for half in range(2):
                flat[pl.ds(at, span), half * 128 : half * 128 + 128] = wide[
                    half, pl.ds(at, span), :
                ].astype(BF16)
            return carry

        lax.fori_loop(0, count * all_rows // span, narrow, 0)
        for fetch in fetches:
            fetch.wait()
        split = count * all_rows // 2
        for side, slot in ((0, slab[0]), (1, 1 - slab[0])):
            total = jnp.dot(
                here[0, side * lines : (side + 1) * lines, :], flat[:split, :], preferred_element_type=F32
            )
            total += jnp.dot(
                here[1, side * lines : (side + 1) * lines, :], flat[split:, :], preferred_element_type=F32
            )
            out[slot] = total.astype(BF16)


def insertion(slab, scores, allowed, stats, own, beside, turned, turned_too, block=8):
    rows, shots, width = own.shape
    count = scores.shape[0]
    lines = turned.shape[0] // 2
    whole = lambda x: pl.BlockSpec(x.shape, lambda i, s: (0, 0))
    shots_spec = pl.BlockSpec((block, shots, width), lambda i, s: (i, 0, 0))
    there = pl.BlockSpec(memory_space=pl.ANY)
    return pl.pallas_call(
        insert_kernel,
        grid_spec=pltpu.PrefetchScalarGridSpec(
            num_scalar_prefetch=1,
            grid=(rows // block,),
            in_specs=[whole(scores), whole(allowed), whole(stats), shots_spec, shots_spec, there, there],
            out_specs=pl.BlockSpec((2, lines, width), lambda i, s: (0, 0, 0)),
            scratch_shapes=[
                pltpu.VMEM((count, shots), BF16),
                pltpu.VMEM((count, shots), BF16),
                pltpu.VMEM((2, count * rows, 128), F32),
                pltpu.VMEM((count * rows, width), BF16),
                pltpu.VMEM((2, *turned.shape), BF16),
                pltpu.SemaphoreType.DMA((2,)),
            ],
        ),
        out_shape=jax.ShapeDtypeStruct((2, lines, width), BF16),
        compiler_params=pltpu.CompilerParams(
            dimension_semantics=("arbitrary",), vmem_limit_bytes=50 << 20
        ),
        name="insertion",
    )(slab, scores, allowed, stats, own, beside, turned, turned_too)


def crossed(x, axes, mask):
    return lax.ppermute(x, axes, [(i, i ^ mask) for i in range(lax.axis_size(axes))])


def combined(pairs):
    highest = jnp.max(jnp.stack([p[0] for p in pairs]), axis=0)
    total = sum(p[1] * jnp.exp(p[0] - highest) for p in pairs)
    return jnp.stack([highest, total])


def in_core_order(stats, core, shots):
    swapped = jnp.concatenate([stats[:, shots:], stats[:, :shots]], axis=1)
    return jnp.where(core == 0, stats, swapped)


def step(images, noise_weight, prior_mask, volume, interp_weights, row_first, row_count):
    owned, _, line_span = interp_weights.shape
    shots, half_rows, width = images.shape
    slab = lax.axis_index("slab")
    core = lax.axis_index("core")
    lines = volume.reshape(line_span, width)

    near = placed_rows(interp_weights, row_first, row_count, slab, half_rows)
    far = placed_rows(interp_weights, row_first, row_count, 1 - slab, half_rows)
    flat = lambda x: x.reshape(owned * half_rows, line_span)
    near, far = gathered(flat(near), flat(far))
    lines_far = shifted(lines, "slab", 1)

    beside = shifted(images, "core", 1)
    own = rows_major(images)
    beside = rows_major(beside)

    mask = prior_mask.astype(BF16)
    choose = lambda which: jnp.einsum(
        "ko,no->kn", column_choice(mask.shape[1], owned, which), mask, preferred_element_type=BF16
    )
    mask_beside = shifted(choose(1 - core), "core", 1)
    allowed = jnp.concatenate([choose(core), mask_beside], axis=1).astype(F32)

    noise_both = jnp.concatenate([noise_weight, noise_weight], axis=1)
    noise_tiled = jnp.tile(noise_both, (3, 1))
    weigh = lambda pick: weighted_slices(near[pick], far[pick], lines, lines_far, noise_tiled, half_rows)
    first, quad_first = weigh(slice(0, 4))
    second, quad_second = weigh(slice(4, 8))
    part = partial_scores(first, second, quad_first, quad_second, own, beside)
    turned = turned_weights(near[:4], far[:4])
    turned_too = turned_weights(near[4:], far[4:])
    scores = part + shifted(part, "slab", 1)

    top = jnp.max(jnp.where(allowed > 0.5, scores, -1e30), axis=0)
    mass = jnp.sum(jnp.where(allowed > 0.5, jnp.exp(scores - top[None]), 0.0), axis=0)
    pair = in_core_order(jnp.stack([top, mass]), core, shots)
    for masks in ((8, 1, 9), (2, 4, 6)):
        pair = combined([pair] + [crossed(pair, ("core", "ori"), m) for m in masks])
    pair = in_core_order(pair, core, shots)
    log_evidence = (pair[0] + jnp.log(pair[1]))[:shots]

    into = insertion(slab.reshape(1), scores, allowed, pair, own, beside, turned, turned_too)
    into = into.reshape(-1, volume.shape[1], width)
    arrived = lax.all_to_all(into, ("slab",) + IMG + ("ori",), 0, 0, tiled=True)
    inserted = jnp.sum(arrived.astype(F32), axis=0, keepdims=True)
    return log_evidence, inserted


def solution(mesh):
    torus = Mesh(
        mesh.devices.reshape(4, 2, 2, mesh.shape["ori"], mesh.shape["slab"]),
        ("y", "xh", "core", "ori", "slab"),
    )
    owner = ("ori",) + IMG
    in_specs = (
        P(IMG, "slab", None),
        P("slab", None),
        P(IMG, "ori"),
        P(None, "slab", None),
        P(owner, None, "slab"),
        P(owner, "slab"),
        P(owner, "slab"),
    )
    out_specs = (P(IMG), P(IMG + ("ori",), "slab", None))
    return jax.shard_map(step, mesh=torus, in_specs=in_specs, out_specs=out_specs, check_vma=False)
```

time: 432 us -> 234 us (0.54)
  blocking collectives: 129 us -> 0 us
  other arithmetic: 98.1 us -> 8.3 us
  Pallas kernels: 0 us -> 64.6 us
  starting transfers between devices: 6.94 us -> 52.8 us
  local copies, waits for them, and re-layouts: 62.2 us -> 31.9 us
  waiting for transfers between devices: 97.9 us -> 68.4 us
  matrix products: 21.3 us -> 3.95 us
  between operations: 14.2 us -> 1.01 us
    all_to_all x6 -> x0, blocking collectives: 129 us -> none  [the longest x1 53.2 us: summed_rows(): lax.all_to_all(own.astype(jnp.bfloat16), far, 0, 0, tiled=True)]
    all_gather x1 -> x0, waiting for transfers between devices: 78.2 us -> none  [local(): lax.all_gather(own_rows, IMG, axis=1, tiled=True).astype(jnp.float32)]
    scatter x25 -> x0, other arithmetic: 72.3 us -> none
    pallas_call x0 -> x8, Pallas kernels: none -> 64.6 us  [the longest x2 16.2 us: rows_major(): pl.pallas_call(rows_major_kernel, grid=(shots // block,), in_specs=[pl.Bl...]
    ppermute x0 -> x25, waiting for transfers between devices: none -> 54.2 us  [the longest x19 52.3 us: shifted(): return lax.ppermute(x, axis, [(i, (i + step) % n) for i in range(n)])]
    scatter x36 -> x0, local copies, waits for them, and re-layouts: 40.8 us -> none
    ppermute x0 -> x25, starting transfers between devices: none -> 40.8 us  [the longest x19 30.7 us: shifted(): return lax.ppermute(x, axis, [(i, (i + step) % n) for i in range(n)])]
    unnamed x7 -> x58, local copies, waits for them, and re-layouts: 0.02 us -> 28.5 us
  transfers between devices with their start and end apart: 3 -> 26, of which waited for: 3 -> 9; matrix products, arithmetic and copies ran while one was open for 0% -> 5% of each run, Pallas kernels for 0% -> 22%
where the time goes in v1:
time: 234 us; the launch traced here: 231 us
  waiting for transfers between devices  68.4 us (29%)
  Pallas kernels  64.6 us (28%)
  starting transfers between devices  52.8 us (23%)
  local copies, waits for them, and re-layouts  31.9 us (14%)
  other arithmetic  8.3 us (4%)
  matrix products  3.95 us (2%)
    ppermute x19, waiting for transfers between devices, shifted(): return lax.ppermute(x, axis, [(i, (i + step) % n) for i in range(n)])  52.3 us
    ppermute x19, starting transfers between devices, shifted(): return lax.ppermute(x, axis, [(i, (i + step) % n) for i in range(n)])  30.7 us
    unnamed x58, local copies, waits for them, and re-layouts  28.5 us
    pallas_call x2, Pallas kernels, rows_major(): pl.pallas_call(rows_major_kernel, grid=(shots // block,), in_specs=[pl.Bl...  16.2 us
    pallas_call x1, Pallas kernels, insertion(): pl.pallas_call(insert_kernel, grid_spec=pltpu.PrefetchScalarGridSpec(num_...  14.9 us
    all_to_all x1, waiting for transfers between devices, step(): arrived = lax.all_to_all(into, ('slab',) + IMG + ('ori',), 0, 0, tiled=True)  14.2 us
    pallas_call x2, Pallas kernels, weighted_slices(): pl.pallas_call(weighted_kernel, out_shape=(jax.ShapeDtypeStruct((rows, co...  13.9 us
    all_to_all x1, starting transfers between devices, step(): arrived = lax.all_to_all(into, ('slab',) + IMG + ('ori',), 0, 0, tiled=True)  12 us
  transfers between devices with their start and end apart: 26, of which 9 were waited for; matrix products, arithmetic and copies ran while one was open for 5% of the time, Pallas kernels for 22%

profile of v1, /device:TPU:32, one launch (start us, length us, event | category | flops | bytes accessed | tf_op | source)
XLA Modules:
  0.0 231.0 jit_solution(1828141542691064981)
XLA Ops:
  2.7 1.6 collective-permute-start.4
  5.3 1.7 collective-permute-start.2
  7.0 2.7 %collective-permute-start.1 = (bf16[960,256]{1,0:T(8,128)(2,1)S(1)}, bf16[960,256]{1,0:T(8,128)(2,1)S(1)}, u32[]{:S(2)}, u32[]{:S(2)}) collective-permute-start(bf16[960,256]{1,0:T(8,128)(2,1)S(1)} %bitcast.13), channel_id=1, source_target_pairs={{0,32},{32,0},{1,33},{33,1},{2,34},{34,2},{3,35},{35,3},{4,36},{36... | collective-permute-start | bytes 1474568 | tf_op jit(solution)/shard_map/ppermute | solution.py:17
  11.6 17.5 %collective-permute-done.8.refs_9_ = bf16[256,256]{1,0:T(8,128)(2,1)S(1)} collective-permute-done((bf16[256,256]{1,0:T(8,128)(2,1)S(1)}, bf16[256,256]{1,0:T(8,128)(2,1)S(1)}, u32[]{:S(2)}, u32[]{:S(2)}) %collective-permute-start.8) | collective-permute-done | bytes 131104 | tf_op jit(solution)/shard_map/ppermute | solution.py:17
  29.7 3.0 %collective-permute-start.3 = (bf16[960,256]{1,0:T(8,128)(2,1)S(1)}, bf16[960,256]{1,0:T(8,128)(2,1)S(1)}, u32[]{:S(2)}, u32[]{:S(2)}) collective-permute-start(bf16[960,256]{1,0:T(8,128)(2,1)S(1)} %bitcast.14), channel_id=1, source_target_pairs={{0,192},{64,0},{128,64},{192,128},{1,193},{65,1},{129,65},{193,129... | collective-permute-start | bytes 1474568 | tf_op jit(solution)/shard_map/ppermute | solution.py:17
  33.5 1.3 collective-permute-start.11
  34.8 3.0 %collective-permute-start.5 = (bf16[960,256]{1,0:T(8,128)(2,1)S(1)}, bf16[960,256]{1,0:T(8,128)(2,1)}, u32[]{:S(2)}, u32[]{:S(2)}) collective-permute-start(bf16[960,256]{1,0:T(8,128)(2,1)S(1)} %collective-permute-done.4.refs_4_), channel_id=1, source_target_pairs={{0,32},{32,0},{1,33},{33,1},{2,34},{34,2},{3,35},{35,3},{4,36},{36... | collective-permute-start | bytes 1474568 | tf_op jit(solution)/shard_map/ppermute | solution.py:17
  37.8 6.5 %collective-permute-done.3.refs_3_ = bf16[960,256]{1,0:T(8,128)(2,1)S(1)} collective-permute-done((bf16[960,256]{1,0:T(8,128)(2,1)S(1)}, bf16[960,256]{1,0:T(8,128)(2,1)S(1)}, u32[]{:S(2)}, u32[]{:S(2)}) %collective-permute-start.3) | collective-permute-done | bytes 491552 | tf_op jit(solution)/shard_map/ppermute | solution.py:17
  44.4 3.7 %collective-permute-start.10 = (bf16[960,256]{1,0:T(8,128)(2,1)S(1)}, bf16[960,256]{1,0:T(8,128)(2,1)}, u32[]{:S(2)}, u32[]{:S(2)}) collective-permute-start(bf16[960,256]{1,0:T(8,128)(2,1)S(1)} %collective-permute-done.1.refs_1_), channel_id=1, source_target_pairs={{0,192},{64,0},{128,64},{192,128},{1,193},{65,1},{129,65},{193,129... | collective-permute-start | bytes 1474568 | tf_op jit(solution)/shard_map/ppermute | solution.py:17
  48.1 6.8 %collective-permute-done.7.refs_7_ = bf16[960,256]{1,0:T(8,128)(2,1)S(1)} collective-permute-done((bf16[960,256]{1,0:T(8,128)(2,1)S(1)}, bf16[960,256]{1,0:T(8,128)(2,1)S(1)}, u32[]{:S(2)}, u32[]{:S(2)}) %collective-permute-start.7) | collective-permute-done | bytes 491552 | tf_op jit(solution)/shard_map/ppermute | solution.py:17
  54.9 1.0 collective-permute-start.9
  56.0 1.6 collective-permute-start.6
  57.5 1.7 collective-permute-start.15
  61.5 4.0 %collective-permute-done.10.refs_1_ = bf16[960,256]{1,0:T(8,128)(2,1)} collective-permute-done((bf16[960,256]{1,0:T(8,128)(2,1)S(1)}, bf16[960,256]{1,0:T(8,128)(2,1)}, u32[]{:S(2)}, u32[]{:S(2)}) %collective-permute-start.10) | collective-permute-done | bytes 491552 | tf_op jit(solution)/shard_map/ppermute | solution.py:17
  65.4 1.1 collective-permute-start.13
  66.6 4.2 %collective-permute-done.9.refs_0_ = bf16[960,256]{1,0:T(8,128)(2,1)} collective-permute-done((bf16[960,256]{1,0:T(8,128)(2,1)S(1)}, bf16[960,256]{1,0:T(8,128)(2,1)}, u32[]{:S(2)}, u32[]{:S(2)}) %collective-permute-start.9) | collective-permute-done | bytes 491552 | tf_op jit(solution)/shard_map/ppermute | solution.py:17
  70.8 2.0 collective-permute-start.14
  72.8 8.5 %collective-permute-done.6.refs_6_ = bf16[960,256]{1,0:T(8,128)(2,1)} collective-permute-done((bf16[960,256]{1,0:T(8,128)(2,1)S(1)}, bf16[960,256]{1,0:T(8,128)(2,1)}, u32[]{:S(2)}, u32[]{:S(2)}) %collective-permute-start.6) | collective-permute-done | bytes 491552 | tf_op jit(solution)/shard_map/ppermute | solution.py:17
  81.3 3.0 %collective-permute-start.12 = (bf16[960,256]{1,0:T(8,128)(2,1)}, bf16[960,256]{1,0:T(8,128)(2,1)}, u32[]{:S(2)}, u32[]{:S(2)}) collective-permute-start(bf16[960,256]{1,0:T(8,128)(2,1)} %collective-permute-done.11.refs_2_), channel_id=1, source_target_pairs={{0,32},{32,0},{1,33},{33,1},{2,34},{34,2},{3,35},{35,3},{4,36},{36... | collective-permute-start | bytes 1474568 | tf_op jit(solution)/shard_map/ppermute | solution.py:17
  85.4 3.2 %copy-done.5 = bf16[192,80,256]{2,1,0:T(8,128)(2,1)S(1)} copy-done((bf16[192,80,256]{2,1,0:T(8,128)(2,1)S(1)}, bf16[192,80,256]{2,1,0:T(8,128)(2,1)}, u32[]{:S(2)}) %copy-start.5) | copy-done | bytes 7864344
  88.6 7.2 %rows_major.2.own = bf16[80,192,256]{2,1,0:T(8,128)(2,1)S(1)} custom-call(bf16[192,80,256]{2,1,0:T(8,128)(2,1)S(1)} %copy-done.5), custom_call_target="tpu_custom_call" | custom-call | tf_op jit(solution)/shard_map/rows_major/pallas_call | solution.py:186
  95.9 3.0 %copy-done.1 = bf16[80,192,256]{2,1,0:T(8,128)(2,1)} copy-done((bf16[80,192,256]{2,1,0:T(8,128)(2,1)}, bf16[80,192,256]{2,1,0:T(8,128)(2,1)S(1)}, u32[]{:S(2)}) %copy-start.1) | copy-done | bytes 7864344
  101.3 1.7 fusion.13
  104.1 1.0 copy-done.12
  105.2 1.0 copy-done.15
  106.2 1.0 copy-done.18
  109.0 6.5 %weighted_slices.2 = (bf16[80,48,256]{2,1,0:T(8,128)(2,1)S(1)}, f32[48,8,128]{2,1,0:T(8,128)S(1)}) custom-call(bf16[960,256]{1,0:T(8,128)(2,1)S(1)} %bitcast.15, bf16[960,256]{1,0:T(8,128)(2,1)S(1)} %copy-done.12, bf16[960,256]{1,0:T(8,128)(2,1)S(1)} %copy-done.9, bf16[960,256]{1,0:T(8,128)(2,1)S(1)} %copy-done.15, ...), custom_call_target="tpu_custom_call" | custom-call | tf_op jit(solution)/shard_map/weighted_slices/pallas_call | solution.py:104
  117.4 7.5 %weighted_slices.3 = (bf16[80,48,256]{2,1,0:T(8,128)(2,1)S(1)}, f32[48,8,128]{2,1,0:T(8,128)S(1)}) custom-call(bf16[960,256]{1,0:T(8,128)(2,1)} %collective-permute-done.9.refs_0_, bf16[960,256]{1,0:T(8,128)(2,1)} %collective-permute-done.10.refs_1_, bf16[960,256]{1,0:T(8,128)(2,1)} %collective-permute-done.11.refs_2_, ...), custom_call_target="tpu_custom_call" | custom-call | tf_op jit(solution)/shard_map/weighted_slices/pallas_call | solution.py:104
  124.9 1.3 copy-done.6
  126.2 8.9 %rows_major.3.beside = bf16[80,192,256]{2,1,0:T(8,128)(2,1)S(1)} custom-call(bf16[192,80,256]{2,1,0:T(8,128)(2,1)} %collective-permute-done.17.shots), custom_call_target="tpu_custom_call" | custom-call | tf_op jit(solution)/shard_map/rows_major/pallas_call | solution.py:186
  135.2 3.1 %copy-done.2 = bf16[80,192,256]{2,1,0:T(8,128)(2,1)} copy-done((bf16[80,192,256]{2,1,0:T(8,128)(2,1)}, bf16[80,192,256]{2,1,0:T(8,128)(2,1)S(1)}, u32[]{:S(2)}) %copy-start.2) | copy-done | bytes 7864344
  138.3 10.7 %partial_scores.1 = f32[96,384]{1,0:T(8,128)} custom-call(bf16[80,48,256]{2,1,0:T(8,128)(2,1)S(1)} %get-tuple-element.6.first, bf16[80,48,256]{2,1,0:T(8,128)(2,1)S(1)} %copy-done.7, f32[48,8,128]{2,1,0:T(8,128)S(1)} %get-tuple-element.8.quad_first, f32[48,8,128]{2,1,0:T(8,128)S(1)} %get-tuple-element.9.quad_second, bf16[80,192,256]{2,1,0:T(8,128)(2,1)S(1)} %bitcast.11, ...), custom_call_target="tpu_custom_call" | custom-call | tf_op jit(solution)/shard_map/partial_scores/pallas_call | solution.py:148
  149.0 1.5 collective-permute-start.18
  150.7 4.7 %collective-permute-done.18 = f32[96,384]{1,0:T(8,128)S(1)} collective-permute-done((f32[96,384]{1,0:T(8,128)}, f32[96,384]{1,0:T(8,128)S(1)}, u32[]{:S(2)}, u32[]{:S(2)}) %collective-permute-start.18) | collective-permute-done | bytes 147488 | tf_op jit(solution)/shard_map/ppermute | solution.py:17
  155.4 1.0 select_reduce_fusion.1
  158.2 1.3 collective-permute-start.21
  159.4 1.8 collective-permute-done.20
  161.3 3.3 %collective-permute-start.22 = (f32[2,384]{1,0:T(2,128)S(1)}, f32[2,384]{1,0:T(2,128)S(1)}, u32[]{:S(2)}, u32[]{:S(2)}) collective-permute-start(f32[2,384]{1,0:T(2,128)S(1)} %pad_maximum_fusion.3), channel_id=1, source_target_pairs={{0,4},{2,6},{4,0},{6,2},{8,12},{10,14},{12,8},{14,10},{16,20},{18,... | collective-permute-start | bytes 9224 | tf_op jit(solution)/shard_map/ppermute | solution.py:318
  164.6 4.9 %collective-permute-start.23 = (f32[2,384]{1,0:T(2,128)S(1)}, f32[2,384]{1,0:T(2,128)S(1)}, u32[]{:S(2)}, u32[]{:S(2)}) collective-permute-start(f32[2,384]{1,0:T(2,128)S(1)} %pad_maximum_fusion.3), channel_id=1, source_target_pairs={{0,8},{2,10},{4,12},{6,14},{8,0},{10,2},{12,4},{14,6},{16,24},{18,... | collective-permute-start | bytes 9224 | tf_op jit(solution)/shard_map/ppermute | solution.py:318
  172.5 1.0 copy-done.16
  173.6 1.0 copy-done.19
  174.6 4.1 %turned_weights.2.turned = bf16[512,3840]{1,0:T(8,128)(2,1)S(1)} custom-call(bf16[960,256]{1,0:T(8,128)(2,1)S(1)} %bitcast.16, bf16[960,256]{1,0:T(8,128)(2,1)S(1)} %copy-done.13, bf16[960,256]{1,0:T(8,128)(2,1)S(1)} %copy-done.10, bf16[960,256]{1,0:T(8,128)(2,1)S(1)} %copy-done.16, bf16[960,256]{1,0:T(8,128)(2,1)S(1)} %collective-permute-done.4.refs_4_, ...), custom_call_target="tpu_custom_call" | custom-call | tf_op jit(solution)/shard_map/turned_weights/pallas_call | solution.py:220
  178.7 1.9 copy-done.3
  180.5 4.9 %turned_weights.3.turned_too = bf16[512,3840]{1,0:T(8,128)(2,1)S(1)} custom-call(bf16[960,256]{1,0:T(8,128)(2,1)} %collective-permute-done.9.refs_0_, bf16[960,256]{1,0:T(8,128)(2,1)} %collective-permute-done.10.refs_1_, bf16[960,256]{1,0:T(8,128)(2,1)} %collective-permute-done.11.refs_2_, bf16[960,256]{1,0:T(8,128)(2,1)} %collective-permute-done.12.refs_3_, ...), custom_call_target="tpu_custom_call" | custom-call | tf_op jit(solution)/shard_map/turned_weights/pallas_call | solution.py:220
  185.5 1.9 copy-done.4
  187.6 14.9 %insertion.1 = bf16[2,256,256]{2,1,0:T(8,128)(2,1)S(1)} custom-call(s32[1]{0:T(128)} %bitcast.6.slab, f32[96,384]{1,0:T(8,128)S(1)} %get-tuple-element.15.scores, f32[96,384]{1,0:T(8,128)S(1)} %maximum_convert_fusion.allowed, f32[2,384]{1,0:T(2,128)S(1)} %fusion.18.stats, bf16[80,192,256]{2,1,0:T(8,128)(2,1)} %copy-done.1, bf16[80,192,256]{2,1,0:T(8,128)(2,1)} %copy-done.2, ...), custom_call_target="tpu_custom_call" | custom-call | tf_op jit(solution)/shard_map/insertion/pallas_call | solution.py:293
  203.3 12.0 %all-to-all-start = ((bf16[256,2,256]{2,1,0:T(2,128)(2,1)}), bf16[256,2,256]{2,1,0:T(2,128)(2,1)S(1)}, u32[]{:S(2)}, u32[]{:S(2)}) async-start(bf16[256,2,256]{2,1,0:T(2,128)(2,1)} %reshape.48), calls=%async_computation | async-start | bytes 524288 | tf_op jit(solution)/shard_map/all_to_all | solution.py:376
  215.9 14.2 %all-to-all-done = bf16[256,2,256]{2,1,0:T(2,128)(2,1)S(1)} async-done(((bf16[256,2,256]{2,1,0:T(2,128)(2,1)}), bf16[256,2,256]{2,1,0:T(2,128)(2,1)S(1)}, u32[]{:S(2)}, u32[]{:S(2)}) %all-to-all-start) | async-done | bytes 262176 | tf_op jit(solution)/shard_map/all_to_all | solution.py:376
  (106 shorter events, 24.2 us)
Async XLA Ops:
  0.6 1.1 copy-start
  0.6 125.6 %collective-permute-start.17 = (bf16[192,80,256]{2,1,0:T(8,128)(2,1)}, bf16[192,80,256]{2,1,0:T(8,128)(2,1)}, u32[]{:S(2)}, u32[]{:S(2)}) collective-permute-start(bf16[192,80,256]{2,1,0:T(8,128)(2,1)} %shots.1), channel_id=1, source_target_pairs={{0,16},{16,0},{1,17},{17,1},{2,18},{18,2},{3,19},{19,3},{4,20},{20... | collective-permute-start | bytes 23592968 | tf_op jit(solution)/shard_map/ppermute | solution.py:17
  2.7 30.1 %collective-permute-start.4 = (bf16[960,256]{1,0:T(8,128)(2,1)S(1)}, bf16[960,256]{1,0:T(8,128)(2,1)S(1)}, u32[]{:S(2)}, u32[]{:S(2)}) collective-permute-start(bf16[960,256]{1,0:T(8,128)(2,1)S(1)} %bitcast.19), channel_id=1, source_target_pairs={{0,1},{1,0},{2,3},{3,2},{4,5},{5,4},{6,7},{7,6},{8,9},{9,8},{10,11... | collective-permute-start | bytes 1474568 | tf_op jit(solution)/shard_map/ppermute | solution.py:17
  5.3 28.2 %collective-permute-start.2 = (bf16[960,256]{1,0:T(8,128)(2,1)S(1)}, bf16[960,256]{1,0:T(8,128)(2,1)S(1)}, u32[]{:S(2)}, u32[]{:S(2)}) collective-permute-start(bf16[960,256]{1,0:T(8,128)(2,1)S(1)} %bitcast.12), channel_id=1, source_target_pairs={{0,64},{64,128},{128,192},{192,0},{1,65},{65,129},{129,193},{193,1... | collective-permute-start | bytes 1474568 | tf_op jit(solution)/shard_map/ppermute | solution.py:17
  7.0 27.8 %collective-permute-start.1 = (bf16[960,256]{1,0:T(8,128)(2,1)S(1)}, bf16[960,256]{1,0:T(8,128)(2,1)S(1)}, u32[]{:S(2)}, u32[]{:S(2)}) collective-permute-start(bf16[960,256]{1,0:T(8,128)(2,1)S(1)} %bitcast.13), channel_id=1, source_target_pairs={{0,32},{32,0},{1,33},{33,1},{2,34},{34,2},{3,35},{35,3},{4,36},{36... | collective-permute-start | bytes 1474568 | tf_op jit(solution)/shard_map/ppermute | solution.py:17
  10.7 18.5 %collective-permute-start.8 = (bf16[256,256]{1,0:T(8,128)(2,1)S(1)}, bf16[256,256]{1,0:T(8,128)(2,1)S(1)}, u32[]{:S(2)}, u32[]{:S(2)}) collective-permute-start(bf16[256,256]{1,0:T(8,128)(2,1)S(1)} %reshape.46.refs_8_), channel_id=1, source_target_pairs={{0,1},{1,0},{2,3},{3,2},{4,5},{5,4},{6,7},{7,6},{8,9},{9,8},{10,11... | collective-permute-start | bytes 393224 | tf_op jit(solution)/shard_map/ppermute | solution.py:17
  29.7 14.6 %collective-permute-start.3 = (bf16[960,256]{1,0:T(8,128)(2,1)S(1)}, bf16[960,256]{1,0:T(8,128)(2,1)S(1)}, u32[]{:S(2)}, u32[]{:S(2)}) collective-permute-start(bf16[960,256]{1,0:T(8,128)(2,1)S(1)} %bitcast.14), channel_id=1, source_target_pairs={{0,192},{64,0},{128,64},{192,128},{1,193},{65,1},{129,65},{193,129... | collective-permute-start | bytes 1474568 | tf_op jit(solution)/shard_map/ppermute | solution.py:17
  32.8 22.1 %collective-permute-start.7 = (bf16[960,256]{1,0:T(8,128)(2,1)S(1)}, bf16[960,256]{1,0:T(8,128)(2,1)S(1)}, u32[]{:S(2)}, u32[]{:S(2)}) collective-permute-start(bf16[960,256]{1,0:T(8,128)(2,1)S(1)} %collective-permute-done.4.refs_4_), channel_id=1, source_target_pairs={{0,192},{64,0},{128,64},{192,128},{1,193},{65,1},{129,65},{193,129... | collective-permute-start | bytes 1474568 | tf_op jit(solution)/shard_map/ppermute | solution.py:17
  33.5 62.3 %copy-start.8 = (bf16[960,256]{1,0:T(8,128)(2,1)}, bf16[960,256]{1,0:T(8,128)(2,1)S(1)}, u32[]{:S(2)}) copy-start(bf16[960,256]{1,0:T(8,128)(2,1)S(1)} %collective-permute-done.2.refs_2_) | copy-start | bytes 1474564
  33.5 22.4 %collective-permute-start.11 = (bf16[960,256]{1,0:T(8,128)(2,1)S(1)}, bf16[960,256]{1,0:T(8,128)(2,1)}, u32[]{:S(2)}, u32[]{:S(2)}) collective-permute-start(bf16[960,256]{1,0:T(8,128)(2,1)S(1)} %collective-permute-done.2.refs_2_), channel_id=1, source_target_pairs={{0,64},{64,128},{128,192},{192,0},{1,65},{65,129},{129,193},{193,1... | collective-permute-start | bytes 1474568 | tf_op jit(solution)/shard_map/ppermute | solution.py:17
  34.8 61.0 %copy-start.11 = (bf16[960,256]{1,0:T(8,128)(2,1)}, bf16[960,256]{1,0:T(8,128)(2,1)S(1)}, u32[]{:S(2)}) copy-start(bf16[960,256]{1,0:T(8,128)(2,1)S(1)} %collective-permute-done.1.refs_1_) | copy-start | bytes 1474564
  34.8 22.7 %collective-permute-start.5 = (bf16[960,256]{1,0:T(8,128)(2,1)S(1)}, bf16[960,256]{1,0:T(8,128)(2,1)}, u32[]{:S(2)}, u32[]{:S(2)}) collective-permute-start(bf16[960,256]{1,0:T(8,128)(2,1)S(1)} %collective-permute-done.4.refs_4_), channel_id=1, source_target_pairs={{0,32},{32,0},{1,33},{33,1},{2,34},{34,2},{3,35},{35,3},{4,36},{36... | collective-permute-start | bytes 1474568 | tf_op jit(solution)/shard_map/ppermute | solution.py:17
  44.4 51.5 %copy-start.14 = (bf16[960,256]{1,0:T(8,128)(2,1)}, bf16[960,256]{1,0:T(8,128)(2,1)S(1)}, u32[]{:S(2)}) copy-start(bf16[960,256]{1,0:T(8,128)(2,1)S(1)} %collective-permute-done.3.refs_3_) | copy-start | bytes 1474564
  44.4 21.1 %collective-permute-start.10 = (bf16[960,256]{1,0:T(8,128)(2,1)S(1)}, bf16[960,256]{1,0:T(8,128)(2,1)}, u32[]{:S(2)}, u32[]{:S(2)}) collective-permute-start(bf16[960,256]{1,0:T(8,128)(2,1)S(1)} %collective-permute-done.1.refs_1_), channel_id=1, source_target_pairs={{0,192},{64,0},{128,64},{192,128},{1,193},{65,1},{129,65},{193,129... | collective-permute-start | bytes 1474568 | tf_op jit(solution)/shard_map/ppermute | solution.py:17
  54.9 40.9 %copy-start.17 = (bf16[960,256]{1,0:T(8,128)(2,1)}, bf16[960,256]{1,0:T(8,128)(2,1)S(1)}, u32[]{:S(2)}) copy-start(bf16[960,256]{1,0:T(8,128)(2,1)S(1)} %collective-permute-done.7.refs_7_) | copy-start | bytes 1474564
  54.9 15.9 %collective-permute-start.9 = (bf16[960,256]{1,0:T(8,128)(2,1)S(1)}, bf16[960,256]{1,0:T(8,128)(2,1)}, u32[]{:S(2)}, u32[]{:S(2)}) collective-permute-start(bf16[960,256]{1,0:T(8,128)(2,1)S(1)} %collective-permute-done.1.refs_1_), channel_id=1, source_target_pairs={{0,64},{64,128},{128,192},{192,0},{1,65},{65,129},{129,193},{193,1... | collective-permute-start | bytes 1474568 | tf_op jit(solution)/shard_map/ppermute | solution.py:17
  56.0 25.4 %collective-permute-start.6 = (bf16[960,256]{1,0:T(8,128)(2,1)S(1)}, bf16[960,256]{1,0:T(8,128)(2,1)}, u32[]{:S(2)}, u32[]{:S(2)}) collective-permute-start(bf16[960,256]{1,0:T(8,128)(2,1)S(1)} %collective-permute-done.4.refs_4_), channel_id=1, source_target_pairs={{0,64},{64,128},{128,192},{192,0},{1,65},{65,129},{129,193},{193,1... | collective-permute-start | bytes 1474568 | tf_op jit(solution)/shard_map/ppermute | solution.py:17
  57.5 26.8 %collective-permute-start.15 = (bf16[960,256]{1,0:T(8,128)(2,1)S(1)}, bf16[960,256]{1,0:T(8,128)(2,1)}, u32[]{:S(2)}, u32[]{:S(2)}) collective-permute-start(bf16[960,256]{1,0:T(8,128)(2,1)S(1)} %collective-permute-done.7.refs_7_), channel_id=1, source_target_pairs={{0,192},{64,0},{128,64},{192,128},{1,193},{65,1},{129,65},{193,129... | collective-permute-start | bytes 1474568 | tf_op jit(solution)/shard_map/ppermute | solution.py:17
  65.4 50.1 %collective-permute-start.13 = (bf16[960,256]{1,0:T(8,128)(2,1)}, bf16[960,256]{1,0:T(8,128)(2,1)}, u32[]{:S(2)}, u32[]{:S(2)}) collective-permute-start(bf16[960,256]{1,0:T(8,128)(2,1)} %collective-permute-done.5.refs_5_), channel_id=1, source_target_pairs={{0,64},{64,128},{128,192},{192,0},{1,65},{65,129},{129,193},{193,1... | collective-permute-start | bytes 1474568 | tf_op jit(solution)/shard_map/ppermute | solution.py:17
  70.8 44.8 %collective-permute-start.14 = (bf16[960,256]{1,0:T(8,128)(2,1)}, bf16[960,256]{1,0:T(8,128)(2,1)}, u32[]{:S(2)}, u32[]{:S(2)}) collective-permute-start(bf16[960,256]{1,0:T(8,128)(2,1)} %collective-permute-done.5.refs_5_), channel_id=1, source_target_pairs={{0,192},{64,0},{128,64},{192,128},{1,193},{65,1},{129,65},{193,129... | collective-permute-start | bytes 1474568 | tf_op jit(solution)/shard_map/ppermute | solution.py:17
  81.3 34.2 %collective-permute-start.12 = (bf16[960,256]{1,0:T(8,128)(2,1)}, bf16[960,256]{1,0:T(8,128)(2,1)}, u32[]{:S(2)}, u32[]{:S(2)}) collective-permute-start(bf16[960,256]{1,0:T(8,128)(2,1)} %collective-permute-done.11.refs_2_), channel_id=1, source_target_pairs={{0,32},{32,0},{1,33},{33,1},{2,34},{34,2},{3,35},{35,3},{4,36},{36... | collective-permute-start | bytes 1474568 | tf_op jit(solution)/shard_map/ppermute | solution.py:17
  84.3 31.3 %collective-permute-start.16 = (bf16[960,256]{1,0:T(8,128)(2,1)}, bf16[960,256]{1,0:T(8,128)(2,1)}, u32[]{:S(2)}, u32[]{:S(2)}) collective-permute-start(bf16[960,256]{1,0:T(8,128)(2,1)} %collective-permute-done.15.refs_6_), channel_id=1, source_target_pairs={{0,32},{32,0},{1,33},{33,1},{2,34},{34,2},{3,35},{35,3},{4,36},{36... | collective-permute-start | bytes 1474568 | tf_op jit(solution)/shard_map/ppermute | solution.py:17
  85.4 3.2 %copy-start.5 = (bf16[192,80,256]{2,1,0:T(8,128)(2,1)S(1)}, bf16[192,80,256]{2,1,0:T(8,128)(2,1)}, u32[]{:S(2)}) copy-start(bf16[192,80,256]{2,1,0:T(8,128)(2,1)} %shots.1) | copy-start | bytes 23592964
  95.9 3.1 %copy-start.1 = (bf16[80,192,256]{2,1,0:T(8,128)(2,1)}, bf16[80,192,256]{2,1,0:T(8,128)(2,1)S(1)}, u32[]{:S(2)}) copy-start(bf16[80,192,256]{2,1,0:T(8,128)(2,1)S(1)} %rows_major.2.own) | copy-start | bytes 23592964
  103.1 1.0 copy-start.9
  104.1 1.0 copy-start.12
  105.1 1.0 copy-start.15
  106.2 1.0 copy-start.18
  115.5 35.2 %collective-permute-start = (bf16[96,192]{1,0:T(8,128)(2,1)}, bf16[96,192]{1,0:T(8,128)(2,1)}, u32[]{:S(2)}, u32[]{:S(2)}) collective-permute-start(bf16[96,192]{1,0:T(8,128)(2,1)} %fusion.13), channel_id=1, source_target_pairs={{0,16},{16,0},{1,17},{17,1},{2,18},{18,2},{3,19},{19,3},{4,20},{20... | collective-permute-start | bytes 110600 | tf_op jit(solution)/shard_map/ppermute | solution.py:17
  117.4 20.9 %slice-start = ((s8[7864320]{0:T(1024)(128)(4,1)}), s8[3670016]{0:T(1024)(128)(4,1)S(1)}, s32[]{:S(2)}) async-start(s8[7864320]{0:T(1024)(128)(4,1)} %bitcast.10), calls=%async_computation.1 | async-start | bytes 7340032
  124.9 1.3 copy-start.6
  126.2 12.1 %slice-start.1 = ((s8[7864320]{0:T(1024)(128)(4,1)}), s8[4194304]{0:T(1024)(128)(4,1)S(1)}, s32[]{:S(2)}) async-start(s8[7864320]{0:T(1024)(128)(4,1)} %bitcast.10), calls=%async_computation.2 | async-start | bytes 8388608
  126.2 12.1 %copy-start.7 = (bf16[80,48,256]{2,1,0:T(8,128)(2,1)S(1)}, bf16[80,48,256]{2,1,0:T(8,128)(2,1)}, u32[]{:S(2)}) copy-start(bf16[80,48,256]{2,1,0:T(8,128)(2,1)} %copy-done.6) | copy-start | bytes 5898244
  135.2 3.1 %copy-start.2 = (bf16[80,192,256]{2,1,0:T(8,128)(2,1)}, bf16[80,192,256]{2,1,0:T(8,128)(2,1)S(1)}, u32[]{:S(2)}) copy-start(bf16[80,192,256]{2,1,0:T(8,128)(2,1)S(1)} %rows_major.3.beside) | copy-start | bytes 23592964
  138.3 12.2 %copy-start.26 = (s32[192,192]{1,0:T(8,128)S(1)}, s32[192,192]{1,0:T(8,128)}, u32[]{:S(2)}) copy-start(s32[192,192]{1,0:T(8,128)} %param.9) | copy-start | bytes 442372
  149.0 6.4 %collective-permute-start.18 = (f32[96,384]{1,0:T(8,128)}, f32[96,384]{1,0:T(8,128)S(1)}, u32[]{:S(2)}, u32[]{:S(2)}) collective-permute-start(f32[96,384]{1,0:T(8,128)} %partial_scores.1), channel_id=1, source_target_pairs={{0,1},{1,0},{2,3},{3,2},{4,5},{5,4},{6,7},{7,6},{8,9},{9,8},{10,11... | collective-permute-start | bytes 442376 | tf_op jit(solution)/shard_map/ppermute | solution.py:17
  157.5 1.9 collective-permute-start.19
  157.6 3.7 %collective-permute-start.20 = (f32[2,384]{1,0:T(2,128)S(1)}, f32[2,384]{1,0:T(2,128)S(1)}, u32[]{:S(2)}, u32[]{:S(2)}) collective-permute-start(f32[2,384]{1,0:T(2,128)S(1)} %fusion.19), channel_id=1, source_target_pairs={{0,2},{2,0},{4,6},{6,4},{8,10},{10,8},{12,14},{14,12},{16,18},{18,... | collective-permute-start | bytes 9224 | tf_op jit(solution)/shard_map/ppermute | solution.py:318
  158.2 3.1 %collective-permute-start.21 = (f32[2,384]{1,0:T(2,128)S(1)}, f32[2,384]{1,0:T(2,128)S(1)}, u32[]{:S(2)}, u32[]{:S(2)}) collective-permute-start(f32[2,384]{1,0:T(2,128)S(1)} %fusion.19), channel_id=1, source_target_pairs={{0,18},{2,16},{4,22},{6,20},{8,26},{10,24},{12,30},{14,28},{16,2},... | collective-permute-start | bytes 9224 | tf_op jit(solution)/shard_map/ppermute | solution.py:318
  161.3 26.1 %collective-permute-start.22 = (f32[2,384]{1,0:T(2,128)S(1)}, f32[2,384]{1,0:T(2,128)S(1)}, u32[]{:S(2)}, u32[]{:S(2)}) collective-permute-start(f32[2,384]{1,0:T(2,128)S(1)} %pad_maximum_fusion.3), channel_id=1, source_target_pairs={{0,4},{2,6},{4,0},{6,2},{8,12},{10,14},{12,8},{14,10},{16,20},{18,... | collective-permute-start | bytes 9224 | tf_op jit(solution)/shard_map/ppermute | solution.py:318
  164.6 22.8 %collective-permute-start.23 = (f32[2,384]{1,0:T(2,128)S(1)}, f32[2,384]{1,0:T(2,128)S(1)}, u32[]{:S(2)}, u32[]{:S(2)}) collective-permute-start(f32[2,384]{1,0:T(2,128)S(1)} %pad_maximum_fusion.3), channel_id=1, source_target_pairs={{0,8},{2,10},{4,12},{6,14},{8,0},{10,2},{12,4},{14,6},{16,24},{18,... | collective-permute-start | bytes 9224 | tf_op jit(solution)/shard_map/ppermute | solution.py:318
  169.6 17.8 %collective-permute-start.24 = (f32[2,384]{1,0:T(2,128)S(1)}, f32[2,384]{1,0:T(2,128)S(1)}, u32[]{:S(2)}, u32[]{:S(2)}) collective-permute-start(f32[2,384]{1,0:T(2,128)S(1)} %pad_maximum_fusion.3), channel_id=1, source_target_pairs={{0,12},{2,14},{4,8},{6,10},{8,4},{10,6},{12,0},{14,2},{16,28},{18,... | collective-permute-start | bytes 9224 | tf_op jit(solution)/shard_map/ppermute | solution.py:318
  170.5 1.0 copy-start.10
  171.5 1.0 copy-start.13
  172.5 1.0 copy-start.16
  178.7 1.9 copy-start.3
  185.5 1.9 copy-start.4
  203.3 26.8 %all-to-all-start = ((bf16[256,2,256]{2,1,0:T(2,128)(2,1)}), bf16[256,2,256]{2,1,0:T(2,128)(2,1)S(1)}, u32[]{:S(2)}, u32[]{:S(2)}) async-start(bf16[256,2,256]{2,1,0:T(2,128)(2,1)} %reshape.48), calls=%async_computation | async-start | bytes 524288 | tf_op jit(solution)/shard_map/all_to_all | solution.py:376
  (7 other events, 5.9 us)

commit v2 on v1

v2 whole, which is shorter than its diff:
```python
import jax
import jax.numpy as jnp
from jax import lax
from jax.experimental import pallas as pl
from jax.experimental.pallas import tpu as pltpu
from jax.sharding import Mesh
from jax.sharding import PartitionSpec as P

IMG = ("y", "xh", "core")
BF16 = jnp.bfloat16
F32 = jnp.float32
SOURCES = ((0, 0), (0, 1), (-1, 0), (1, 0), (-1, 1), (1, 1), (2, 0), (2, 1))


def shifted(x, axis, step):
    n = lax.axis_size(axis)
    return lax.ppermute(x, axis, [(i, (i + step) % n) for i in range(n)])


def gathered(near, far):
    beside = shifted(near, "xh", 1)
    up = shifted(near, "y", 1)
    down = shifted(near, "y", -1)
    far = shifted(far, "slab", 1)
    across = shifted(up, "y", 1)
    beside_down = shifted(beside, "y", -1)
    beside_up = shifted(beside, "y", 1)
    far_beside = shifted(far, "xh", 1)
    far_down = shifted(far, "y", -1)
    far_up = shifted(far, "y", 1)
    far_across = shifted(far_down, "y", -1)
    far_beside_down = shifted(far_beside, "y", -1)
    far_beside_up = shifted(far_beside, "y", 1)
    across_beside = shifted(across, "xh", 1)
    far_across_beside = shifted(far_across, "xh", 1)
    return (
        [near, beside, up, down, beside_up, beside_down, across, across_beside],
        [far, far_beside, far_up, far_down, far_beside_up, far_beside_down, far_across, far_across_beside],
    )


def placed_rows(weights, row_first, row_count, half, half_rows):
    owned, reach, _ = weights.shape
    row = lax.broadcasted_iota(jnp.int32, (owned, half_rows, reach), 1)
    entry = lax.broadcasted_iota(jnp.int32, (owned, half_rows, reach), 2)
    at = half * half_rows + row - row_first[:, :, None]
    chosen = (entry == at) & (entry < row_count[:, :, None])
    return jnp.einsum("orj,ojl->orl", chosen.astype(BF16), weights, preferred_element_type=BF16)


def weighted_kernel(*refs):
    chips = (len(refs) - 8) // 2
    chunks = refs[: 2 * chips]
    lines, lines_far, noise, out, quad, wide, taken, done = refs[2 * chips :]
    rows = out.shape[0]
    pitch = rows + 1
    step = noise.shape[0]
    some = step // rows
    owned = chunks[0].shape[0] // rows
    fetch = lambda chip, side: pltpu.make_async_copy(
        chunks[side * chips + chip], taken.at[chip, side], done.at[chip, side]
    )
    for chip in range(chips):
        for side in range(2):
            fetch(chip, side).start()
    for chip in range(chips):
        for side in range(2):
            fetch(chip, side).wait()
        for i in range(owned // some):
            at = slice(i * step, (i + 1) * step)
            slices = jnp.dot(taken[chip, 0, at, :], lines[...], preferred_element_type=F32)
            slices += jnp.dot(taken[chip, 1, at, :], lines_far[...], preferred_element_type=F32)
            slices = slices.astype(BF16).astype(F32)
            weighted = noise[...] * slices
            first = chip * owned + i * some
            for k in range(some):
                one = weighted[k * rows : (k + 1) * rows, :]
                to = slice((first + k) * pitch, (first + k) * pitch + rows)
                wide[0, to, :] = one[:, :128]
                wide[1, to, :] = one[:, 128:]
            square = weighted * slices
            square = square[:, :128] + square[:, 128:]
            quad[first : first + some] = jnp.sum(square.reshape(some, rows // 8, 8, 128), axis=1)

    def turn(r, carry):
        for half in range(2):
            out[r, :, half * 128 : half * 128 + 128] = wide[
                half, pl.ds(r, chips * owned, stride=pitch), :
            ].astype(BF16)
        return carry

    lax.fori_loop(0, rows, turn, 0, unroll=8)


def weighted_slices(near, far, lines, lines_far, noise, rows):
    chips = len(near)
    count = chips * near[0].shape[0] // rows
    width = lines.shape[1]
    there = pl.BlockSpec(memory_space=pl.ANY)
    here = pl.BlockSpec(memory_space=pltpu.VMEM)
    return pl.pallas_call(
        weighted_kernel,
        in_specs=[there] * (2 * chips) + [here] * 3,
        out_shape=(
            jax.ShapeDtypeStruct((rows, count, width), BF16),
            jax.ShapeDtypeStruct((count, 8, 128), F32),
        ),
        scratch_shapes=[
            pltpu.VMEM((2, count * (rows + 1), 128), F32),
            pltpu.VMEM((chips, 2, *near[0].shape), BF16),
            pltpu.SemaphoreType.DMA((chips, 2)),
        ],
        compiler_params=pltpu.CompilerParams(vmem_limit_bytes=16 << 20),
        name="weighted_slices",
    )(*near, *far, lines, lines_far, noise)


def score_kernel(first, second, quad_first, quad_second, own, beside, out, acc):
    rows, shots, _ = own.shape
    block = 8
    acc[...] = jnp.zeros_like(acc)

    def add(i, carry):
        at = [i * block + r for r in range(block)]
        slices = jnp.concatenate(
            [jnp.concatenate([first[r], second[r]], axis=0) for r in at], axis=1
        )
        for k, shot in enumerate((own, beside)):
            acc[k] += lax.dot_general(
                slices,
                jnp.concatenate([shot[r] for r in at], axis=1),
                (((1,), (1,)), ((), ())),
                preferred_element_type=F32,
            )
        return carry

    lax.fori_loop(0, rows // block, add, 0)
    quad = jnp.concatenate([jnp.sum(quad_first[...], axis=1), jnp.sum(quad_second[...], axis=1)], axis=0)
    half = 0.5 * jnp.sum(quad, axis=1, keepdims=True)
    out[:, :shots] = acc[0] - half
    out[:, shots:] = acc[1] - half


def partial_scores(first, second, quad_first, quad_second, own, beside):
    _, shots, _ = own.shape
    count = first.shape[1]
    return pl.pallas_call(
        score_kernel,
        out_shape=jax.ShapeDtypeStruct((2 * count, 2 * shots), F32),
        scratch_shapes=[pltpu.VMEM((2, 2 * count, shots), F32)],
        compiler_params=pltpu.CompilerParams(vmem_limit_bytes=4 << 20),
        name="partial_scores",
    )(first, second, quad_first, quad_second, own, beside)


def rows_major_kernel(shots, out, taken, given, wide, came, went):
    total, rows, _ = shots.shape
    block = taken.shape[1]
    pitch = rows + 1
    steps = total // block
    span = lambda i: slice(i * block, (i + 1) * block)
    fetch = lambda i: pltpu.make_async_copy(shots.at[span(i)], taken.at[i % 2], came.at[i % 2])
    give = lambda i: pltpu.make_async_copy(given.at[i % 2], out.at[:, span(i), :], went.at[i % 2])
    fetch(0).start()
    for i in range(steps):
        if i + 1 < steps:
            fetch(i + 1).start()
        fetch(i).wait()

        def spread(n, carry, i=i):
            for k in range(8):
                one = taken[i % 2, n * 8 + k].astype(F32)
                at = pl.multiple_of(n * 8 * pitch, 8) + k * pitch
                wide[0, pl.ds(at, rows), :] = one[:, :128]
                wide[1, pl.ds(at, rows), :] = one[:, 128:]
            return carry

        lax.fori_loop(0, block // 8, spread, 0)
        if i >= 2:
            give(i - 2).wait()

        def turn(r, carry, i=i):
            for half in range(2):
                given[i % 2, r, :, half * 128 : half * 128 + 128] = wide[
                    half, pl.ds(r, block, stride=pitch), :
                ].astype(BF16)
            return carry

        lax.fori_loop(0, rows, turn, 0, unroll=8)
        give(i).start()
    for i in range(max(steps - 2, 0), steps):
        give(i).wait()


def rows_major(images, block=48):
    shots, rows, width = images.shape
    return pl.pallas_call(
        rows_major_kernel,
        in_specs=[pl.BlockSpec(memory_space=pl.ANY)],
        out_specs=pl.BlockSpec(memory_space=pltpu.HBM),
        out_shape=jax.ShapeDtypeStruct((rows, shots, width), BF16),
        scratch_shapes=[
            pltpu.VMEM((2, block, rows, width), BF16),
            pltpu.VMEM((2, rows, block, width), BF16),
            pltpu.VMEM((2, block * (rows + 1), 128), F32),
            pltpu.SemaphoreType.DMA((2,)),
            pltpu.SemaphoreType.DMA((2,)),
        ],
        compiler_params=pltpu.CompilerParams(vmem_limit_bytes=14 << 20),
        name="rows_major",
    )(images)


def choice_kernel(my_y, my_x, my_core, mask, kept, sent):
    shape = (kept.shape[0], mask.shape[1])
    owned = shape[0] // len(SOURCES)
    row = lax.broadcasted_iota(jnp.int32, shape, 0)
    column = lax.broadcasted_iota(jnp.int32, shape, 1)
    values = mask[...].astype(F32).astype(BF16)
    for out, core in ((kept, my_core[0]), (sent, 1 - my_core[0])):
        wanted = jnp.zeros(shape, jnp.int32)
        for at, (dy, dx) in enumerate(SOURCES):
            chip = ((my_y[0] + (dy + 4)) & 3) * 2 + ((my_x[0] + dx) & 1)
            first = (chip * 2 + core) * owned - at * owned
            wanted = jnp.where(row >= at * owned, first, wanted)
        chosen = jnp.where(column == row + wanted, 1.0, 0.0).astype(BF16)
        out[...] = lax.dot_general(
            chosen, values, (((1,), (1,)), ((), ())), preferred_element_type=F32
        ).astype(BF16)


def mask_choice(my_y, my_x, my_core, mask, count):
    shape = jax.ShapeDtypeStruct((count, mask.shape[0]), BF16)
    scalar = pl.BlockSpec(memory_space=pltpu.SMEM)
    return pl.pallas_call(
        choice_kernel,
        in_specs=[scalar] * 3 + [pl.BlockSpec(memory_space=pltpu.VMEM)],
        out_shape=(shape, shape),
        compiler_params=pltpu.CompilerParams(vmem_limit_bytes=4 << 20),
        name="mask_choice",
    )(my_y.reshape(1), my_x.reshape(1), my_core.reshape(1), mask)


def turn_kernel(*refs):
    chunks, out, flat = refs[:-2], refs[-2], refs[-1]
    half = len(chunks) // 2
    size, lines = chunks[0].shape
    for side in range(2):
        for i in range(half):
            flat[side, i * size : (i + 1) * size, :] = chunks[side * half + i][...]
    for side in range(2):

        def turn(i, carry, side=side):
            at = pl.multiple_of(i * 128, 128)
            out[side * lines : (side + 1) * lines, pl.ds(at, 128)] = flat[side, pl.ds(at, 128), :].T
            return carry

        lax.fori_loop(0, half * size // 128, turn, 0, unroll=2)


def turned_weights(near, far):
    size, lines = near[0].shape
    span = len(near) * size
    return pl.pallas_call(
        turn_kernel,
        out_shape=jax.ShapeDtypeStruct((2 * lines, span), BF16),
        scratch_shapes=[pltpu.VMEM((2, span, lines), BF16)],
        compiler_params=pltpu.CompilerParams(vmem_limit_bytes=13 << 20),
        name="turned_weights",
    )(*near, *far)


def insert_kernel(
    slab, scores, allowed, stats, own, beside, turned, turned_too, out, post_own, post_beside, wide, flat
):
    rows, shots, _ = own.shape
    pitch = rows + 1
    count = scores.shape[0]
    lines = out.shape[1]
    block = 8
    mass = jnp.exp(scores[...] - stats[0:1, :])
    post = jnp.where(allowed[...] > 0.5, mass, 0.0) / stats[1:2, :]
    post_own[...] = post[:, :shots].astype(BF16)
    post_beside[...] = post[:, shots:].astype(BF16)

    def gather(i, carry):
        for r in range(block):
            sums = jnp.dot(post_own[...], own[i * block + r], preferred_element_type=F32)
            sums += jnp.dot(post_beside[...], beside[i * block + r], preferred_element_type=F32)
            for half in range(2):
                wide[half, pl.ds(i * block + r, count, stride=pitch), :] = sums[
                    :, half * 128 : half * 128 + 128
                ]
        return carry

    lax.fori_loop(0, rows // block, gather, 0)

    def narrow(i, carry):
        for k in range(8):
            at = pl.multiple_of(i * 8 * pitch, 8) + k * pitch
            to = pl.multiple_of(i * 8 * rows, 16) + k * rows
            for half in range(2):
                flat[pl.ds(to, rows), half * 128 : half * 128 + 128] = wide[
                    half, pl.ds(at, rows), :
                ].astype(BF16)
        return carry

    lax.fori_loop(0, count // 8, narrow, 0)
    split = count * rows // 2
    for side, slot in ((0, slab[0]), (1, 1 - slab[0])):
        part = slice(side * lines, (side + 1) * lines)
        total = jnp.dot(turned[part, :], flat[:split, :], preferred_element_type=F32)
        total += jnp.dot(turned_too[part, :], flat[split:, :], preferred_element_type=F32)
        out[slot] = total.astype(BF16)


def insertion(slab, scores, allowed, stats, own, beside, turned, turned_too):
    rows, shots, width = own.shape
    count = scores.shape[0]
    lines = turned.shape[0] // 2
    return pl.pallas_call(
        insert_kernel,
        in_specs=[pl.BlockSpec(memory_space=pltpu.SMEM)]
        + [pl.BlockSpec(memory_space=pltpu.VMEM)] * 7,
        out_shape=jax.ShapeDtypeStruct((2, lines, width), BF16),
        scratch_shapes=[
            pltpu.VMEM((count, shots), BF16),
            pltpu.VMEM((count, shots), BF16),
            pltpu.VMEM((2, count * (rows + 1), 128), F32),
            pltpu.VMEM((count * rows, width), BF16),
        ],
        compiler_params=pltpu.CompilerParams(vmem_limit_bytes=14 << 20),
        name="insertion",
    )(slab, scores, allowed, stats, own, beside, turned, turned_too)


def crossed(x, axes, mask):
    return lax.ppermute(x, axes, [(i, i ^ mask) for i in range(lax.axis_size(axes))])


def combined(pairs):
    highest = jnp.max(jnp.stack([p[0] for p in pairs]), axis=0)
    total = sum(p[1] * jnp.exp(p[0] - highest) for p in pairs)
    return jnp.stack([highest, total])


def in_core_order(stats, core, shots):
    swapped = jnp.concatenate([stats[:, shots:], stats[:, :shots]], axis=1)
    return jnp.where(core == 0, stats, swapped)


def step(images, noise_weight, prior_mask, volume, interp_weights, row_first, row_count):
    owned, _, line_span = interp_weights.shape
    shots, half_rows, width = images.shape
    slab = lax.axis_index("slab")
    core = lax.axis_index("core")
    lines = volume.reshape(line_span, width)

    near = placed_rows(interp_weights, row_first, row_count, slab, half_rows)
    far = placed_rows(interp_weights, row_first, row_count, 1 - slab, half_rows)
    flat = lambda x: x.reshape(owned * half_rows, line_span)
    near, far = gathered(flat(near), flat(far))
    lines_far = shifted(lines, "slab", 1)

    beside = shifted(images, "core", 1)
    own = rows_major(images)
    beside = rows_major(beside)

    kept, sent = mask_choice(
        lax.axis_index("y"), lax.axis_index("xh"), core, prior_mask, len(SOURCES) * owned
    )
    allowed = jnp.concatenate([kept, shifted(sent, "core", 1)], axis=1).astype(F32)

    noise_both = jnp.concatenate([noise_weight, noise_weight], axis=1)
    noise_tiled = jnp.tile(noise_both, (3, 1))
    weigh = lambda pick: weighted_slices(
        near[pick], far[pick], lines, lines_far, noise_tiled, half_rows
    )
    first, quad_first = weigh(slice(0, 4))
    second, quad_second = weigh(slice(4, 8))
    part = partial_scores(first, second, quad_first, quad_second, own, beside)
    turned = turned_weights(near[:4], far[:4])
    turned_too = turned_weights(near[4:], far[4:])
    scores = part + shifted(part, "slab", 1)

    top = jnp.max(jnp.where(allowed > 0.5, scores, -1e30), axis=0)
    mass = jnp.sum(jnp.where(allowed > 0.5, jnp.exp(scores - top[None]), 0.0), axis=0)
    pair = in_core_order(jnp.stack([top, mass]), core, shots)
    for masks in ((8, 1, 9), (2, 4, 6)):
        pair = combined([pair] + [crossed(pair, ("core", "ori"), m) for m in masks])
    pair = in_core_order(pair, core, shots)
    log_evidence = (pair[0] + jnp.log(pair[1]))[:shots]

    into = insertion(slab.reshape(1), scores, allowed, pair, own, beside, turned, turned_too)
    into = into.reshape(-1, volume.shape[1], width)
    arrived = lax.all_to_all(into, ("slab",) + IMG + ("ori",), 0, 0, tiled=True)
    inserted = jnp.sum(arrived.astype(F32), axis=0, keepdims=True)
    return log_evidence, inserted


def solution(mesh):
    torus = Mesh(
        mesh.devices.reshape(4, 2, 2, mesh.shape["ori"], mesh.shape["slab"]),
        ("y", "xh", "core", "ori", "slab"),
    )
    owner = ("ori",) + IMG
    in_specs = (
        P(IMG, "slab", None),
        P("slab", None),
        P(IMG, "ori"),
        P(None, "slab", None),
        P(owner, None, "slab"),
        P(owner, "slab"),
        P(owner, "slab"),
    )
    out_specs = (P(IMG), P(IMG + ("ori",), "slab", None))
    return jax.shard_map(step, mesh=torus, in_specs=in_specs, out_specs=out_specs, check_vma=False)
```

time: 234 us -> 190 us (0.81)
  Pallas kernels: 64.6 us -> 41 us
  local copies, waits for them, and re-layouts: 31.9 us -> 18.6 us
  starting transfers between devices: 52.8 us -> 49.8 us
  other arithmetic: 8.3 us -> 5.7 us
    pallas_call x6 -> x7, Pallas kernels: 55.6 us -> 35.2 us  [the longest x2 11.2 us: rows_major(): pl.pallas_call(rows_major_kernel, in_specs=[pl.BlockSpec(memory_space=pl....]
    unnamed x58 -> x62, local copies, waits for them, and re-layouts: 28.5 us -> 16.8 us
    all_to_all x1, starting transfers between devices: 12 us -> 8.61 us  [step(): arrived = lax.all_to_all(into, ('slab',) + IMG + ('ori',), 0, 0, tiled=True)]
    pallas_call x2, Pallas kernels: 9.01 us -> 5.77 us  [turned_weights(): pl.pallas_call(turn_kernel, out_shape=jax.ShapeDtypeStruct((2 * lines, sp...]
    add x8 -> x0, other arithmetic: 2.79 us -> none  [column_choice(): picks.append(first + jnp.arange(owned))]
  transfers between devices with their start and end apart: 26 -> 26, of which waited for: 9 -> 10; matrix products, arithmetic and copies ran while one was open for 5% -> 3% of each run, Pallas kernels for 22% -> 11%
where the time goes in v2:
time: 190 us; the launch traced here: 187 us
  waiting for transfers between devices  68.4 us (36%)
  starting transfers between devices  49.8 us (26%)
  Pallas kernels  41 us (22%)
  local copies, waits for them, and re-layouts  18.6 us (10%)
  other arithmetic  5.7 us (3%)
  matrix products  2.01 us (1%)
    ppermute x19, waiting for transfers between devices, shifted(): return lax.ppermute(x, axis, [(i, (i + step) % n) for i in range(n)])  52.4 us
    ppermute x19, starting transfers between devices, shifted(): return lax.ppermute(x, axis, [(i, (i + step) % n) for i in range(n)])  31.1 us
    unnamed x62, local copies, waits for them, and re-layouts  16.8 us
    all_to_all x1, waiting for transfers between devices, step(): arrived = lax.all_to_all(into, ('slab',) + IMG + ('ori',), 0, 0, tiled=True)  14.2 us
    pallas_call x2, Pallas kernels, rows_major(): pl.pallas_call(rows_major_kernel, in_specs=[pl.BlockSpec(memory_space=pl....  11.2 us
    ppermute x6, starting transfers between devices, crossed(): lax.ppermute(x, axes, [(i, i ^ mask) for i in range(lax.axis_size(axes))])  10.2 us
    pallas_call x2, Pallas kernels, weighted_slices(): pl.pallas_call(weighted_kernel, in_specs=[there] * (2 * chips) + [here] *...  9.42 us
    all_to_all x1, starting transfers between devices, step(): arrived = lax.all_to_all(into, ('slab',) + IMG + ('ori',), 0, 0, tiled=True)  8.61 us
  transfers between devices with their start and end apart: 26, of which 10 were waited for; matrix products, arithmetic and copies ran while one was open for 3% of the time, Pallas kernels for 11%

profile of v2, /device:TPU:32, one launch (start us, length us, event | category | flops | bytes accessed | tf_op | source)
XLA Modules:
  0.0 186.6 jit_solution(9503041727831643785)
XLA Ops:
  1.7 1.0 fusion.4
  2.7 1.6 collective-permute-start.4
  4.3 1.0 fusion.2
  5.3 1.7 collective-permute-start.2
  7.0 2.7 %collective-permute-start.1 = (bf16[960,256]{1,0:T(8,128)(2,1)S(1)}, bf16[960,256]{1,0:T(8,128)(2,1)S(1)}, u32[]{:S(2)}, u32[]{:S(2)}) collective-permute-start(bf16[960,256]{1,0:T(8,128)(2,1)S(1)} %bitcast.16), channel_id=1, source_target_pairs={{0,32},{32,0},{1,33},{33,1},{2,34},{34,2},{3,35},{35,3},{4,36},{36... | collective-permute-start | bytes 1474568 | tf_op jit(solution)/shard_map/ppermute | solution.py:17
  9.7 1.0 reshape.56.refs_8_
  11.6 17.5 %collective-permute-done.8.refs_9_ = bf16[256,256]{1,0:T(8,128)(2,1)S(1)} collective-permute-done((bf16[256,256]{1,0:T(8,128)(2,1)S(1)}, bf16[256,256]{1,0:T(8,128)(2,1)S(1)}, u32[]{:S(2)}, u32[]{:S(2)}) %collective-permute-start.8) | collective-permute-done | bytes 131104 | tf_op jit(solution)/shard_map/ppermute | solution.py:17
  29.1 3.0 %collective-permute-start.3 = (bf16[960,256]{1,0:T(8,128)(2,1)S(1)}, bf16[960,256]{1,0:T(8,128)(2,1)S(1)}, u32[]{:S(2)}, u32[]{:S(2)}) collective-permute-start(bf16[960,256]{1,0:T(8,128)(2,1)S(1)} %bitcast.17), channel_id=1, source_target_pairs={{0,192},{64,0},{128,64},{192,128},{1,193},{65,1},{129,65},{193,129... | collective-permute-start | bytes 1474568 | tf_op jit(solution)/shard_map/ppermute | solution.py:17
  32.9 1.3 collective-permute-start.11
  34.2 3.0 %collective-permute-start.5 = (bf16[960,256]{1,0:T(8,128)(2,1)S(1)}, bf16[960,256]{1,0:T(8,128)(2,1)S(1)}, u32[]{:S(2)}, u32[]{:S(2)}) collective-permute-start(bf16[960,256]{1,0:T(8,128)(2,1)S(1)} %collective-permute-done.4.refs_4_), channel_id=1, source_target_pairs={{0,32},{32,0},{1,33},{33,1},{2,34},{34,2},{3,35},{35,3},{4,36},{36... | collective-permute-start | bytes 1474568 | tf_op jit(solution)/shard_map/ppermute | solution.py:17
  37.2 6.6 %collective-permute-done.3.refs_3_ = bf16[960,256]{1,0:T(8,128)(2,1)S(1)} collective-permute-done((bf16[960,256]{1,0:T(8,128)(2,1)S(1)}, bf16[960,256]{1,0:T(8,128)(2,1)S(1)}, u32[]{:S(2)}, u32[]{:S(2)}) %collective-permute-start.3) | collective-permute-done | bytes 491552 | tf_op jit(solution)/shard_map/ppermute | solution.py:17
  43.7 3.7 %collective-permute-start.10 = (bf16[960,256]{1,0:T(8,128)(2,1)S(1)}, bf16[960,256]{1,0:T(8,128)(2,1)S(1)}, u32[]{:S(2)}, u32[]{:S(2)}) collective-permute-start(bf16[960,256]{1,0:T(8,128)(2,1)S(1)} %collective-permute-done.1.refs_1_), channel_id=1, source_target_pairs={{0,192},{64,0},{128,64},{192,128},{1,193},{65,1},{129,65},{193,129... | collective-permute-start | bytes 1474568 | tf_op jit(solution)/shard_map/ppermute | solution.py:17
  47.4 6.8 %collective-permute-done.7.refs_7_ = bf16[960,256]{1,0:T(8,128)(2,1)S(1)} collective-permute-done((bf16[960,256]{1,0:T(8,128)(2,1)S(1)}, bf16[960,256]{1,0:T(8,128)(2,1)S(1)}, u32[]{:S(2)}, u32[]{:S(2)}) %collective-permute-start.7) | collective-permute-done | bytes 491552 | tf_op jit(solution)/shard_map/ppermute | solution.py:17
  54.3 1.0 collective-permute-start.9
  55.3 1.6 collective-permute-start.6
  56.9 1.7 collective-permute-start.15
  58.6 6.2 %collective-permute-done.10.refs_1_ = bf16[960,256]{1,0:T(8,128)(2,1)S(1)} collective-permute-done((bf16[960,256]{1,0:T(8,128)(2,1)S(1)}, bf16[960,256]{1,0:T(8,128)(2,1)S(1)}, u32[]{:S(2)}, u32[]{:S(2)}) %collective-permute-start.10) | collective-permute-done | bytes 491552 | tf_op jit(solution)/shard_map/ppermute | solution.py:17
  64.8 3.0 %collective-permute-start.12 = (bf16[960,256]{1,0:T(8,128)(2,1)S(1)}, bf16[960,256]{1,0:T(8,128)(2,1)S(1)}, u32[]{:S(2)}, u32[]{:S(2)}) collective-permute-start(bf16[960,256]{1,0:T(8,128)(2,1)S(1)} %collective-permute-done.11.refs_2_), channel_id=1, source_target_pairs={{0,32},{32,0},{1,33},{33,1},{2,34},{34,2},{3,35},{35,3},{4,36},{36... | collective-permute-start | bytes 1474568 | tf_op jit(solution)/shard_map/ppermute | solution.py:17
  67.8 2.2 %collective-permute-done.9.refs_0_ = bf16[960,256]{1,0:T(8,128)(2,1)S(1)} collective-permute-done((bf16[960,256]{1,0:T(8,128)(2,1)S(1)}, bf16[960,256]{1,0:T(8,128)(2,1)S(1)}, u32[]{:S(2)}, u32[]{:S(2)}) %collective-permute-start.9) | collective-permute-done | bytes 491552 | tf_op jit(solution)/shard_map/ppermute | solution.py:17
  70.0 10.5 %collective-permute-done.6.refs_6_ = bf16[960,256]{1,0:T(8,128)(2,1)S(1)} collective-permute-done((bf16[960,256]{1,0:T(8,128)(2,1)S(1)}, bf16[960,256]{1,0:T(8,128)(2,1)S(1)}, u32[]{:S(2)}, u32[]{:S(2)}) %collective-permute-start.6) | collective-permute-done | bytes 491552 | tf_op jit(solution)/shard_map/ppermute | solution.py:17
  80.6 2.0 %collective-permute-start.14 = (bf16[960,256]{1,0:T(8,128)(2,1)S(1)}, bf16[960,256]{1,0:T(8,128)(2,1)S(1)}, u32[]{:S(2)}, u32[]{:S(2)}) collective-permute-start(bf16[960,256]{1,0:T(8,128)(2,1)S(1)} %collective-permute-done.5.refs_5_), channel_id=1, source_target_pairs={{0,192},{64,0},{128,64},{192,128},{1,193},{65,1},{129,65},{193,129... | collective-permute-start | bytes 1474568 | tf_op jit(solution)/shard_map/ppermute | solution.py:17
  82.6 3.0 %collective-permute-start.16 = (bf16[960,256]{1,0:T(8,128)(2,1)S(1)}, bf16[960,256]{1,0:T(8,128)(2,1)S(1)}, u32[]{:S(2)}, u32[]{:S(2)}) collective-permute-start(bf16[960,256]{1,0:T(8,128)(2,1)S(1)} %collective-permute-done.15.refs_6_), channel_id=1, source_target_pairs={{0,32},{32,0},{1,33},{33,1},{2,34},{34,2},{3,35},{35,3},{4,36},{36... | collective-permute-start | bytes 1474568 | tf_op jit(solution)/shard_map/ppermute | solution.py:17
  85.6 3.2 %copy-done.4 = bf16[192,80,256]{2,1,0:T(8,128)(2,1)S(1)} copy-done((bf16[192,80,256]{2,1,0:T(8,128)(2,1)S(1)}, bf16[192,80,256]{2,1,0:T(8,128)(2,1)}, u32[]{:S(2)}) %copy-start.4) | copy-done | bytes 7864344
  88.8 5.0 %rows_major.2.own = bf16[80,192,256]{2,1,0:T(8,128)(2,1)S(1)} custom-call(bf16[192,80,256]{2,1,0:T(8,128)(2,1)S(1)} %copy-done.4), custom_call_target="tpu_custom_call" | custom-call | tf_op jit(solution)/shard_map/rows_major/pallas_call | solution.py:197
  94.9 4.7 %weighted_slices.2 = (bf16[80,48,256]{2,1,0:T(8,128)(2,1)S(1)}, f32[48,8,128]{2,1,0:T(8,128)S(1)}) custom-call(bf16[960,256]{1,0:T(8,128)(2,1)S(1)} %bitcast.18, bf16[960,256]{1,0:T(8,128)(2,1)S(1)} %collective-permute-done.1.refs_1_, bf16[960,256]{1,0:T(8,128)(2,1)S(1)} %collective-permute-done.2.refs_2_, ...), custom_call_target="tpu_custom_call" | custom-call | tf_op jit(solution)/shard_map/weighted_slices/pallas_call | solution.py:101
  99.7 4.7 %weighted_slices.3 = (bf16[80,48,256]{2,1,0:T(8,128)(2,1)S(1)}, f32[48,8,128]{2,1,0:T(8,128)S(1)}) custom-call(bf16[960,256]{1,0:T(8,128)(2,1)S(1)} %collective-permute-done.9.refs_0_, bf16[960,256]{1,0:T(8,128)(2,1)S(1)} %collective-permute-done.10.refs_1_, bf16[960,256]{1,0:T(8,128)(2,1)S(1)} %collective-permute-done.11.refs_2_, ...), custom_call_target="tpu_custom_call" | custom-call | tf_op jit(solution)/shard_map/weighted_slices/pallas_call | solution.py:101
  106.0 6.1 %rows_major.3.beside = bf16[80,192,256]{2,1,0:T(8,128)(2,1)S(1)} custom-call(bf16[192,80,256]{2,1,0:T(8,128)(2,1)} %collective-permute-done.17.shots), custom_call_target="tpu_custom_call" | custom-call | tf_op jit(solution)/shard_map/rows_major/pallas_call | solution.py:197
  112.2 7.2 %partial_scores.1 = f32[96,384]{1,0:T(8,128)} custom-call(bf16[80,48,256]{2,1,0:T(8,128)(2,1)S(1)} %get-tuple-element.10.first, bf16[80,48,256]{2,1,0:T(8,128)(2,1)S(1)} %get-tuple-element.11.second, f32[48,8,128]{2,1,0:T(8,128)S(1)} %get-tuple-element.12.quad_first, f32[48,8,128]{2,1,0:T(8,128)S(1)} %get-tuple-element.13.quad_second, ...), custom_call_target="tpu_custom_call" | custom-call | tf_op jit(solution)/shard_map/partial_scores/pallas_call | solution.py:147
  122.3 1.6 collective-permute-done
  123.9 0.9 collective-permute-done.18
  124.8 1.1 select_reduce_fusion.1
  127.3 1.7 collective-permute-start.21
  129.0 1.8 collective-permute-done.20
  130.9 3.4 %collective-permute-start.22 = (f32[2,384]{1,0:T(2,128)S(1)}, f32[2,384]{1,0:T(2,128)S(1)}, u32[]{:S(2)}, u32[]{:S(2)}) collective-permute-start(f32[2,384]{1,0:T(2,128)S(1)} %pad_maximum_fusion.3), channel_id=1, source_target_pairs={{0,4},{2,6},{4,0},{6,2},{8,12},{10,14},{12,8},{14,10},{16,20},{18,... | collective-permute-start | bytes 9224 | tf_op jit(solution)/shard_map/ppermute | solution.py:338
  134.2 4.9 %collective-permute-start.23 = (f32[2,384]{1,0:T(2,128)S(1)}, f32[2,384]{1,0:T(2,128)S(1)}, u32[]{:S(2)}, u32[]{:S(2)}) collective-permute-start(f32[2,384]{1,0:T(2,128)S(1)} %pad_maximum_fusion.3), channel_id=1, source_target_pairs={{0,8},{2,10},{4,12},{6,14},{8,0},{10,2},{12,4},{14,6},{16,24},{18,... | collective-permute-start | bytes 9224 | tf_op jit(solution)/shard_map/ppermute | solution.py:338
  140.1 1.0 copy-done.8
  141.1 1.0 copy-done.14
  142.1 2.9 %turned_weights.2.turned = bf16[512,3840]{1,0:T(8,128)(2,1)S(1)} custom-call(bf16[960,256]{1,0:T(8,128)(2,1)S(1)} %bitcast.19, bf16[960,256]{1,0:T(8,128)(2,1)S(1)} %collective-permute-done.1.refs_1_, bf16[960,256]{1,0:T(8,128)(2,1)S(1)} %collective-permute-done.2.refs_2_, bf16[960,256]{1,0:T(8,128)(2,1)S(1)} %collective-permute-done.3.refs_3_, ...), custom_call_target="tpu_custom_call" | custom-call | tf_op jit(solution)/shard_map/turned_weights/pallas_call | solution.py:264
  145.0 1.6 copy-done.12
  146.6 1.0 copy-done.16
  147.7 1.0 copy-done.18
  148.7 1.0 copy-done.20
  149.7 1.0 copy-done.22
  150.8 1.0 copy-done.24
  151.8 2.9 %turned_weights.3.turned_too = bf16[512,3840]{1,0:T(8,128)(2,1)S(1)} custom-call(bf16[960,256]{1,0:T(8,128)(2,1)S(1)} %copy-done.12, bf16[960,256]{1,0:T(8,128)(2,1)S(1)} %copy-done.10, bf16[960,256]{1,0:T(8,128)(2,1)S(1)} %copy-done.6, bf16[960,256]{1,0:T(8,128)(2,1)S(1)} %copy-done.18, bf16[960,256]{1,0:T(8,128)(2,1)S(1)} %copy-done.20, ...), custom_call_target="tpu_custom_call" | custom-call | tf_op jit(solution)/shard_map/turned_weights/pallas_call | solution.py:264
  154.9 6.6 %insertion.1 = bf16[2,256,256]{2,1,0:T(8,128)(2,1)S(1)} custom-call(s32[1]{0:T(128)} %bitcast.9.slab, f32[96,384]{1,0:T(8,128)S(1)} %get-tuple-element.19.scores, f32[96,384]{1,0:T(8,128)S(1)} %maximum_convert_fusion.allowed, f32[2,384]{1,0:T(2,128)S(1)} %fusion.12.stats, bf16[80,192,256]{2,1,0:T(8,128)(2,1)S(1)} %bitcast.14, ...), custom_call_target="tpu_custom_call" | custom-call | tf_op jit(solution)/shard_map/insertion/pallas_call | solution.py:321
  162.3 8.6 %all-to-all-start = ((bf16[256,2,256]{2,1,0:T(2,128)(2,1)}), bf16[256,2,256]{2,1,0:T(2,128)(2,1)S(1)}, u32[]{:S(2)}, u32[]{:S(2)}) async-start(bf16[256,2,256]{2,1,0:T(2,128)(2,1)} %reshape.58), calls=%async_computation | async-start | bytes 524288 | tf_op jit(solution)/shard_map/all_to_all | solution.py:396
  171.5 14.2 %all-to-all-done = bf16[256,2,256]{2,1,0:T(2,128)(2,1)S(1)} async-done(((bf16[256,2,256]{2,1,0:T(2,128)(2,1)}), bf16[256,2,256]{2,1,0:T(2,128)(2,1)S(1)}, u32[]{:S(2)}, u32[]{:S(2)}) %all-to-all-start) | async-done | bytes 262176 | tf_op jit(solution)/shard_map/all_to_all | solution.py:396
  (99 shorter events, 13.0 us)
Async XLA Ops:
  0.6 1.1 copy-start
  0.6 105.4 %collective-permute-start.17 = (bf16[192,80,256]{2,1,0:T(8,128)(2,1)}, bf16[192,80,256]{2,1,0:T(8,128)(2,1)}, u32[]{:S(2)}, u32[]{:S(2)}) collective-permute-start(bf16[192,80,256]{2,1,0:T(8,128)(2,1)} %shots.1), channel_id=1, source_target_pairs={{0,16},{16,0},{1,17},{17,1},{2,18},{18,2},{3,19},{19,3},{4,20},{20... | collective-permute-start | bytes 23592968 | tf_op jit(solution)/shard_map/ppermute | solution.py:17
  2.7 29.4 %collective-permute-start.4 = (bf16[960,256]{1,0:T(8,128)(2,1)S(1)}, bf16[960,256]{1,0:T(8,128)(2,1)S(1)}, u32[]{:S(2)}, u32[]{:S(2)}) collective-permute-start(bf16[960,256]{1,0:T(8,128)(2,1)S(1)} %bitcast.22), channel_id=1, source_target_pairs={{0,1},{1,0},{2,3},{3,2},{4,5},{5,4},{6,7},{7,6},{8,9},{9,8},{10,11... | collective-permute-start | bytes 1474568 | tf_op jit(solution)/shard_map/ppermute | solution.py:17
  5.3 27.6 %collective-permute-start.2 = (bf16[960,256]{1,0:T(8,128)(2,1)S(1)}, bf16[960,256]{1,0:T(8,128)(2,1)S(1)}, u32[]{:S(2)}, u32[]{:S(2)}) collective-permute-start(bf16[960,256]{1,0:T(8,128)(2,1)S(1)} %bitcast.15), channel_id=1, source_target_pairs={{0,64},{64,128},{128,192},{192,0},{1,65},{65,129},{129,193},{193,1... | collective-permute-start | bytes 1474568 | tf_op jit(solution)/shard_map/ppermute | solution.py:17
  7.0 27.2 %collective-permute-start.1 = (bf16[960,256]{1,0:T(8,128)(2,1)S(1)}, bf16[960,256]{1,0:T(8,128)(2,1)S(1)}, u32[]{:S(2)}, u32[]{:S(2)}) collective-permute-start(bf16[960,256]{1,0:T(8,128)(2,1)S(1)} %bitcast.16), channel_id=1, source_target_pairs={{0,32},{32,0},{1,33},{33,1},{2,34},{34,2},{3,35},{35,3},{4,36},{36... | collective-permute-start | bytes 1474568 | tf_op jit(solution)/shard_map/ppermute | solution.py:17
  10.7 18.5 %collective-permute-start.8 = (bf16[256,256]{1,0:T(8,128)(2,1)S(1)}, bf16[256,256]{1,0:T(8,128)(2,1)S(1)}, u32[]{:S(2)}, u32[]{:S(2)}) collective-permute-start(bf16[256,256]{1,0:T(8,128)(2,1)S(1)} %reshape.56.refs_8_), channel_id=1, source_target_pairs={{0,1},{1,0},{2,3},{3,2},{4,5},{5,4},{6,7},{7,6},{8,9},{9,8},{10,11... | collective-permute-start | bytes 393224 | tf_op jit(solution)/shard_map/ppermute | solution.py:17
  29.1 14.6 %collective-permute-start.3 = (bf16[960,256]{1,0:T(8,128)(2,1)S(1)}, bf16[960,256]{1,0:T(8,128)(2,1)S(1)}, u32[]{:S(2)}, u32[]{:S(2)}) collective-permute-start(bf16[960,256]{1,0:T(8,128)(2,1)S(1)} %bitcast.17), channel_id=1, source_target_pairs={{0,192},{64,0},{128,64},{192,128},{1,193},{65,1},{129,65},{193,129... | collective-permute-start | bytes 1474568 | tf_op jit(solution)/shard_map/ppermute | solution.py:17
  32.1 22.1 %collective-permute-start.7 = (bf16[960,256]{1,0:T(8,128)(2,1)S(1)}, bf16[960,256]{1,0:T(8,128)(2,1)S(1)}, u32[]{:S(2)}, u32[]{:S(2)}) collective-permute-start(bf16[960,256]{1,0:T(8,128)(2,1)S(1)} %collective-permute-done.4.refs_4_), channel_id=1, source_target_pairs={{0,192},{64,0},{128,64},{192,128},{1,193},{65,1},{129,65},{193,129... | collective-permute-start | bytes 1474568 | tf_op jit(solution)/shard_map/ppermute | solution.py:17
  32.9 22.4 %collective-permute-start.11 = (bf16[960,256]{1,0:T(8,128)(2,1)S(1)}, bf16[960,256]{1,0:T(8,128)(2,1)S(1)}, u32[]{:S(2)}, u32[]{:S(2)}) collective-permute-start(bf16[960,256]{1,0:T(8,128)(2,1)S(1)} %collective-permute-done.2.refs_2_), channel_id=1, source_target_pairs={{0,64},{64,128},{128,192},{192,0},{1,65},{65,129},{129,193},{193,1... | collective-permute-start | bytes 1474568 | tf_op jit(solution)/shard_map/ppermute | solution.py:17
  34.2 22.7 %collective-permute-start.5 = (bf16[960,256]{1,0:T(8,128)(2,1)S(1)}, bf16[960,256]{1,0:T(8,128)(2,1)S(1)}, u32[]{:S(2)}, u32[]{:S(2)}) collective-permute-start(bf16[960,256]{1,0:T(8,128)(2,1)S(1)} %collective-permute-done.4.refs_4_), channel_id=1, source_target_pairs={{0,32},{32,0},{1,33},{33,1},{2,34},{34,2},{3,35},{35,3},{4,36},{36... | collective-permute-start | bytes 1474568 | tf_op jit(solution)/shard_map/ppermute | solution.py:17
  43.7 21.1 %collective-permute-start.10 = (bf16[960,256]{1,0:T(8,128)(2,1)S(1)}, bf16[960,256]{1,0:T(8,128)(2,1)S(1)}, u32[]{:S(2)}, u32[]{:S(2)}) collective-permute-start(bf16[960,256]{1,0:T(8,128)(2,1)S(1)} %collective-permute-done.1.refs_1_), channel_id=1, source_target_pairs={{0,192},{64,0},{128,64},{192,128},{1,193},{65,1},{129,65},{193,129... | collective-permute-start | bytes 1474568 | tf_op jit(solution)/shard_map/ppermute | solution.py:17
  54.3 15.8 %collective-permute-start.9 = (bf16[960,256]{1,0:T(8,128)(2,1)S(1)}, bf16[960,256]{1,0:T(8,128)(2,1)S(1)}, u32[]{:S(2)}, u32[]{:S(2)}) collective-permute-start(bf16[960,256]{1,0:T(8,128)(2,1)S(1)} %collective-permute-done.1.refs_1_), channel_id=1, source_target_pairs={{0,64},{64,128},{128,192},{192,0},{1,65},{65,129},{129,193},{193,1... | collective-permute-start | bytes 1474568 | tf_op jit(solution)/shard_map/ppermute | solution.py:17
  55.3 44.3 %copy-start.5 = (bf16[960,256]{1,0:T(8,128)(2,1)}, bf16[960,256]{1,0:T(8,128)(2,1)S(1)}, u32[]{:S(2)}) copy-start(bf16[960,256]{1,0:T(8,128)(2,1)S(1)} %collective-permute-done.11.refs_2_) | copy-start | bytes 1474564
  55.3 25.2 %collective-permute-start.6 = (bf16[960,256]{1,0:T(8,128)(2,1)S(1)}, bf16[960,256]{1,0:T(8,128)(2,1)S(1)}, u32[]{:S(2)}, u32[]{:S(2)}) collective-permute-start(bf16[960,256]{1,0:T(8,128)(2,1)S(1)} %collective-permute-done.4.refs_4_), channel_id=1, source_target_pairs={{0,64},{64,128},{128,192},{192,0},{1,65},{65,129},{129,193},{193,1... | collective-permute-start | bytes 1474568 | tf_op jit(solution)/shard_map/ppermute | solution.py:17
  56.9 37.9 %copy-start.7 = (bf16[960,256]{1,0:T(8,128)(2,1)}, bf16[960,256]{1,0:T(8,128)(2,1)S(1)}, u32[]{:S(2)}) copy-start(bf16[960,256]{1,0:T(8,128)(2,1)S(1)} %collective-permute-done.5.refs_5_) | copy-start | bytes 1474564
  56.9 25.7 %collective-permute-start.15 = (bf16[960,256]{1,0:T(8,128)(2,1)S(1)}, bf16[960,256]{1,0:T(8,128)(2,1)S(1)}, u32[]{:S(2)}, u32[]{:S(2)}) collective-permute-start(bf16[960,256]{1,0:T(8,128)(2,1)S(1)} %collective-permute-done.7.refs_7_), channel_id=1, source_target_pairs={{0,192},{64,0},{128,64},{192,128},{1,193},{65,1},{129,65},{193,129... | collective-permute-start | bytes 1474568 | tf_op jit(solution)/shard_map/ppermute | solution.py:17
  64.8 34.9 %copy-start.9 = (bf16[960,256]{1,0:T(8,128)(2,1)}, bf16[960,256]{1,0:T(8,128)(2,1)S(1)}, u32[]{:S(2)}) copy-start(bf16[960,256]{1,0:T(8,128)(2,1)S(1)} %collective-permute-done.10.refs_1_) | copy-start | bytes 1474564
  64.8 34.8 %collective-permute-start.12 = (bf16[960,256]{1,0:T(8,128)(2,1)S(1)}, bf16[960,256]{1,0:T(8,128)(2,1)S(1)}, u32[]{:S(2)}, u32[]{:S(2)}) collective-permute-start(bf16[960,256]{1,0:T(8,128)(2,1)S(1)} %collective-permute-done.11.refs_2_), channel_id=1, source_target_pairs={{0,32},{32,0},{1,33},{33,1},{2,34},{34,2},{3,35},{35,3},{4,36},{36... | collective-permute-start | bytes 1474568 | tf_op jit(solution)/shard_map/ppermute | solution.py:17
  70.0 29.6 %copy-start.11 = (bf16[960,256]{1,0:T(8,128)(2,1)}, bf16[960,256]{1,0:T(8,128)(2,1)S(1)}, u32[]{:S(2)}) copy-start(bf16[960,256]{1,0:T(8,128)(2,1)S(1)} %collective-permute-done.9.refs_0_) | copy-start | bytes 1474564
  70.0 29.6 %collective-permute-start.13 = (bf16[960,256]{1,0:T(8,128)(2,1)S(1)}, bf16[960,256]{1,0:T(8,128)(2,1)S(1)}, u32[]{:S(2)}, u32[]{:S(2)}) collective-permute-start(bf16[960,256]{1,0:T(8,128)(2,1)S(1)} %collective-permute-done.5.refs_5_), channel_id=1, source_target_pairs={{0,64},{64,128},{128,192},{192,0},{1,65},{65,129},{129,193},{193,1... | collective-permute-start | bytes 1474568 | tf_op jit(solution)/shard_map/ppermute | solution.py:17
  80.6 14.3 %copy-start.13 = (bf16[960,256]{1,0:T(8,128)(2,1)}, bf16[960,256]{1,0:T(8,128)(2,1)S(1)}, u32[]{:S(2)}) copy-start(bf16[960,256]{1,0:T(8,128)(2,1)S(1)} %collective-permute-done.6.refs_6_) | copy-start | bytes 1474564
  80.6 19.1 %collective-permute-start.14 = (bf16[960,256]{1,0:T(8,128)(2,1)S(1)}, bf16[960,256]{1,0:T(8,128)(2,1)S(1)}, u32[]{:S(2)}, u32[]{:S(2)}) collective-permute-start(bf16[960,256]{1,0:T(8,128)(2,1)S(1)} %collective-permute-done.5.refs_5_), channel_id=1, source_target_pairs={{0,192},{64,0},{128,64},{192,128},{1,193},{65,1},{129,65},{193,129... | collective-permute-start | bytes 1474568 | tf_op jit(solution)/shard_map/ppermute | solution.py:17
  82.6 17.1 %copy-start.15 = (bf16[960,256]{1,0:T(8,128)(2,1)}, bf16[960,256]{1,0:T(8,128)(2,1)S(1)}, u32[]{:S(2)}) copy-start(bf16[960,256]{1,0:T(8,128)(2,1)S(1)} %collective-permute-done.15.refs_6_) | copy-start | bytes 1474564
  82.6 17.0 %collective-permute-start.16 = (bf16[960,256]{1,0:T(8,128)(2,1)S(1)}, bf16[960,256]{1,0:T(8,128)(2,1)S(1)}, u32[]{:S(2)}, u32[]{:S(2)}) collective-permute-start(bf16[960,256]{1,0:T(8,128)(2,1)S(1)} %collective-permute-done.15.refs_6_), channel_id=1, source_target_pairs={{0,32},{32,0},{1,33},{33,1},{2,34},{34,2},{3,35},{35,3},{4,36},{36... | collective-permute-start | bytes 1474568 | tf_op jit(solution)/shard_map/ppermute | solution.py:17
  85.6 3.2 %copy-start.4 = (bf16[192,80,256]{2,1,0:T(8,128)(2,1)S(1)}, bf16[192,80,256]{2,1,0:T(8,128)(2,1)}, u32[]{:S(2)}) copy-start(bf16[192,80,256]{2,1,0:T(8,128)(2,1)} %shots.1) | copy-start | bytes 23592964
  88.8 6.0 %copy-start.26 = (bf16[256,256]{1,0:T(8,128)(2,1)S(1)}, bf16[256,256]{1,0:T(8,128)(2,1)}, u32[]{:S(2)}) copy-start(bf16[256,256]{1,0:T(8,128)(2,1)} %copy-done.25) | copy-start | bytes 393220
  93.9 18.3 %copy-start.1 = (bf16[80,192,256]{2,1,0:T(8,128)(2,1)}, bf16[80,192,256]{2,1,0:T(8,128)(2,1)S(1)}, u32[]{:S(2)}) copy-start(bf16[80,192,256]{2,1,0:T(8,128)(2,1)S(1)} %rows_major.2.own) | copy-start | bytes 23592964
  99.6 4.8 %copy-start.17 = (bf16[960,256]{1,0:T(8,128)(2,1)}, bf16[960,256]{1,0:T(8,128)(2,1)S(1)}, u32[]{:S(2)}) copy-start(bf16[960,256]{1,0:T(8,128)(2,1)S(1)} %collective-permute-done.12.refs_3_) | copy-start | bytes 1474564
  99.6 4.8 %copy-start.19 = (bf16[960,256]{1,0:T(8,128)(2,1)}, bf16[960,256]{1,0:T(8,128)(2,1)S(1)}, u32[]{:S(2)}) copy-start(bf16[960,256]{1,0:T(8,128)(2,1)S(1)} %collective-permute-done.13.refs_4_) | copy-start | bytes 1474564
  112.2 7.2 %copy-start.2 = (bf16[80,192,256]{2,1,0:T(8,128)(2,1)}, bf16[80,192,256]{2,1,0:T(8,128)(2,1)S(1)}, u32[]{:S(2)}) copy-start(bf16[80,192,256]{2,1,0:T(8,128)(2,1)S(1)} %rows_major.3.beside) | copy-start | bytes 23592964
  119.4 5.5 %collective-permute-start.18 = (f32[96,384]{1,0:T(8,128)}, f32[96,384]{1,0:T(8,128)}, u32[]{:S(2)}, u32[]{:S(2)}) collective-permute-start(f32[96,384]{1,0:T(8,128)} %partial_scores.1), channel_id=1, source_target_pairs={{0,1},{1,0},{2,3},{3,2},{4,5},{5,4},{6,7},{7,6},{8,9},{9,8},{10,11... | collective-permute-start | bytes 442376 | tf_op jit(solution)/shard_map/ppermute | solution.py:17
  122.3 1.6 collective-permute-start
  122.3 22.7 %copy-start.6 = (bf16[960,256]{1,0:T(8,128)(2,1)S(1)}, bf16[960,256]{1,0:T(8,128)(2,1)}, u32[]{:S(2)}) copy-start(bf16[960,256]{1,0:T(8,128)(2,1)} %copy-done.5) | copy-start | bytes 1474564
  122.3 22.7 %copy-start.10 = (bf16[960,256]{1,0:T(8,128)(2,1)S(1)}, bf16[960,256]{1,0:T(8,128)(2,1)}, u32[]{:S(2)}) copy-start(bf16[960,256]{1,0:T(8,128)(2,1)} %copy-done.9) | copy-start | bytes 1474564
  127.1 1.9 %collective-permute-start.19 = (f32[2,384]{1,0:T(2,128)S(1)}, f32[2,384]{1,0:T(2,128)S(1)}, u32[]{:S(2)}, u32[]{:S(2)}) collective-permute-start(f32[2,384]{1,0:T(2,128)S(1)} %fusion.13), channel_id=1, source_target_pairs={{0,16},{2,18},{4,20},{6,22},{8,24},{10,26},{12,28},{14,30},{16,0},... | collective-permute-start | bytes 9224 | tf_op jit(solution)/shard_map/ppermute | solution.py:338
  127.1 3.7 %collective-permute-start.20 = (f32[2,384]{1,0:T(2,128)S(1)}, f32[2,384]{1,0:T(2,128)S(1)}, u32[]{:S(2)}, u32[]{:S(2)}) collective-permute-start(f32[2,384]{1,0:T(2,128)S(1)} %fusion.13), channel_id=1, source_target_pairs={{0,2},{2,0},{4,6},{6,4},{8,10},{10,8},{12,14},{14,12},{16,18},{18,... | collective-permute-start | bytes 9224 | tf_op jit(solution)/shard_map/ppermute | solution.py:338
  127.3 3.5 %collective-permute-start.21 = (f32[2,384]{1,0:T(2,128)S(1)}, f32[2,384]{1,0:T(2,128)S(1)}, u32[]{:S(2)}, u32[]{:S(2)}) collective-permute-start(f32[2,384]{1,0:T(2,128)S(1)} %fusion.13), channel_id=1, source_target_pairs={{0,18},{2,16},{4,22},{6,20},{8,26},{10,24},{12,30},{14,28},{16,2},... | collective-permute-start | bytes 9224 | tf_op jit(solution)/shard_map/ppermute | solution.py:338
  130.9 23.8 %collective-permute-start.22 = (f32[2,384]{1,0:T(2,128)S(1)}, f32[2,384]{1,0:T(2,128)S(1)}, u32[]{:S(2)}, u32[]{:S(2)}) collective-permute-start(f32[2,384]{1,0:T(2,128)S(1)} %pad_maximum_fusion.3), channel_id=1, source_target_pairs={{0,4},{2,6},{4,0},{6,2},{8,12},{10,14},{12,8},{14,10},{16,20},{18,... | collective-permute-start | bytes 9224 | tf_op jit(solution)/shard_map/ppermute | solution.py:338
  134.2 20.5 %collective-permute-start.23 = (f32[2,384]{1,0:T(2,128)S(1)}, f32[2,384]{1,0:T(2,128)S(1)}, u32[]{:S(2)}, u32[]{:S(2)}) collective-permute-start(f32[2,384]{1,0:T(2,128)S(1)} %pad_maximum_fusion.3), channel_id=1, source_target_pairs={{0,8},{2,10},{4,12},{6,14},{8,0},{10,2},{12,4},{14,6},{16,24},{18,... | collective-permute-start | bytes 9224 | tf_op jit(solution)/shard_map/ppermute | solution.py:338
  139.1 15.6 %collective-permute-start.24 = (f32[2,384]{1,0:T(2,128)S(1)}, f32[2,384]{1,0:T(2,128)S(1)}, u32[]{:S(2)}, u32[]{:S(2)}) collective-permute-start(f32[2,384]{1,0:T(2,128)S(1)} %pad_maximum_fusion.3), channel_id=1, source_target_pairs={{0,12},{2,14},{4,8},{6,10},{8,4},{10,6},{12,0},{14,2},{16,28},{18,... | collective-permute-start | bytes 9224 | tf_op jit(solution)/shard_map/ppermute | solution.py:338
  140.0 1.0 copy-start.8
  141.1 1.0 copy-start.14
  142.1 12.8 %slice-start = ((s8[7864320]{0:T(1024)(128)(4,1)}), s8[4194304]{0:T(1024)(128)(4,1)S(1)}, s32[]{:S(2)}) async-start(s8[7864320]{0:T(1024)(128)(4,1)} %bitcast.13), calls=%async_computation.1 | async-start | bytes 8388608
  142.1 12.8 %copy-start.3 = (bf16[80,192,256]{2,1,0:T(8,128)(2,1)S(1)}, bf16[80,192,256]{2,1,0:T(8,128)(2,1)}, u32[]{:S(2)}) copy-start(bf16[80,192,256]{2,1,0:T(8,128)(2,1)} %copy-done.2) | copy-start | bytes 23592964
  145.0 1.6 copy-start.12
  146.6 1.0 copy-start.16
  151.8 3.1 %slice-start.1 = ((s8[7864320]{0:T(1024)(128)(4,1)}), s8[3670016]{0:T(1024)(128)(4,1)S(1)}, s32[]{:S(2)}) async-start(s8[7864320]{0:T(1024)(128)(4,1)} %bitcast.13), calls=%async_computation.2 | async-start | bytes 7340032
  162.3 23.4 %all-to-all-start = ((bf16[256,2,256]{2,1,0:T(2,128)(2,1)}), bf16[256,2,256]{2,1,0:T(2,128)(2,1)S(1)}, u32[]{:S(2)}, u32[]{:S(2)}) async-start(bf16[256,2,256]{2,1,0:T(2,128)(2,1)} %reshape.58), calls=%async_computation | async-start | bytes 524288 | tf_op jit(solution)/shard_map/all_to_all | solution.py:396
  (9 other events, 7.9 us)

commit v3 on v2

--- a/solution.py
+++ b/solution.py
@@ -39,37 +39,29 @@
     )
 
 
-def placed_rows(weights, row_first, row_count, half, half_rows):
+def placed_rows(weights, row_first, row_count, start, half_rows):
     owned, reach, _ = weights.shape
     row = lax.broadcasted_iota(jnp.int32, (owned, half_rows, reach), 1)
     entry = lax.broadcasted_iota(jnp.int32, (owned, half_rows, reach), 2)
-    at = half * half_rows + row - row_first[:, :, None]
+    at = start + row - row_first[:, :, None]
     chosen = (entry == at) & (entry < row_count[:, :, None])
     return jnp.einsum("orj,ojl->orl", chosen.astype(BF16), weights, preferred_element_type=BF16)
 
 
 def weighted_kernel(*refs):
-    chips = (len(refs) - 8) // 2
+    chips = (len(refs) - 6) // 2
     chunks = refs[: 2 * chips]
-    lines, lines_far, noise, out, quad, wide, taken, done = refs[2 * chips :]
+    lines, lines_far, noise, out, quad, wide = refs[2 * chips :]
     rows = out.shape[0]
     pitch = rows + 1
     step = noise.shape[0]
     some = step // rows
     owned = chunks[0].shape[0] // rows
-    fetch = lambda chip, side: pltpu.make_async_copy(
-        chunks[side * chips + chip], taken.at[chip, side], done.at[chip, side]
-    )
     for chip in range(chips):
-        for side in range(2):
-            fetch(chip, side).start()
-    for chip in range(chips):
-        for side in range(2):
-            fetch(chip, side).wait()
         for i in range(owned // some):
             at = slice(i * step, (i + 1) * step)
-            slices = jnp.dot(taken[chip, 0, at, :], lines[...], preferred_element_type=F32)
-            slices += jnp.dot(taken[chip, 1, at, :], lines_far[...], preferred_element_type=F32)
+            slices = jnp.dot(chunks[chip][at, :], lines[...], preferred_element_type=F32)
+            slices += jnp.dot(chunks[chips + chip][at, :], lines_far[...], preferred_element_type=F32)
             slices = slices.astype(BF16).astype(F32)
             weighted = noise[...] * slices
             first = chip * owned + i * some
@@ -96,21 +88,16 @@
     chips = len(near)
     count = chips * near[0].shape[0] // rows
     width = lines.shape[1]
-    there = pl.BlockSpec(memory_space=pl.ANY)
-    here = pl.BlockSpec(memory_space=pltpu.VMEM)
     return pl.pallas_call(
         weighted_kernel,
-        in_specs=[there] * (2 * chips) + [here] * 3,
         out_shape=(
             jax.ShapeDtypeStruct((rows, count, width), BF16),
             jax.ShapeDtypeStruct((count, 8, 128), F32),
         ),
         scratch_shapes=[
             pltpu.VMEM((2, count * (rows + 1), 128), F32),
-            pltpu.VMEM((chips, 2, *near[0].shape), BF16),
-            pltpu.SemaphoreType.DMA((chips, 2)),
         ],
-        compiler_params=pltpu.CompilerParams(vmem_limit_bytes=16 << 20),
+        compiler_params=pltpu.CompilerParams(vmem_limit_bytes=10 << 20),
         name="weighted_slices",
     )(*near, *far, lines, lines_far, noise)
 
@@ -150,17 +137,20 @@
         scratch_shapes=[pltpu.VMEM((2, 2 * count, shots), F32)],
         compiler_params=pltpu.CompilerParams(vmem_limit_bytes=4 << 20),
         name="partial_scores",
-    )(first, second, quad_first, quad_second, own, beside)
-
-
-def rows_major_kernel(shots, out, taken, given, wide, came, went):
+    )(first, second, quad_first, quad_second, held(own), held(beside))
+
+
+def held(x, space=pltpu.VMEM):
+    return pltpu.with_memory_space_constraint(x, space)
+
+
+def rows_major_kernel(shots, out, taken, wide, came):
     total, rows, _ = shots.shape
     block = taken.shape[1]
     pitch = rows + 1
     steps = total // block
     span = lambda i: slice(i * block, (i + 1) * block)
     fetch = lambda i: pltpu.make_async_copy(shots.at[span(i)], taken.at[i % 2], came.at[i % 2])
-    give = lambda i: pltpu.make_async_copy(given.at[i % 2], out.at[:, span(i), :], went.at[i % 2])
     fetch(0).start()
     for i in range(steps):
         if i + 1 < steps:
@@ -176,20 +166,15 @@
             return carry
 
         lax.fori_loop(0, block // 8, spread, 0)
-        if i >= 2:
-            give(i - 2).wait()
 
         def turn(r, carry, i=i):
             for half in range(2):
-                given[i % 2, r, :, half * 128 : half * 128 + 128] = wide[
+                out[r, span(i), half * 128 : half * 128 + 128] = wide[
                     half, pl.ds(r, block, stride=pitch), :
                 ].astype(BF16)
             return carry
 
         lax.fori_loop(0, rows, turn, 0, unroll=8)
-        give(i).start()
-    for i in range(max(steps - 2, 0), steps):
-        give(i).wait()
 
 
 def rows_major(images, block=48):
@@ -197,16 +182,14 @@
     return pl.pallas_call(
         rows_major_kernel,
         in_specs=[pl.BlockSpec(memory_space=pl.ANY)],
-        out_specs=pl.BlockSpec(memory_space=pltpu.HBM),
-        out_shape=jax.ShapeDtypeStruct((rows, shots, width), BF16),
+        out_specs=pl.BlockSpec(memory_space=pltpu.VMEM),
+        out_shape=pltpu.VMEM((rows, shots, width), BF16),
         scratch_shapes=[
             pltpu.VMEM((2, block, rows, width), BF16),
-            pltpu.VMEM((2, rows, block, width), BF16),
             pltpu.VMEM((2, block * (rows + 1), 128), F32),
             pltpu.SemaphoreType.DMA((2,)),
-            pltpu.SemaphoreType.DMA((2,)),
         ],
-        compiler_params=pltpu.CompilerParams(vmem_limit_bytes=14 << 20),
+        compiler_params=pltpu.CompilerParams(vmem_limit_bytes=9 << 20),
         name="rows_major",
     )(images)
 
@@ -243,40 +226,35 @@
 
 def turn_kernel(*refs):
     chunks, out, flat = refs[:-2], refs[-2], refs[-1]
-    half = len(chunks) // 2
+    size = chunks[0].shape[0]
+    for i, chunk in enumerate(chunks):
+        flat[i * size : (i + 1) * size, :] = chunk[...]
+
+    def turn(i, carry):
+        at = pl.multiple_of(i * 128, 128)
+        out[:, pl.ds(at, 128)] = flat[pl.ds(at, 128), :].T
+        return carry
+
+    lax.fori_loop(0, len(chunks) * size // 128, turn, 0, unroll=2)
+
+
+def turned_weights(chunks):
     size, lines = chunks[0].shape
-    for side in range(2):
-        for i in range(half):
-            flat[side, i * size : (i + 1) * size, :] = chunks[side * half + i][...]
-    for side in range(2):
-
-        def turn(i, carry, side=side):
-            at = pl.multiple_of(i * 128, 128)
-            out[side * lines : (side + 1) * lines, pl.ds(at, 128)] = flat[side, pl.ds(at, 128), :].T
-            return carry
-
-        lax.fori_loop(0, half * size // 128, turn, 0, unroll=2)
-
-
-def turned_weights(near, far):
-    size, lines = near[0].shape
-    span = len(near) * size
+    span = len(chunks) * size
     return pl.pallas_call(
         turn_kernel,
-        out_shape=jax.ShapeDtypeStruct((2 * lines, span), BF16),
-        scratch_shapes=[pltpu.VMEM((2, span, lines), BF16)],
-        compiler_params=pltpu.CompilerParams(vmem_limit_bytes=13 << 20),
+        out_shape=pltpu.VMEM((lines, span), BF16),
+        scratch_shapes=[pltpu.VMEM((span, lines), BF16)],
+        compiler_params=pltpu.CompilerParams(vmem_limit_bytes=5 << 20),
         name="turned_weights",
-    )(*near, *far)
-
-
-def insert_kernel(
-    slab, scores, allowed, stats, own, beside, turned, turned_too, out, post_own, post_beside, wide, flat
-):
+    )(*chunks)
+
+
+def insert_kernel(my_core, scores, allowed, stats, own, beside, *refs):
+    turned, (out, post_own, post_beside, wide, flat) = refs[:4], refs[4:]
     rows, shots, _ = own.shape
     pitch = rows + 1
     count = scores.shape[0]
-    lines = out.shape[1]
     block = 8
     mass = jnp.exp(scores[...] - stats[0:1, :])
     post = jnp.where(allowed[...] > 0.5, mass, 0.0) / stats[1:2, :]
@@ -307,22 +285,25 @@
 
     lax.fori_loop(0, count // 8, narrow, 0)
     split = count * rows // 2
-    for side, slot in ((0, slab[0]), (1, 1 - slab[0])):
-        part = slice(side * lines, (side + 1) * lines)
-        total = jnp.dot(turned[part, :], flat[:split, :], preferred_element_type=F32)
-        total += jnp.dot(turned_too[part, :], flat[split:, :], preferred_element_type=F32)
-        out[slot] = total.astype(BF16)
-
-
-def insertion(slab, scores, allowed, stats, own, beside, turned, turned_too):
+    for side in range(2):
+        total = jnp.dot(turned[side][...], flat[:split, :], preferred_element_type=F32)
+        total += jnp.dot(turned[2 + side][...], flat[split:, :], preferred_element_type=F32)
+        lines, width = total.shape
+        parts = total.reshape(8, 2, lines // 16, width)
+        for other in range(2):
+            mine = jnp.where(my_core[0] == other, parts[:, 0], parts[:, 1])
+            out[2 * other + side] = mine.reshape(lines // 2, width).astype(BF16)
+
+
+def insertion(my_core, scores, allowed, stats, own, beside, turned):
     rows, shots, width = own.shape
     count = scores.shape[0]
-    lines = turned.shape[0] // 2
+    lines = turned[0].shape[0]
     return pl.pallas_call(
         insert_kernel,
         in_specs=[pl.BlockSpec(memory_space=pltpu.SMEM)]
-        + [pl.BlockSpec(memory_space=pltpu.VMEM)] * 7,
-        out_shape=jax.ShapeDtypeStruct((2, lines, width), BF16),
+        + [pl.BlockSpec(memory_space=pltpu.VMEM)] * 9,
+        out_shape=jax.ShapeDtypeStruct((4, lines // 2, width), BF16),
         scratch_shapes=[
             pltpu.VMEM((count, shots), BF16),
             pltpu.VMEM((count, shots), BF16),
@@ -331,7 +312,7 @@
         ],
         compiler_params=pltpu.CompilerParams(vmem_limit_bytes=14 << 20),
         name="insertion",
-    )(slab, scores, allowed, stats, own, beside, turned, turned_too)
+    )(my_core.reshape(1), scores, allowed, stats, held(own), held(beside), *map(held, turned))
 
 
 def crossed(x, axes, mask):
@@ -344,9 +325,9 @@
     return jnp.stack([highest, total])
 
 
-def in_core_order(stats, core, shots):
+def in_core_order(stats, first_core, shots):
     swapped = jnp.concatenate([stats[:, shots:], stats[:, :shots]], axis=1)
-    return jnp.where(core == 0, stats, swapped)
+    return jnp.where(first_core, stats, swapped)
 
 
 def step(images, noise_weight, prior_mask, volume, interp_weights, row_first, row_count):
@@ -354,21 +335,30 @@
     shots, half_rows, width = images.shape
     slab = lax.axis_index("slab")
     core = lax.axis_index("core")
-    lines = volume.reshape(line_span, width)
-
-    near = placed_rows(interp_weights, row_first, row_count, slab, half_rows)
-    far = placed_rows(interp_weights, row_first, row_count, 1 - slab, half_rows)
+    interp_weights, lines, near_at, far_at, my_y, my_x, core, first_core = lax.optimization_barrier(
+        (
+            interp_weights,
+            volume.reshape(line_span, width),
+            slab * half_rows,
+            (1 - slab) * half_rows,
+            lax.axis_index("y"),
+            lax.axis_index("xh"),
+            core,
+            core == 0,
+        )
+    )
+
+    near = placed_rows(interp_weights, row_first, row_count, near_at, half_rows)
+    far = placed_rows(interp_weights, row_first, row_count, far_at, half_rows)
     flat = lambda x: x.reshape(owned * half_rows, line_span)
     near, far = gathered(flat(near), flat(far))
     lines_far = shifted(lines, "slab", 1)
 
     beside = shifted(images, "core", 1)
-    own = rows_major(images)
+    own = rows_major(held(images, pltpu.HBM))
     beside = rows_major(beside)
 
-    kept, sent = mask_choice(
-        lax.axis_index("y"), lax.axis_index("xh"), core, prior_mask, len(SOURCES) * owned
-    )
+    kept, sent = mask_choice(my_y, my_x, core, prior_mask, len(SOURCES) * owned)
     allowed = jnp.concatenate([kept, shifted(sent, "core", 1)], axis=1).astype(F32)
 
     noise_both = jnp.concatenate([noise_weight, noise_weight], axis=1)
@@ -379,21 +369,28 @@
     first, quad_first = weigh(slice(0, 4))
     second, quad_second = weigh(slice(4, 8))
     part = partial_scores(first, second, quad_first, quad_second, own, beside)
-    turned = turned_weights(near[:4], far[:4])
-    turned_too = turned_weights(near[4:], far[4:])
+    turned = [
+        turned_weights(near[:4]),
+        turned_weights(far[:4]),
+        turned_weights(near[4:]),
+        turned_weights(far[4:]),
+    ]
     scores = part + shifted(part, "slab", 1)
 
     top = jnp.max(jnp.where(allowed > 0.5, scores, -1e30), axis=0)
     mass = jnp.sum(jnp.where(allowed > 0.5, jnp.exp(scores - top[None]), 0.0), axis=0)
-    pair = in_core_order(jnp.stack([top, mass]), core, shots)
+    pair = in_core_order(jnp.stack([top, mass]), first_core, shots)
     for masks in ((8, 1, 9), (2, 4, 6)):
         pair = combined([pair] + [crossed(pair, ("core", "ori"), m) for m in masks])
-    pair = in_core_order(pair, core, shots)
+    pair = in_core_order(pair, first_core, shots)
     log_evidence = (pair[0] + jnp.log(pair[1]))[:shots]
 
-    into = insertion(slab.reshape(1), scores, allowed, pair, own, beside, turned, turned_too)
-    into = into.reshape(-1, volume.shape[1], width)
-    arrived = lax.all_to_all(into, ("slab",) + IMG + ("ori",), 0, 0, tiled=True)
+    into = insertion(core, scores, allowed, pair, own, beside, turned)
+    square = into[0].astype(F32)
+    for m in range(1, 4):
+        square += crossed(into[m], ("core", "slab"), m).astype(F32)
+    square = square.astype(BF16).reshape(-1, volume.shape[1], width)
+    arrived = lax.all_to_all(square, ("y", "xh", "ori"), 0, 0, tiled=True)
     inserted = jnp.sum(arrived.astype(F32), axis=0, keepdims=True)
     return log_evidence, inserted
 

time: 190 us -> 167 us (0.88); the launches traced: 187 us -> 166 us
  local copies, waits for them, and re-layouts: 18.6 us -> 1.74 us
  Pallas kernels: 41 us -> 32.9 us
  starting transfers between devices: 49.8 us -> 54.6 us
  other arithmetic: 5.7 us -> 1.95 us
  waiting for transfers between devices: 68.4 us -> 71.5 us
    unnamed x62 -> x6, local copies, waits for them, and re-layouts: 16.8 us -> 0.02 us
    pallas_call x4 -> x6, Pallas kernels: 15.2 us -> 9.07 us  [the longest x4 5.78 us: turned_weights(): pl.pallas_call(turn_kernel, out_shape=pltpu.VMEM((lines, span), BF16), sc...]
    ppermute x19, waiting for transfers between devices: 52.4 us -> 55.9 us  [shifted(): return lax.ppermute(x, axis, [(i, (i + step) % n) for i in range(n)])]
    all_to_all x1, waiting for transfers between devices: 14.2 us -> 10.7 us  [step(): arrived = lax.all_to_all(square, ('y', 'xh', 'ori'), 0, 0, tiled=True)]
    ppermute x6 -> x9, waiting for transfers between devices: 1.84 us -> 4.89 us  [crossed(): lax.ppermute(x, axes, [(i, i ^ mask) for i in range(lax.axis_size(axes))])]
    ppermute x6 -> x9, starting transfers between devices: 10.2 us -> 12.4 us  [crossed(): lax.ppermute(x, axes, [(i, i ^ mask) for i in range(lax.axis_size(axes))])]
  transfers between devices with their start and end apart: 26 -> 29, of which waited for: 10 -> 13; matrix products, arithmetic and copies ran while one was open for 3% -> 2% of each run, Pallas kernels for 11% -> 9%
where the time goes in v3:
time: 167 us; the launch traced here: 166 us
  waiting for transfers between devices  71.5 us (43%)
  starting transfers between devices  54.6 us (33%)
  Pallas kernels  32.9 us (20%)
  matrix products  2.02 us (1%)
  other arithmetic  1.95 us (1%)
  local copies, waits for them, and re-layouts  1.74 us (1%)
    ppermute x19, waiting for transfers between devices, shifted(): return lax.ppermute(x, axis, [(i, (i + step) % n) for i in range(n)])  55.9 us
    ppermute x19, starting transfers between devices, shifted(): return lax.ppermute(x, axis, [(i, (i + step) % n) for i in range(n)])  32 us
    ppermute x9, starting transfers between devices, crossed(): lax.ppermute(x, axes, [(i, i ^ mask) for i in range(lax.axis_size(axes))])  12.4 us
    all_to_all x1, waiting for transfers between devices, step(): arrived = lax.all_to_all(square, ('y', 'xh', 'ori'), 0, 0, tiled=True)  10.7 us
    pallas_call x2, Pallas kernels, rows_major(): pl.pallas_call(rows_major_kernel, in_specs=[pl.BlockSpec(memory_space=pl....  10.4 us
    all_to_all x1, starting transfers between devices, step(): arrived = lax.all_to_all(square, ('y', 'xh', 'ori'), 0, 0, tiled=True)  10.2 us
    pallas_call x1, Pallas kernels, insertion(): pl.pallas_call(insert_kernel, in_specs=[pl.BlockSpec(memory_space=pltpu.S...  6.69 us
    pallas_call x1, Pallas kernels, partial_scores(): pl.pallas_call(score_kernel, out_shape=jax.ShapeDtypeStruct((2 * count, 2...  6.64 us
  transfers between devices with their start and end apart: 29, of which 13 were waited for; matrix products, arithmetic and copies ran while one was open for 2% of the time, Pallas kernels for 9%

profile of v3, /device:TPU:32, one launch (start us, length us, event | category | flops | bytes accessed | tf_op | source)
XLA Modules:
  0.0 165.7 jit_solution(17852671870237754637)
XLA Ops:
  0.8 1.0 reshape.51.refs_8_
  1.8 1.0 fusion.4
  2.8 1.6 collective-permute-start.4
  4.4 1.0 fusion.2
  5.4 1.7 collective-permute-start.2
  7.1 2.7 %collective-permute-start.1 = (bf16[960,256]{1,0:T(8,128)(2,1)S(1)}, bf16[960,256]{1,0:T(8,128)(2,1)S(1)}, u32[]{:S(2)}, u32[]{:S(2)}) collective-permute-start(bf16[960,256]{1,0:T(8,128)(2,1)S(1)} %bitcast.24), channel_id=1, source_target_pairs={{0,32},{32,0},{1,33},{33,1},{2,34},{34,2},{3,35},{35,3},{4,36},{36... | collective-permute-start | bytes 1474568 | tf_op jit(solution)/shard_map/ppermute | solution.py:17
  10.0 19.8 %collective-permute-done.8.refs_9_ = bf16[256,256]{1,0:T(8,128)(2,1)S(1)} collective-permute-done((bf16[256,256]{1,0:T(8,128)(2,1)S(1)}, bf16[256,256]{1,0:T(8,128)(2,1)S(1)}, u32[]{:S(2)}, u32[]{:S(2)}) %collective-permute-start.8) | collective-permute-done | bytes 131104 | tf_op jit(solution)/shard_map/ppermute | solution.py:17
  29.8 3.0 %collective-permute-start.3 = (bf16[960,256]{1,0:T(8,128)(2,1)S(1)}, bf16[960,256]{1,0:T(8,128)(2,1)S(1)}, u32[]{:S(2)}, u32[]{:S(2)}) collective-permute-start(bf16[960,256]{1,0:T(8,128)(2,1)S(1)} %bitcast.25), channel_id=1, source_target_pairs={{0,192},{64,0},{128,64},{192,128},{1,193},{65,1},{129,65},{193,129... | collective-permute-start | bytes 1474568 | tf_op jit(solution)/shard_map/ppermute | solution.py:17
  32.8 0.7 collective-permute-start.7
  33.6 1.3 collective-permute-start.11
  34.9 3.0 %collective-permute-start.5 = (bf16[960,256]{1,0:T(8,128)(2,1)S(1)}, bf16[960,256]{1,0:T(8,128)(2,1)S(1)}, u32[]{:S(2)}, u32[]{:S(2)}) collective-permute-start(bf16[960,256]{1,0:T(8,128)(2,1)S(1)} %collective-permute-done.4.refs_4_.refs_0_), channel_id=1, source_target_pairs={{0,32},{32,0},{1,33},{33,1},{2,34},{34,2},{3,35},{35,3},{4,36},{36... | collective-permute-start | bytes 1474568 | tf_op jit(solution)/shard_map/ppermute | solution.py:17
  37.9 6.6 %collective-permute-done.3.refs_3_ = bf16[960,256]{1,0:T(8,128)(2,1)S(1)} collective-permute-done((bf16[960,256]{1,0:T(8,128)(2,1)S(1)}, bf16[960,256]{1,0:T(8,128)(2,1)S(1)}, u32[]{:S(2)}, u32[]{:S(2)}) %collective-permute-start.3) | collective-permute-done | bytes 491552 | tf_op jit(solution)/shard_map/ppermute | solution.py:17
  44.4 3.7 %collective-permute-start.10 = (bf16[960,256]{1,0:T(8,128)(2,1)S(1)}, bf16[960,256]{1,0:T(8,128)(2,1)S(1)}, u32[]{:S(2)}, u32[]{:S(2)}) collective-permute-start(bf16[960,256]{1,0:T(8,128)(2,1)S(1)} %collective-permute-done.1.refs_1_), channel_id=1, source_target_pairs={{0,192},{64,0},{128,64},{192,128},{1,193},{65,1},{129,65},{193,129... | collective-permute-start | bytes 1474568 | tf_op jit(solution)/shard_map/ppermute | solution.py:17
  48.1 6.8 %collective-permute-done.7.refs_7_.refs_3_ = bf16[960,256]{1,0:T(8,128)(2,1)S(1)} collective-permute-done((bf16[960,256]{1,0:T(8,128)(2,1)S(1)}, bf16[960,256]{1,0:T(8,128)(2,1)S(1)}, u32[]{:S(2)}, u32[]{:S(2)}) %collective-permute-start.7) | collective-permute-done | bytes 491552 | tf_op jit(solution)/shard_map/ppermute | solution.py:17
  55.0 1.0 collective-permute-start.9
  56.0 1.6 collective-permute-start.6
  57.6 1.7 collective-permute-start.15
  59.2 6.2 %collective-permute-done.10.refs_1_ = bf16[960,256]{1,0:T(8,128)(2,1)S(1)} collective-permute-done((bf16[960,256]{1,0:T(8,128)(2,1)S(1)}, bf16[960,256]{1,0:T(8,128)(2,1)S(1)}, u32[]{:S(2)}, u32[]{:S(2)}) %collective-permute-start.10) | collective-permute-done | bytes 491552 | tf_op jit(solution)/shard_map/ppermute | solution.py:17
  65.5 3.0 %collective-permute-start.12 = (bf16[960,256]{1,0:T(8,128)(2,1)S(1)}, bf16[960,256]{1,0:T(8,128)(2,1)S(1)}, u32[]{:S(2)}, u32[]{:S(2)}) collective-permute-start(bf16[960,256]{1,0:T(8,128)(2,1)S(1)} %collective-permute-done.11.refs_2_), channel_id=1, source_target_pairs={{0,32},{32,0},{1,33},{33,1},{2,34},{34,2},{3,35},{35,3},{4,36},{36... | collective-permute-start | bytes 1474568 | tf_op jit(solution)/shard_map/ppermute | solution.py:17
  68.5 2.2 %collective-permute-done.9.refs_0_ = bf16[960,256]{1,0:T(8,128)(2,1)S(1)} collective-permute-done((bf16[960,256]{1,0:T(8,128)(2,1)S(1)}, bf16[960,256]{1,0:T(8,128)(2,1)S(1)}, u32[]{:S(2)}, u32[]{:S(2)}) %collective-permute-start.9) | collective-permute-done | bytes 491552 | tf_op jit(solution)/shard_map/ppermute | solution.py:17
  70.7 10.5 %collective-permute-done.6.refs_6_.refs_2_ = bf16[960,256]{1,0:T(8,128)(2,1)S(1)} collective-permute-done((bf16[960,256]{1,0:T(8,128)(2,1)S(1)}, bf16[960,256]{1,0:T(8,128)(2,1)S(1)}, u32[]{:S(2)}, u32[]{:S(2)}) %collective-permute-start.6) | collective-permute-done | bytes 491552 | tf_op jit(solution)/shard_map/ppermute | solution.py:17
  81.3 2.0 %collective-permute-start.14 = (bf16[960,256]{1,0:T(8,128)(2,1)S(1)}, bf16[960,256]{1,0:T(8,128)(2,1)S(1)}, u32[]{:S(2)}, u32[]{:S(2)}) collective-permute-start(bf16[960,256]{1,0:T(8,128)(2,1)S(1)} %collective-permute-done.5.refs_5_.refs_1_), channel_id=1, source_target_pairs={{0,192},{64,0},{128,64},{192,128},{1,193},{65,1},{129,65},{193,129... | collective-permute-start | bytes 1474568 | tf_op jit(solution)/shard_map/ppermute | solution.py:17
  83.3 3.0 %collective-permute-start.16 = (bf16[960,256]{1,0:T(8,128)(2,1)S(1)}, bf16[960,256]{1,0:T(8,128)(2,1)S(1)}, u32[]{:S(2)}, u32[]{:S(2)}) collective-permute-start(bf16[960,256]{1,0:T(8,128)(2,1)S(1)} %collective-permute-done.15.refs_6_.refs_2_), channel_id=1, source_target_pairs={{0,32},{32,0},{1,33},{33,1},{2,34},{34,2},{3,35},{35,3},{4,36},{36... | collective-permute-start | bytes 1474568 | tf_op jit(solution)/shard_map/ppermute | solution.py:17
  86.3 5.2 %rows_major.2.own = bf16[80,192,256]{2,1,0:T(8,128)(2,1)S(1)} custom-call(bf16[192,80,256]{2,1,0:T(8,128)(2,1)} %shots.1), custom_call_target="tpu_custom_call" | custom-call | tf_op jit(solution)/shard_map/rows_major/pallas_call | solution.py:182
  91.5 1.7 %weighted_slices.2 = (bf16[80,48,256]{2,1,0:T(8,128)(2,1)S(1)}, f32[48,8,128]{2,1,0:T(8,128)S(1)}) custom-call(bf16[960,256]{1,0:T(8,128)(2,1)S(1)} %bitcast.26, bf16[960,256]{1,0:T(8,128)(2,1)S(1)} %collective-permute-done.1.refs_1_, bf16[960,256]{1,0:T(8,128)(2,1)S(1)} %collective-permute-done.2.refs_2_, ...), custom_call_target="tpu_custom_call" | custom-call | tf_op jit(solution)/shard_map/weighted_slices/pallas_call | solution.py:91
  93.6 1.6 weighted_slices.3
  95.3 5.2 %rows_major.3.beside = bf16[80,192,256]{2,1,0:T(8,128)(2,1)S(1)} custom-call(bf16[192,80,256]{2,1,0:T(8,128)(2,1)} %collective-permute-done.17.shots), custom_call_target="tpu_custom_call" | custom-call | tf_op jit(solution)/shard_map/rows_major/pallas_call | solution.py:182
  100.5 6.6 %partial_scores.1 = f32[96,384]{1,0:T(8,128)S(1)} custom-call(bf16[80,48,256]{2,1,0:T(8,128)(2,1)S(1)} %get-tuple-element.26.first, bf16[80,48,256]{2,1,0:T(8,128)(2,1)S(1)} %get-tuple-element.27.second, f32[48,8,128]{2,1,0:T(8,128)S(1)} %get-tuple-element.28.quad_first, f32[48,8,128]{2,1,0:T(8,128)S(1)} %get-tuple-element.29.quad_second, ...), custom_call_target="tpu_custom_call" | custom-call | tf_op jit(solution)/shard_map/partial_scores/pallas_call | solution.py:134
  107.1 1.5 collective-permute-start.18
  109.0 1.2 collective-permute-done
  110.2 2.1 %collective-permute-done.18 = f32[96,384]{1,0:T(8,128)S(1)} collective-permute-done((f32[96,384]{1,0:T(8,128)S(1)}, f32[96,384]{1,0:T(8,128)S(1)}, u32[]{:S(2)}, u32[]{:S(2)}) %collective-permute-start.18) | collective-permute-done | bytes 147488 | tf_op jit(solution)/shard_map/ppermute | solution.py:17
  112.9 1.7 %collective-permute-start.21 = (f32[2,384]{1,0:T(2,128)S(1)}, f32[2,384]{1,0:T(2,128)S(1)}, u32[]{:S(2)}, u32[]{:S(2)}) collective-permute-start(f32[2,384]{1,0:T(2,128)S(1)} %fusion.16), channel_id=1, source_target_pairs={{0,18},{2,16},{4,22},{6,20},{8,26},{10,24},{12,30},{14,28},{16,2},... | collective-permute-start | bytes 9224 | tf_op jit(solution)/shard_map/ppermute | solution.py:319
  114.6 1.8 %collective-permute-done.20 = f32[2,384]{1,0:T(2,128)S(1)} collective-permute-done((f32[2,384]{1,0:T(2,128)S(1)}, f32[2,384]{1,0:T(2,128)S(1)}, u32[]{:S(2)}, u32[]{:S(2)}) %collective-permute-start.20) | collective-permute-done | bytes 3104 | tf_op jit(solution)/shard_map/ppermute | solution.py:319
  116.5 3.3 %collective-permute-start.22 = (f32[2,384]{1,0:T(2,128)S(1)}, f32[2,384]{1,0:T(2,128)S(1)}, u32[]{:S(2)}, u32[]{:S(2)}) collective-permute-start(f32[2,384]{1,0:T(2,128)S(1)} %pad_maximum_fusion.3), channel_id=1, source_target_pairs={{0,4},{2,6},{4,0},{6,2},{8,12},{10,14},{12,8},{14,10},{16,20},{18,... | collective-permute-start | bytes 9224 | tf_op jit(solution)/shard_map/ppermute | solution.py:319
  119.8 4.9 %collective-permute-start.23 = (f32[2,384]{1,0:T(2,128)S(1)}, f32[2,384]{1,0:T(2,128)S(1)}, u32[]{:S(2)}, u32[]{:S(2)}) collective-permute-start(f32[2,384]{1,0:T(2,128)S(1)} %pad_maximum_fusion.3), channel_id=1, source_target_pairs={{0,8},{2,10},{4,12},{6,14},{8,0},{10,2},{12,4},{14,6},{16,24},{18,... | collective-permute-start | bytes 9224 | tf_op jit(solution)/shard_map/ppermute | solution.py:319
  124.8 1.4 turned_weights.4.refs_0_
  126.3 1.4 turned_weights.5.refs_1_
  127.7 1.4 turned_weights.6.refs_2_
  129.2 1.4 turned_weights.7.refs_3_
  130.9 6.7 %insertion.1 = bf16[4,128,256]{2,1,0:T(8,128)(2,1)S(1)} custom-call(s32[1]{0:T(128)} %bitcast.2.my_core, f32[96,384]{1,0:T(8,128)S(1)} %get-tuple-element.35.scores, f32[96,384]{1,0:T(8,128)S(1)} %maximum_convert_fusion.allowed, f32[2,384]{1,0:T(2,128)S(1)} %fusion.15.stats, bf16[80,192,256]{2,1,0:T(8,128)(2,1)S(1)} %rows_major.2.own, ...), custom_call_target="tpu_custom_call" | custom-call | tf_op jit(solution)/shard_map/insertion/pallas_call | solution.py:302
  137.6 1.6 collective-permute-start.25
  139.2 0.6 collective-permute-start.27
  139.8 2.1 %collective-permute-done.25 = bf16[128,256]{1,0:T(8,128)(2,1)S(1)} collective-permute-done((bf16[128,256]{1,0:T(8,128)(2,1)S(1)}, bf16[128,256]{1,0:T(8,128)(2,1)S(1)}, u32[]{:S(2)}, u32[]{:S(2)}) %collective-permute-start.25) | collective-permute-done | bytes 65568 | tf_op jit(solution)/shard_map/ppermute | solution.py:319
  141.9 0.9 collective-permute-done.27
  142.9 0.7 reshape.57
  143.6 10.2 %all-to-all-start = ((bf16[64,2,256]{2,1,0:T(2,128)(2,1)}), bf16[64,2,256]{2,1,0:T(2,128)(2,1)S(1)}, u32[]{:S(2)}, u32[]{:S(2)}) async-start(bf16[64,2,256]{2,1,0:T(2,128)(2,1)} %reshape.57), calls=%async_computation | async-start | bytes 131072 | tf_op jit(solution)/shard_map/all_to_all | solution.py:393
  154.3 10.7 %all-to-all-done = bf16[64,2,256]{2,1,0:T(2,128)(2,1)S(1)} async-done(((bf16[64,2,256]{2,1,0:T(2,128)(2,1)}), bf16[64,2,256]{2,1,0:T(2,128)(2,1)S(1)}, u32[]{:S(2)}, u32[]{:S(2)}) %all-to-all-start) | async-done | bytes 65568 | tf_op jit(solution)/shard_map/all_to_all | solution.py:393
  165.0 0.7 convert_reduce_fusion
  (52 shorter events, 2.6 us)
Async XLA Ops:
  0.6 1.2 copy-start
  0.6 94.6 %collective-permute-start.17 = (bf16[192,80,256]{2,1,0:T(8,128)(2,1)}, bf16[192,80,256]{2,1,0:T(8,128)(2,1)}, u32[]{:S(2)}, u32[]{:S(2)}) collective-permute-start(bf16[192,80,256]{2,1,0:T(8,128)(2,1)} %shots.1), channel_id=1, source_target_pairs={{0,16},{16,0},{1,17},{17,1},{2,18},{18,2},{3,19},{19,3},{4,20},{20... | collective-permute-start | bytes 23592968 | tf_op jit(solution)/shard_map/ppermute | solution.py:17
  2.8 30.0 %collective-permute-start.4 = (bf16[960,256]{1,0:T(8,128)(2,1)S(1)}, bf16[960,256]{1,0:T(8,128)(2,1)S(1)}, u32[]{:S(2)}, u32[]{:S(2)}) collective-permute-start(bf16[960,256]{1,0:T(8,128)(2,1)S(1)} %bitcast.30), channel_id=1, source_target_pairs={{0,1},{1,0},{2,3},{3,2},{4,5},{5,4},{6,7},{7,6},{8,9},{9,8},{10,11... | collective-permute-start | bytes 1474568 | tf_op jit(solution)/shard_map/ppermute | solution.py:17
  5.4 86.1 %copy-start.2 = (f32[80,128]{1,0:T(8,128)S(1)}, f32[80,128]{1,0:T(8,128)}, u32[]{:S(2)}) copy-start(f32[80,128]{1,0:T(8,128)} %param.8) | copy-start | bytes 122884
  5.4 28.1 %collective-permute-start.2 = (bf16[960,256]{1,0:T(8,128)(2,1)S(1)}, bf16[960,256]{1,0:T(8,128)(2,1)S(1)}, u32[]{:S(2)}, u32[]{:S(2)}) collective-permute-start(bf16[960,256]{1,0:T(8,128)(2,1)S(1)} %bitcast.23), channel_id=1, source_target_pairs={{0,64},{64,128},{128,192},{192,0},{1,65},{65,129},{129,193},{193,1... | collective-permute-start | bytes 1474568 | tf_op jit(solution)/shard_map/ppermute | solution.py:17
  7.1 27.8 %collective-permute-start.1 = (bf16[960,256]{1,0:T(8,128)(2,1)S(1)}, bf16[960,256]{1,0:T(8,128)(2,1)S(1)}, u32[]{:S(2)}, u32[]{:S(2)}) collective-permute-start(bf16[960,256]{1,0:T(8,128)(2,1)S(1)} %bitcast.24), channel_id=1, source_target_pairs={{0,32},{32,0},{1,33},{33,1},{2,34},{34,2},{3,35},{35,3},{4,36},{36... | collective-permute-start | bytes 1474568 | tf_op jit(solution)/shard_map/ppermute | solution.py:17
  9.8 20.0 %collective-permute-start.8 = (bf16[256,256]{1,0:T(8,128)(2,1)S(1)}, bf16[256,256]{1,0:T(8,128)(2,1)S(1)}, u32[]{:S(2)}, u32[]{:S(2)}) collective-permute-start(bf16[256,256]{1,0:T(8,128)(2,1)S(1)} %reshape.51.refs_8_), channel_id=1, source_target_pairs={{0,1},{1,0},{2,3},{3,2},{4,5},{5,4},{6,7},{7,6},{8,9},{9,8},{10,11... | collective-permute-start | bytes 393224 | tf_op jit(solution)/shard_map/ppermute | solution.py:17
  29.8 14.6 %collective-permute-start.3 = (bf16[960,256]{1,0:T(8,128)(2,1)S(1)}, bf16[960,256]{1,0:T(8,128)(2,1)S(1)}, u32[]{:S(2)}, u32[]{:S(2)}) collective-permute-start(bf16[960,256]{1,0:T(8,128)(2,1)S(1)} %bitcast.25), channel_id=1, source_target_pairs={{0,192},{64,0},{128,64},{192,128},{1,193},{65,1},{129,65},{193,129... | collective-permute-start | bytes 1474568 | tf_op jit(solution)/shard_map/ppermute | solution.py:17
  32.8 22.1 %collective-permute-start.7 = (bf16[960,256]{1,0:T(8,128)(2,1)S(1)}, bf16[960,256]{1,0:T(8,128)(2,1)S(1)}, u32[]{:S(2)}, u32[]{:S(2)}) collective-permute-start(bf16[960,256]{1,0:T(8,128)(2,1)S(1)} %collective-permute-done.4.refs_4_.refs_0_), channel_id=1, source_target_pairs={{0,192},{64,0},{128,64},{192,128},{1,193},{65,1},{129,65},{193,129... | collective-permute-start | bytes 1474568 | tf_op jit(solution)/shard_map/ppermute | solution.py:17
  33.6 22.4 %collective-permute-start.11 = (bf16[960,256]{1,0:T(8,128)(2,1)S(1)}, bf16[960,256]{1,0:T(8,128)(2,1)S(1)}, u32[]{:S(2)}, u32[]{:S(2)}) collective-permute-start(bf16[960,256]{1,0:T(8,128)(2,1)S(1)} %collective-permute-done.2.refs_2_), channel_id=1, source_target_pairs={{0,64},{64,128},{128,192},{192,0},{1,65},{65,129},{129,193},{193,1... | collective-permute-start | bytes 1474568 | tf_op jit(solution)/shard_map/ppermute | solution.py:17
  34.9 22.7 %collective-permute-start.5 = (bf16[960,256]{1,0:T(8,128)(2,1)S(1)}, bf16[960,256]{1,0:T(8,128)(2,1)S(1)}, u32[]{:S(2)}, u32[]{:S(2)}) collective-permute-start(bf16[960,256]{1,0:T(8,128)(2,1)S(1)} %collective-permute-done.4.refs_4_.refs_0_), channel_id=1, source_target_pairs={{0,32},{32,0},{1,33},{33,1},{2,34},{34,2},{3,35},{35,3},{4,36},{36... | collective-permute-start | bytes 1474568 | tf_op jit(solution)/shard_map/ppermute | solution.py:17
  44.4 21.1 %collective-permute-start.10 = (bf16[960,256]{1,0:T(8,128)(2,1)S(1)}, bf16[960,256]{1,0:T(8,128)(2,1)S(1)}, u32[]{:S(2)}, u32[]{:S(2)}) collective-permute-start(bf16[960,256]{1,0:T(8,128)(2,1)S(1)} %collective-permute-done.1.refs_1_), channel_id=1, source_target_pairs={{0,192},{64,0},{128,64},{192,128},{1,193},{65,1},{129,65},{193,129... | collective-permute-start | bytes 1474568 | tf_op jit(solution)/shard_map/ppermute | solution.py:17
  55.0 15.8 %collective-permute-start.9 = (bf16[960,256]{1,0:T(8,128)(2,1)S(1)}, bf16[960,256]{1,0:T(8,128)(2,1)S(1)}, u32[]{:S(2)}, u32[]{:S(2)}) collective-permute-start(bf16[960,256]{1,0:T(8,128)(2,1)S(1)} %collective-permute-done.1.refs_1_), channel_id=1, source_target_pairs={{0,64},{64,128},{128,192},{192,0},{1,65},{65,129},{129,193},{193,1... | collective-permute-start | bytes 1474568 | tf_op jit(solution)/shard_map/ppermute | solution.py:17
  56.0 25.3 %collective-permute-start.6 = (bf16[960,256]{1,0:T(8,128)(2,1)S(1)}, bf16[960,256]{1,0:T(8,128)(2,1)S(1)}, u32[]{:S(2)}, u32[]{:S(2)}) collective-permute-start(bf16[960,256]{1,0:T(8,128)(2,1)S(1)} %collective-permute-done.4.refs_4_.refs_0_), channel_id=1, source_target_pairs={{0,64},{64,128},{128,192},{192,0},{1,65},{65,129},{129,193},{193,1... | collective-permute-start | bytes 1474568 | tf_op jit(solution)/shard_map/ppermute | solution.py:17
  57.6 25.7 %collective-permute-start.15 = (bf16[960,256]{1,0:T(8,128)(2,1)S(1)}, bf16[960,256]{1,0:T(8,128)(2,1)S(1)}, u32[]{:S(2)}, u32[]{:S(2)}) collective-permute-start(bf16[960,256]{1,0:T(8,128)(2,1)S(1)} %collective-permute-done.7.refs_7_.refs_3_), channel_id=1, source_target_pairs={{0,192},{64,0},{128,64},{192,128},{1,193},{65,1},{129,65},{193,129... | collective-permute-start | bytes 1474568 | tf_op jit(solution)/shard_map/ppermute | solution.py:17
  65.5 27.7 %collective-permute-start.12 = (bf16[960,256]{1,0:T(8,128)(2,1)S(1)}, bf16[960,256]{1,0:T(8,128)(2,1)S(1)}, u32[]{:S(2)}, u32[]{:S(2)}) collective-permute-start(bf16[960,256]{1,0:T(8,128)(2,1)S(1)} %collective-permute-done.11.refs_2_), channel_id=1, source_target_pairs={{0,32},{32,0},{1,33},{33,1},{2,34},{34,2},{3,35},{35,3},{4,36},{36... | collective-permute-start | bytes 1474568 | tf_op jit(solution)/shard_map/ppermute | solution.py:17
  70.7 22.5 %collective-permute-start.13 = (bf16[960,256]{1,0:T(8,128)(2,1)S(1)}, bf16[960,256]{1,0:T(8,128)(2,1)S(1)}, u32[]{:S(2)}, u32[]{:S(2)}) collective-permute-start(bf16[960,256]{1,0:T(8,128)(2,1)S(1)} %collective-permute-done.5.refs_5_.refs_1_), channel_id=1, source_target_pairs={{0,64},{64,128},{128,192},{192,0},{1,65},{65,129},{129,193},{193,1... | collective-permute-start | bytes 1474568 | tf_op jit(solution)/shard_map/ppermute | solution.py:17
  81.3 12.0 %collective-permute-start.14 = (bf16[960,256]{1,0:T(8,128)(2,1)S(1)}, bf16[960,256]{1,0:T(8,128)(2,1)S(1)}, u32[]{:S(2)}, u32[]{:S(2)}) collective-permute-start(bf16[960,256]{1,0:T(8,128)(2,1)S(1)} %collective-permute-done.5.refs_5_.refs_1_), channel_id=1, source_target_pairs={{0,192},{64,0},{128,64},{192,128},{1,193},{65,1},{129,65},{193,129... | collective-permute-start | bytes 1474568 | tf_op jit(solution)/shard_map/ppermute | solution.py:17
  83.3 10.3 %collective-permute-start.16 = (bf16[960,256]{1,0:T(8,128)(2,1)S(1)}, bf16[960,256]{1,0:T(8,128)(2,1)S(1)}, u32[]{:S(2)}, u32[]{:S(2)}) collective-permute-start(bf16[960,256]{1,0:T(8,128)(2,1)S(1)} %collective-permute-done.15.refs_6_.refs_2_), channel_id=1, source_target_pairs={{0,32},{32,0},{1,33},{33,1},{2,34},{34,2},{3,35},{35,3},{4,36},{36... | collective-permute-start | bytes 1474568 | tf_op jit(solution)/shard_map/ppermute | solution.py:17
  100.5 8.2 %copy-start.1 = (s32[192,192]{1,0:T(8,128)S(1)}, s32[192,192]{1,0:T(8,128)}, u32[]{:S(2)}) copy-start(s32[192,192]{1,0:T(8,128)} %mask.1) | copy-start | bytes 442372
  107.1 5.2 %collective-permute-start.18 = (f32[96,384]{1,0:T(8,128)S(1)}, f32[96,384]{1,0:T(8,128)S(1)}, u32[]{:S(2)}, u32[]{:S(2)}) collective-permute-start(f32[96,384]{1,0:T(8,128)S(1)} %partial_scores.1), channel_id=1, source_target_pairs={{0,1},{1,0},{2,3},{3,2},{4,5},{5,4},{6,7},{7,6},{8,9},{9,8},{10,11... | collective-permute-start | bytes 442376 | tf_op jit(solution)/shard_map/ppermute | solution.py:17
  108.9 1.3 collective-permute-start
  112.7 1.9 %collective-permute-start.19 = (f32[2,384]{1,0:T(2,128)S(1)}, f32[2,384]{1,0:T(2,128)S(1)}, u32[]{:S(2)}, u32[]{:S(2)}) collective-permute-start(f32[2,384]{1,0:T(2,128)S(1)} %fusion.16), channel_id=1, source_target_pairs={{0,16},{2,18},{4,20},{6,22},{8,24},{10,26},{12,28},{14,30},{16,0},... | collective-permute-start | bytes 9224 | tf_op jit(solution)/shard_map/ppermute | solution.py:319
  112.7 3.7 %collective-permute-start.20 = (f32[2,384]{1,0:T(2,128)S(1)}, f32[2,384]{1,0:T(2,128)S(1)}, u32[]{:S(2)}, u32[]{:S(2)}) collective-permute-start(f32[2,384]{1,0:T(2,128)S(1)} %fusion.16), channel_id=1, source_target_pairs={{0,2},{2,0},{4,6},{6,4},{8,10},{10,8},{12,14},{14,12},{16,18},{18,... | collective-permute-start | bytes 9224 | tf_op jit(solution)/shard_map/ppermute | solution.py:319
  112.9 3.5 %collective-permute-start.21 = (f32[2,384]{1,0:T(2,128)S(1)}, f32[2,384]{1,0:T(2,128)S(1)}, u32[]{:S(2)}, u32[]{:S(2)}) collective-permute-start(f32[2,384]{1,0:T(2,128)S(1)} %fusion.16), channel_id=1, source_target_pairs={{0,18},{2,16},{4,22},{6,20},{8,26},{10,24},{12,30},{14,28},{16,2},... | collective-permute-start | bytes 9224 | tf_op jit(solution)/shard_map/ppermute | solution.py:319
  116.5 14.2 %collective-permute-start.22 = (f32[2,384]{1,0:T(2,128)S(1)}, f32[2,384]{1,0:T(2,128)S(1)}, u32[]{:S(2)}, u32[]{:S(2)}) collective-permute-start(f32[2,384]{1,0:T(2,128)S(1)} %pad_maximum_fusion.3), channel_id=1, source_target_pairs={{0,4},{2,6},{4,0},{6,2},{8,12},{10,14},{12,8},{14,10},{16,20},{18,... | collective-permute-start | bytes 9224 | tf_op jit(solution)/shard_map/ppermute | solution.py:319
  119.8 10.8 %collective-permute-start.23 = (f32[2,384]{1,0:T(2,128)S(1)}, f32[2,384]{1,0:T(2,128)S(1)}, u32[]{:S(2)}, u32[]{:S(2)}) collective-permute-start(f32[2,384]{1,0:T(2,128)S(1)} %pad_maximum_fusion.3), channel_id=1, source_target_pairs={{0,8},{2,10},{4,12},{6,14},{8,0},{10,2},{12,4},{14,6},{16,24},{18,... | collective-permute-start | bytes 9224 | tf_op jit(solution)/shard_map/ppermute | solution.py:319
  124.7 5.9 %collective-permute-start.24 = (f32[2,384]{1,0:T(2,128)S(1)}, f32[2,384]{1,0:T(2,128)S(1)}, u32[]{:S(2)}, u32[]{:S(2)}) collective-permute-start(f32[2,384]{1,0:T(2,128)S(1)} %pad_maximum_fusion.3), channel_id=1, source_target_pairs={{0,12},{2,14},{4,8},{6,10},{8,4},{10,6},{12,0},{14,2},{16,28},{18,... | collective-permute-start | bytes 9224 | tf_op jit(solution)/shard_map/ppermute | solution.py:319
  137.6 4.4 %collective-permute-start.25 = (bf16[128,256]{1,0:T(8,128)(2,1)S(1)}, bf16[128,256]{1,0:T(8,128)(2,1)S(1)}, u32[]{:S(2)}, u32[]{:S(2)}) collective-permute-start(bf16[128,256]{1,0:T(8,128)(2,1)S(1)} %get-tuple-element.36), channel_id=1, source_target_pairs={{0,1},{1,0},{16,17},{17,16},{2,3},{3,2},{18,19},{19,18},{4,5},{5,4... | collective-permute-start | bytes 196616 | tf_op jit(solution)/shard_map/ppermute | solution.py:319
  139.2 2.8 %collective-permute-start.26 = (bf16[128,256]{1,0:T(8,128)(2,1)S(1)}, bf16[128,256]{1,0:T(8,128)(2,1)S(1)}, u32[]{:S(2)}, u32[]{:S(2)}) collective-permute-start(bf16[128,256]{1,0:T(8,128)(2,1)S(1)} %get-tuple-element.38), channel_id=1, source_target_pairs={{0,16},{1,17},{16,0},{17,1},{2,18},{3,19},{18,2},{19,3},{4,20},{5,... | collective-permute-start | bytes 196616 | tf_op jit(solution)/shard_map/ppermute | solution.py:319
  139.2 3.7 %collective-permute-start.27 = (bf16[128,256]{1,0:T(8,128)(2,1)S(1)}, bf16[128,256]{1,0:T(8,128)(2,1)S(1)}, u32[]{:S(2)}, u32[]{:S(2)}) collective-permute-start(bf16[128,256]{1,0:T(8,128)(2,1)S(1)} %get-tuple-element.37), channel_id=1, source_target_pairs={{0,17},{1,16},{16,1},{17,0},{2,19},{3,18},{18,3},{19,2},{4,21},{5,... | collective-permute-start | bytes 196616 | tf_op jit(solution)/shard_map/ppermute | solution.py:319
  143.6 21.5 %all-to-all-start = ((bf16[64,2,256]{2,1,0:T(2,128)(2,1)}), bf16[64,2,256]{2,1,0:T(2,128)(2,1)S(1)}, u32[]{:S(2)}, u32[]{:S(2)}) async-start(bf16[64,2,256]{2,1,0:T(2,128)(2,1)} %reshape.57), calls=%async_computation | async-start | bytes 131072 | tf_op jit(solution)/shard_map/all_to_all | solution.py:393

commit v4 on v3

--- a/solution.py
+++ b/solution.py
@@ -10,6 +10,9 @@
 BF16 = jnp.bfloat16
 F32 = jnp.float32
 SOURCES = ((0, 0), (0, 1), (-1, 0), (1, 0), (-1, 1), (1, 1), (2, 0), (2, 1))
+
+
+ROUNDS = ((3, 2, 1), (14, 6, 8))
 
 
 def shifted(x, axis, step):
@@ -28,14 +31,18 @@
     far_beside = shifted(far, "xh", 1)
     far_down = shifted(far, "y", -1)
     far_up = shifted(far, "y", 1)
-    far_across = shifted(far_down, "y", -1)
+    middle = far_down.shape[0] // 2
+    far_across = shifted(far_down[:middle], "y", -1)
+    far_across_too = shifted(far_down[middle:], "y", -1)
     far_beside_down = shifted(far_beside, "y", -1)
     far_beside_up = shifted(far_beside, "y", 1)
     across_beside = shifted(across, "xh", 1)
     far_across_beside = shifted(far_across, "xh", 1)
+    far_across_beside_too = shifted(far_across_too, "xh", 1)
     return (
         [near, beside, up, down, beside_up, beside_down, across, across_beside],
-        [far, far_beside, far_up, far_down, far_beside_up, far_beside_down, far_across, far_across_beside],
+        [far, far_beside, far_up, far_down, far_beside_up, far_beside_down]
+        + [far_across, far_across_too, far_across_beside, far_across_beside_too],
     )
 
 
@@ -49,35 +56,33 @@
 
 
 def weighted_kernel(*refs):
-    chips = (len(refs) - 6) // 2
-    chunks = refs[: 2 * chips]
-    lines, lines_far, noise, out, quad, wide = refs[2 * chips :]
+    *chunks, lines, lines_far, noise, out, quad, wide = refs
     rows = out.shape[0]
     pitch = rows + 1
     step = noise.shape[0]
     some = step // rows
-    owned = chunks[0].shape[0] // rows
-    for chip in range(chips):
-        for i in range(owned // some):
-            at = slice(i * step, (i + 1) * step)
-            slices = jnp.dot(chunks[chip][at, :], lines[...], preferred_element_type=F32)
-            slices += jnp.dot(chunks[chips + chip][at, :], lines_far[...], preferred_element_type=F32)
-            slices = slices.astype(BF16).astype(F32)
-            weighted = noise[...] * slices
-            first = chip * owned + i * some
-            for k in range(some):
-                one = weighted[k * rows : (k + 1) * rows, :]
-                to = slice((first + k) * pitch, (first + k) * pitch + rows)
-                wide[0, to, :] = one[:, :128]
-                wide[1, to, :] = one[:, 128:]
-            square = weighted * slices
-            square = square[:, :128] + square[:, 128:]
-            quad[first : first + some] = jnp.sum(square.reshape(some, rows // 8, 8, 128), axis=1)
+    count = quad.shape[0]
+    pieces = [(c, slice(i, i + step)) for c in chunks for i in range(0, c.shape[0], step)]
+    half = len(pieces) // 2
+    for i, ((near, at), (far, far_at)) in enumerate(zip(pieces[:half], pieces[half:])):
+        slices = jnp.dot(near[at, :], lines[...], preferred_element_type=F32)
+        slices += jnp.dot(far[far_at, :], lines_far[...], preferred_element_type=F32)
+        slices = slices.astype(BF16).astype(F32)
+        weighted = noise[...] * slices
+        first = i * some
+        for k in range(some):
+            one = weighted[k * rows : (k + 1) * rows, :]
+            to = slice((first + k) * pitch, (first + k) * pitch + rows)
+            wide[0, to, :] = one[:, :128]
+            wide[1, to, :] = one[:, 128:]
+        square = weighted * slices
+        square = square[:, :128] + square[:, 128:]
+        quad[first : first + some] = jnp.sum(square.reshape(some, rows // 8, 8, 128), axis=1)
 
     def turn(r, carry):
         for half in range(2):
             out[r, :, half * 128 : half * 128 + 128] = wide[
-                half, pl.ds(r, chips * owned, stride=pitch), :
+                half, pl.ds(r, count, stride=pitch), :
             ].astype(BF16)
         return carry
 
@@ -85,8 +90,7 @@
 
 
 def weighted_slices(near, far, lines, lines_far, noise, rows):
-    chips = len(near)
-    count = chips * near[0].shape[0] // rows
+    count = sum(x.shape[0] for x in near) // rows
     width = lines.shape[1]
     return pl.pallas_call(
         weighted_kernel,
@@ -225,22 +229,23 @@
 
 
 def turn_kernel(*refs):
-    chunks, out, flat = refs[:-2], refs[-2], refs[-1]
-    size = chunks[0].shape[0]
-    for i, chunk in enumerate(chunks):
-        flat[i * size : (i + 1) * size, :] = chunk[...]
+    *chunks, out, flat = refs
+    at = 0
+    for chunk in chunks:
+        flat[at : at + chunk.shape[0], :] = chunk[...]
+        at += chunk.shape[0]
 
     def turn(i, carry):
         at = pl.multiple_of(i * 128, 128)
         out[:, pl.ds(at, 128)] = flat[pl.ds(at, 128), :].T
         return carry
 
-    lax.fori_loop(0, len(chunks) * size // 128, turn, 0, unroll=2)
+    lax.fori_loop(0, flat.shape[0] // 128, turn, 0, unroll=2)
 
 
 def turned_weights(chunks):
-    size, lines = chunks[0].shape
-    span = len(chunks) * size
+    span = sum(x.shape[0] for x in chunks)
+    lines = chunks[0].shape[1]
     return pl.pallas_call(
         turn_kernel,
         out_shape=pltpu.VMEM((lines, span), BF16),
@@ -367,7 +372,7 @@
         near[pick], far[pick], lines, lines_far, noise_tiled, half_rows
     )
     first, quad_first = weigh(slice(0, 4))
-    second, quad_second = weigh(slice(4, 8))
+    second, quad_second = weigh(slice(4, None))
     part = partial_scores(first, second, quad_first, quad_second, own, beside)
     turned = [
         turned_weights(near[:4]),
@@ -380,7 +385,7 @@
     top = jnp.max(jnp.where(allowed > 0.5, scores, -1e30), axis=0)
     mass = jnp.sum(jnp.where(allowed > 0.5, jnp.exp(scores - top[None]), 0.0), axis=0)
     pair = in_core_order(jnp.stack([top, mass]), first_core, shots)
-    for masks in ((8, 1, 9), (2, 4, 6)):
+    for masks in ROUNDS:
         pair = combined([pair] + [crossed(pair, ("core", "ori"), m) for m in masks])
     pair = in_core_order(pair, first_core, shots)
     log_evidence = (pair[0] + jnp.log(pair[1]))[:shots]

time: 167 us -> 160 us (0.958)
  waiting for transfers between devices: 71.5 us -> 62.8 us
    ppermute x19 -> x21, waiting for transfers between devices: 55.9 us -> 46.6 us  [shifted(): return lax.ppermute(x, axis, [(i, (i + step) % n) for i in range(n)])]
    ppermute x19 -> x21, starting transfers between devices: 32 us -> 35 us  [shifted(): return lax.ppermute(x, axis, [(i, (i + step) % n) for i in range(n)])]
    all_to_all x1, starting transfers between devices: 10.2 us -> 8.45 us  [step(): arrived = lax.all_to_all(square, ('y', 'xh', 'ori'), 0, 0, tiled=True)]
  transfers between devices with their start and end apart: 29 -> 31, of which waited for: 13 -> 15; matrix products, arithmetic and copies ran while one was open for 2% -> 2% of each run, Pallas kernels for 9% -> 9%
where the time goes in v4:
time: 160 us; the launch traced here: 158 us
  waiting for transfers between devices  62.8 us (39%)
  starting transfers between devices  55.7 us (35%)
  Pallas kernels  32.8 us (20%)
  matrix products  2.02 us (1%)
  other arithmetic  1.94 us (1%)
  local copies, waits for them, and re-layouts  1.76 us (1%)
    ppermute x21, waiting for transfers between devices, shifted(): return lax.ppermute(x, axis, [(i, (i + step) % n) for i in range(n)])  46.6 us
    ppermute x21, starting transfers between devices, shifted(): return lax.ppermute(x, axis, [(i, (i + step) % n) for i in range(n)])  35 us
    ppermute x9, starting transfers between devices, crossed(): lax.ppermute(x, axes, [(i, i ^ mask) for i in range(lax.axis_size(axes))])  12.2 us
    all_to_all x1, waiting for transfers between devices, step(): arrived = lax.all_to_all(square, ('y', 'xh', 'ori'), 0, 0, tiled=True)  10.7 us
    pallas_call x2, Pallas kernels, rows_major(): pl.pallas_call(rows_major_kernel, in_specs=[pl.BlockSpec(memory_space=pl....  10.4 us
    all_to_all x1, starting transfers between devices, step(): arrived = lax.all_to_all(square, ('y', 'xh', 'ori'), 0, 0, tiled=True)  8.45 us
    pallas_call x1, Pallas kernels, insertion(): pl.pallas_call(insert_kernel, in_specs=[pl.BlockSpec(memory_space=pltpu.S...  6.68 us
    pallas_call x1, Pallas kernels, partial_scores(): pl.pallas_call(score_kernel, out_shape=jax.ShapeDtypeStruct((2 * count, 2...  6.51 us
  transfers between devices with their start and end apart: 31, of which 15 were waited for; matrix products, arithmetic and copies ran while one was open for 2% of the time, Pallas kernels for 9%

profile of v4, /device:TPU:32, one launch (start us, length us, event | category | flops | bytes accessed | tf_op | source)
XLA Modules:
  0.0 158.0 jit_solution(6300775634396438688)
XLA Ops:
  0.8 1.0 reshape.51.refs_8_.refs_10_
  1.8 1.0 fusion.4
  2.8 1.6 collective-permute-start.4
  4.4 1.0 fusion.2
  5.4 1.7 %collective-permute-start.2 = (bf16[960,256]{1,0:T(8,128)(2,1)S(1)}, bf16[960,256]{1,0:T(8,128)(2,1)S(1)}, u32[]{:S(2)}, u32[]{:S(2)}) collective-permute-start(bf16[960,256]{1,0:T(8,128)(2,1)S(1)} %bitcast.23), channel_id=1, source_target_pairs={{0,64},{64,128},{128,192},{192,0},{1,65},{65,129},{129,193},{193,1... | collective-permute-start | bytes 1474568 | tf_op jit(solution)/shard_map/ppermute | solution.py:20
  7.6 3.0 %collective-permute-start.1 = (bf16[960,256]{1,0:T(8,128)(2,1)S(1)}, bf16[960,256]{1,0:T(8,128)(2,1)S(1)}, u32[]{:S(2)}, u32[]{:S(2)}) collective-permute-start(bf16[960,256]{1,0:T(8,128)(2,1)S(1)} %bitcast.24), channel_id=1, source_target_pairs={{0,32},{32,0},{1,33},{33,1},{2,34},{34,2},{3,35},{35,3},{4,36},{36... | collective-permute-start | bytes 1474568 | tf_op jit(solution)/shard_map/ppermute | solution.py:20
  10.6 9.2 %collective-permute-done.8.refs_9_.refs_11_ = bf16[256,256]{1,0:T(8,128)(2,1)S(1)} collective-permute-done((bf16[256,256]{1,0:T(8,128)(2,1)S(1)}, bf16[256,256]{1,0:T(8,128)(2,1)S(1)}, u32[]{:S(2)}, u32[]{:S(2)}) %collective-permute-start.8) | collective-permute-done | bytes 131104 | tf_op jit(solution)/shard_map/ppermute | solution.py:20
  19.8 3.0 %collective-permute-start.3 = (bf16[960,256]{1,0:T(8,128)(2,1)S(1)}, bf16[960,256]{1,0:T(8,128)(2,1)S(1)}, u32[]{:S(2)}, u32[]{:S(2)}) collective-permute-start(bf16[960,256]{1,0:T(8,128)(2,1)S(1)} %bitcast.25), channel_id=1, source_target_pairs={{0,192},{64,0},{128,64},{192,128},{1,193},{65,1},{129,65},{193,129... | collective-permute-start | bytes 1474568 | tf_op jit(solution)/shard_map/ppermute | solution.py:20
  22.8 0.7 collective-permute-start.7
  23.6 1.3 collective-permute-start.11
  24.9 7.1 %collective-permute-done.1.refs_1_ = bf16[960,256]{1,0:T(8,128)(2,1)S(1)} collective-permute-done((bf16[960,256]{1,0:T(8,128)(2,1)S(1)}, bf16[960,256]{1,0:T(8,128)(2,1)S(1)}, u32[]{:S(2)}, u32[]{:S(2)}) %collective-permute-start.1) | collective-permute-done | bytes 491552 | tf_op jit(solution)/shard_map/ppermute | solution.py:20
  32.0 0.8 collective-permute-start.5
  32.8 1.6 %collective-permute-done.3.refs_3_ = bf16[960,256]{1,0:T(8,128)(2,1)S(1)} collective-permute-done((bf16[960,256]{1,0:T(8,128)(2,1)S(1)}, bf16[960,256]{1,0:T(8,128)(2,1)S(1)}, u32[]{:S(2)}, u32[]{:S(2)}) %collective-permute-start.3) | collective-permute-done | bytes 491552 | tf_op jit(solution)/shard_map/ppermute | solution.py:20
  34.4 3.7 %collective-permute-start.10 = (bf16[960,256]{1,0:T(8,128)(2,1)S(1)}, bf16[960,256]{1,0:T(8,128)(2,1)S(1)}, u32[]{:S(2)}, u32[]{:S(2)}) collective-permute-start(bf16[960,256]{1,0:T(8,128)(2,1)S(1)} %collective-permute-done.1.refs_1_), channel_id=1, source_target_pairs={{0,192},{64,0},{128,64},{192,128},{1,193},{65,1},{129,65},{193,129... | collective-permute-start | bytes 1474568 | tf_op jit(solution)/shard_map/ppermute | solution.py:20
  38.1 6.8 %collective-permute-done.7.refs_7_.refs_3_ = bf16[960,256]{1,0:T(8,128)(2,1)S(1)} collective-permute-done((bf16[960,256]{1,0:T(8,128)(2,1)S(1)}, bf16[960,256]{1,0:T(8,128)(2,1)S(1)}, u32[]{:S(2)}, u32[]{:S(2)}) %collective-permute-start.7) | collective-permute-done | bytes 491552 | tf_op jit(solution)/shard_map/ppermute | solution.py:20
  45.0 1.0 collective-permute-start.9
  46.0 1.6 collective-permute-start.6
  47.6 1.7 %collective-permute-start.15 = (bf16[480,256]{1,0:T(8,128)(2,1)S(1)}, bf16[480,256]{1,0:T(8,128)(2,1)S(1)}, u32[]{:S(2)}, u32[]{:S(2)}) collective-permute-start(bf16[480,256]{1,0:T(8,128)(2,1)S(1)} %get-tuple-element.37), channel_id=1, source_target_pairs={{0,192},{64,0},{128,64},{192,128},{1,193},{65,1},{129,65},{193,129... | collective-permute-start | bytes 737288 | tf_op jit(solution)/shard_map/ppermute | solution.py:20
  49.4 6.1 %collective-permute-done.10.refs_1_ = bf16[960,256]{1,0:T(8,128)(2,1)S(1)} collective-permute-done((bf16[960,256]{1,0:T(8,128)(2,1)S(1)}, bf16[960,256]{1,0:T(8,128)(2,1)S(1)}, u32[]{:S(2)}, u32[]{:S(2)}) %collective-permute-start.10) | collective-permute-done | bytes 491552 | tf_op jit(solution)/shard_map/ppermute | solution.py:20
  55.5 3.7 %collective-permute-start.16 = (bf16[480,256]{1,0:T(8,128)(2,1)S(1)}, bf16[480,256]{1,0:T(8,128)(2,1)S(1)}, u32[]{:S(2)}, u32[]{:S(2)}) collective-permute-start(bf16[480,256]{1,0:T(8,128)(2,1)S(1)} %get-tuple-element.36), channel_id=1, source_target_pairs={{0,192},{64,0},{128,64},{192,128},{1,193},{65,1},{129,65},{193,129... | collective-permute-start | bytes 737288 | tf_op jit(solution)/shard_map/ppermute | solution.py:20
  59.2 1.5 collective-permute-done.9.refs_0_
  60.7 3.0 %collective-permute-start.12 = (bf16[960,256]{1,0:T(8,128)(2,1)S(1)}, bf16[960,256]{1,0:T(8,128)(2,1)S(1)}, u32[]{:S(2)}, u32[]{:S(2)}) collective-permute-start(bf16[960,256]{1,0:T(8,128)(2,1)S(1)} %collective-permute-done.11.refs_2_), channel_id=1, source_target_pairs={{0,32},{32,0},{1,33},{33,1},{2,34},{34,2},{3,35},{35,3},{4,36},{36... | collective-permute-start | bytes 1474568 | tf_op jit(solution)/shard_map/ppermute | solution.py:20
  64.3 3.1 %collective-permute-done.6.refs_6_.refs_2_ = bf16[960,256]{1,0:T(8,128)(2,1)S(1)} collective-permute-done((bf16[960,256]{1,0:T(8,128)(2,1)S(1)}, bf16[960,256]{1,0:T(8,128)(2,1)S(1)}, u32[]{:S(2)}, u32[]{:S(2)}) %collective-permute-start.6) | collective-permute-done | bytes 491552 | tf_op jit(solution)/shard_map/ppermute | solution.py:20
  67.3 3.2 %collective-permute-start.14 = (bf16[960,256]{1,0:T(8,128)(2,1)S(1)}, bf16[960,256]{1,0:T(8,128)(2,1)S(1)}, u32[]{:S(2)}, u32[]{:S(2)}) collective-permute-start(bf16[960,256]{1,0:T(8,128)(2,1)S(1)} %collective-permute-done.5.refs_5_.refs_1_), channel_id=1, source_target_pairs={{0,192},{64,0},{128,64},{192,128},{1,193},{65,1},{129,65},{193,129... | collective-permute-start | bytes 1474568 | tf_op jit(solution)/shard_map/ppermute | solution.py:20
  70.6 6.8 %collective-permute-done.17.refs_8_.refs_4_ = bf16[480,256]{1,0:T(8,128)(2,1)S(1)} collective-permute-done((bf16[480,256]{1,0:T(8,128)(2,1)S(1)}, bf16[480,256]{1,0:T(8,128)(2,1)S(1)}, u32[]{:S(2)}, u32[]{:S(2)}) %collective-permute-start.17) | collective-permute-done | bytes 245792 | tf_op jit(solution)/shard_map/ppermute | solution.py:20
  77.4 3.0 %collective-permute-start.18 = (bf16[480,256]{1,0:T(8,128)(2,1)S(1)}, bf16[480,256]{1,0:T(8,128)(2,1)S(1)}, u32[]{:S(2)}, u32[]{:S(2)}) collective-permute-start(bf16[480,256]{1,0:T(8,128)(2,1)S(1)} %collective-permute-done.16.refs_7_.refs_3_), channel_id=1, source_target_pairs={{0,32},{32,0},{1,33},{33,1},{2,34},{34,2},{3,35},{35,3},{4,36},{36... | collective-permute-start | bytes 737288 | tf_op jit(solution)/shard_map/ppermute | solution.py:20
  80.4 5.2 %rows_major.2.own = bf16[80,192,256]{2,1,0:T(8,128)(2,1)S(1)} custom-call(bf16[192,80,256]{2,1,0:T(8,128)(2,1)} %shots.1), custom_call_target="tpu_custom_call" | custom-call | tf_op jit(solution)/shard_map/rows_major/pallas_call | solution.py:186
  85.6 1.6 %weighted_slices.2 = (bf16[80,48,256]{2,1,0:T(8,128)(2,1)S(1)}, f32[48,8,128]{2,1,0:T(8,128)S(1)}) custom-call(bf16[960,256]{1,0:T(8,128)(2,1)S(1)} %bitcast.26, bf16[960,256]{1,0:T(8,128)(2,1)S(1)} %collective-permute-done.1.refs_1_, bf16[960,256]{1,0:T(8,128)(2,1)S(1)} %collective-permute-done.2.refs_2_, ...), custom_call_target="tpu_custom_call" | custom-call | tf_op jit(solution)/shard_map/weighted_slices/pallas_call | solution.py:95
  87.3 1.6 %weighted_slices.3 = (bf16[80,48,256]{2,1,0:T(8,128)(2,1)S(1)}, f32[48,8,128]{2,1,0:T(8,128)S(1)}) custom-call(bf16[960,256]{1,0:T(8,128)(2,1)S(1)} %collective-permute-done.9.refs_0_, bf16[960,256]{1,0:T(8,128)(2,1)S(1)} %collective-permute-done.10.refs_1_, bf16[960,256]{1,0:T(8,128)(2,1)S(1)} %collective-permute-done.11.refs_2_, ...), custom_call_target="tpu_custom_call" | custom-call | tf_op jit(solution)/shard_map/weighted_slices/pallas_call | solution.py:95
  89.0 5.2 %rows_major.3.beside = bf16[80,192,256]{2,1,0:T(8,128)(2,1)S(1)} custom-call(bf16[192,80,256]{2,1,0:T(8,128)(2,1)} %collective-permute-done.19.shots), custom_call_target="tpu_custom_call" | custom-call | tf_op jit(solution)/shard_map/rows_major/pallas_call | solution.py:186
  94.2 6.5 %partial_scores.1 = f32[96,384]{1,0:T(8,128)S(1)} custom-call(bf16[80,48,256]{2,1,0:T(8,128)(2,1)S(1)} %get-tuple-element.26.first, bf16[80,48,256]{2,1,0:T(8,128)(2,1)S(1)} %get-tuple-element.27.second, f32[48,8,128]{2,1,0:T(8,128)S(1)} %get-tuple-element.28.quad_first, f32[48,8,128]{2,1,0:T(8,128)S(1)} %get-tuple-element.29.quad_second, ...), custom_call_target="tpu_custom_call" | custom-call | tf_op jit(solution)/shard_map/partial_scores/pallas_call | solution.py:138
  101.7 1.2 collective-permute-done
  102.9 3.0 %collective-permute-done.20 = f32[96,384]{1,0:T(8,128)S(1)} collective-permute-done((f32[96,384]{1,0:T(8,128)S(1)}, f32[96,384]{1,0:T(8,128)S(1)}, u32[]{:S(2)}, u32[]{:S(2)}) %collective-permute-start.20) | collective-permute-done | bytes 147488 | tf_op jit(solution)/shard_map/ppermute | solution.py:20
  106.3 2.0 %collective-permute-start.21 = (f32[2,384]{1,0:T(2,128)S(1)}, f32[2,384]{1,0:T(2,128)S(1)}, u32[]{:S(2)}, u32[]{:S(2)}) collective-permute-start(f32[2,384]{1,0:T(2,128)S(1)} %fusion.16), channel_id=1, source_target_pairs={{0,6},{2,4},{4,2},{6,0},{8,14},{10,12},{12,10},{14,8},{16,22},{18,... | collective-permute-start | bytes 9224 | tf_op jit(solution)/shard_map/ppermute | solution.py:324
  108.2 1.5 collective-permute-start.22
  109.7 1.4 collective-permute-start.23
  111.1 1.7 %collective-permute-done.22 = f32[2,384]{1,0:T(2,128)S(1)} collective-permute-done((f32[2,384]{1,0:T(2,128)S(1)}, f32[2,384]{1,0:T(2,128)S(1)}, u32[]{:S(2)}, u32[]{:S(2)}) %collective-permute-start.22) | collective-permute-done | bytes 3104 | tf_op jit(solution)/shard_map/ppermute | solution.py:324
  113.6 4.8 %collective-permute-start.25 = (f32[2,384]{1,0:T(2,128)S(1)}, f32[2,384]{1,0:T(2,128)S(1)}, u32[]{:S(2)}, u32[]{:S(2)}) collective-permute-start(f32[2,384]{1,0:T(2,128)S(1)} %pad_maximum_fusion.3), channel_id=1, source_target_pairs={{0,12},{2,14},{4,8},{6,10},{8,4},{10,6},{12,0},{14,2},{16,28},{18,... | collective-permute-start | bytes 9224 | tf_op jit(solution)/shard_map/ppermute | solution.py:324
  118.5 1.4 turned_weights.4.refs_0_
  119.9 1.4 turned_weights.5.refs_1_
  121.4 1.4 turned_weights.7.refs_3_
  122.8 1.4 turned_weights.6.refs_2_
  124.5 6.7 %insertion.1 = bf16[4,128,256]{2,1,0:T(8,128)(2,1)S(1)} custom-call(s32[1]{0:T(128)} %bitcast.2.my_core, f32[96,384]{1,0:T(8,128)S(1)} %get-tuple-element.35.scores, f32[96,384]{1,0:T(8,128)S(1)} %maximum_convert_fusion.allowed, f32[2,384]{1,0:T(2,128)S(1)} %fusion.15.stats, bf16[80,192,256]{2,1,0:T(8,128)(2,1)S(1)} %rows_major.2.own, ...), custom_call_target="tpu_custom_call" | custom-call | tf_op jit(solution)/shard_map/insertion/pallas_call | solution.py:307
  131.2 0.9 collective-permute-start.27
  132.3 1.3 collective-permute-start.29
  133.6 2.8 %collective-permute-done.27 = bf16[128,256]{1,0:T(8,128)(2,1)S(1)} collective-permute-done((bf16[128,256]{1,0:T(8,128)(2,1)S(1)}, bf16[128,256]{1,0:T(8,128)(2,1)S(1)}, u32[]{:S(2)}, u32[]{:S(2)}) %collective-permute-start.27) | collective-permute-done | bytes 65568 | tf_op jit(solution)/shard_map/ppermute | solution.py:324
  137.6 8.4 %all-to-all-start = ((bf16[64,2,256]{2,1,0:T(2,128)(2,1)}), bf16[64,2,256]{2,1,0:T(2,128)(2,1)S(1)}, u32[]{:S(2)}, u32[]{:S(2)}) async-start(bf16[64,2,256]{2,1,0:T(2,128)(2,1)} %reshape.57), calls=%async_computation | async-start | bytes 131072 | tf_op jit(solution)/shard_map/all_to_all | solution.py:398
  146.6 10.7 %all-to-all-done = bf16[64,2,256]{2,1,0:T(2,128)(2,1)S(1)} async-done(((bf16[64,2,256]{2,1,0:T(2,128)(2,1)}), bf16[64,2,256]{2,1,0:T(2,128)(2,1)S(1)}, u32[]{:S(2)}, u32[]{:S(2)}) %all-to-all-start) | async-done | bytes 65568 | tf_op jit(solution)/shard_map/all_to_all | solution.py:398
  (57 shorter events, 6.3 us)
Async XLA Ops:
  0.6 1.2 copy-start
  0.6 88.3 %collective-permute-start.19 = (bf16[192,80,256]{2,1,0:T(8,128)(2,1)}, bf16[192,80,256]{2,1,0:T(8,128)(2,1)}, u32[]{:S(2)}, u32[]{:S(2)}) collective-permute-start(bf16[192,80,256]{2,1,0:T(8,128)(2,1)} %shots.1), channel_id=1, source_target_pairs={{0,16},{16,0},{1,17},{17,1},{2,18},{18,2},{3,19},{19,3},{4,20},{20... | collective-permute-start | bytes 23592968 | tf_op jit(solution)/shard_map/ppermute | solution.py:20
  2.8 20.0 %collective-permute-start.4 = (bf16[960,256]{1,0:T(8,128)(2,1)S(1)}, bf16[960,256]{1,0:T(8,128)(2,1)S(1)}, u32[]{:S(2)}, u32[]{:S(2)}) collective-permute-start(bf16[960,256]{1,0:T(8,128)(2,1)S(1)} %bitcast.30), channel_id=1, source_target_pairs={{0,1},{1,0},{2,3},{3,2},{4,5},{5,4},{6,7},{7,6},{8,9},{9,8},{10,11... | collective-permute-start | bytes 1474568 | tf_op jit(solution)/shard_map/ppermute | solution.py:20
  5.4 18.2 %collective-permute-start.2 = (bf16[960,256]{1,0:T(8,128)(2,1)S(1)}, bf16[960,256]{1,0:T(8,128)(2,1)S(1)}, u32[]{:S(2)}, u32[]{:S(2)}) collective-permute-start(bf16[960,256]{1,0:T(8,128)(2,1)S(1)} %bitcast.23), channel_id=1, source_target_pairs={{0,64},{64,128},{128,192},{192,0},{1,65},{65,129},{129,193},{193,1... | collective-permute-start | bytes 1474568 | tf_op jit(solution)/shard_map/ppermute | solution.py:20
  7.1 12.7 %collective-permute-start.8 = (bf16[256,256]{1,0:T(8,128)(2,1)S(1)}, bf16[256,256]{1,0:T(8,128)(2,1)S(1)}, u32[]{:S(2)}, u32[]{:S(2)}) collective-permute-start(bf16[256,256]{1,0:T(8,128)(2,1)S(1)} %reshape.51.refs_8_.refs_10_), channel_id=1, source_target_pairs={{0,1},{1,0},{2,3},{3,2},{4,5},{5,4},{6,7},{7,6},{8,9},{9,8},{10,11... | collective-permute-start | bytes 393224 | tf_op jit(solution)/shard_map/ppermute | solution.py:20
  7.6 24.4 %collective-permute-start.1 = (bf16[960,256]{1,0:T(8,128)(2,1)S(1)}, bf16[960,256]{1,0:T(8,128)(2,1)S(1)}, u32[]{:S(2)}, u32[]{:S(2)}) collective-permute-start(bf16[960,256]{1,0:T(8,128)(2,1)S(1)} %bitcast.24), channel_id=1, source_target_pairs={{0,32},{32,0},{1,33},{33,1},{2,34},{34,2},{3,35},{35,3},{4,36},{36... | collective-permute-start | bytes 1474568 | tf_op jit(solution)/shard_map/ppermute | solution.py:20
  19.8 14.6 %collective-permute-start.3 = (bf16[960,256]{1,0:T(8,128)(2,1)S(1)}, bf16[960,256]{1,0:T(8,128)(2,1)S(1)}, u32[]{:S(2)}, u32[]{:S(2)}) collective-permute-start(bf16[960,256]{1,0:T(8,128)(2,1)S(1)} %bitcast.25), channel_id=1, source_target_pairs={{0,192},{64,0},{128,64},{192,128},{1,193},{65,1},{129,65},{193,129... | collective-permute-start | bytes 1474568 | tf_op jit(solution)/shard_map/ppermute | solution.py:20
  22.8 22.1 %collective-permute-start.7 = (bf16[960,256]{1,0:T(8,128)(2,1)S(1)}, bf16[960,256]{1,0:T(8,128)(2,1)S(1)}, u32[]{:S(2)}, u32[]{:S(2)}) collective-permute-start(bf16[960,256]{1,0:T(8,128)(2,1)S(1)} %collective-permute-done.4.refs_4_.refs_0_), channel_id=1, source_target_pairs={{0,192},{64,0},{128,64},{192,128},{1,193},{65,1},{129,65},{193,129... | collective-permute-start | bytes 1474568 | tf_op jit(solution)/shard_map/ppermute | solution.py:20
  23.6 22.4 %collective-permute-start.11 = (bf16[960,256]{1,0:T(8,128)(2,1)S(1)}, bf16[960,256]{1,0:T(8,128)(2,1)S(1)}, u32[]{:S(2)}, u32[]{:S(2)}) collective-permute-start(bf16[960,256]{1,0:T(8,128)(2,1)S(1)} %collective-permute-done.2.refs_2_), channel_id=1, source_target_pairs={{0,64},{64,128},{128,192},{192,0},{1,65},{65,129},{129,193},{193,1... | collective-permute-start | bytes 1474568 | tf_op jit(solution)/shard_map/ppermute | solution.py:20
  32.0 15.6 %collective-permute-start.5 = (bf16[960,256]{1,0:T(8,128)(2,1)S(1)}, bf16[960,256]{1,0:T(8,128)(2,1)S(1)}, u32[]{:S(2)}, u32[]{:S(2)}) collective-permute-start(bf16[960,256]{1,0:T(8,128)(2,1)S(1)} %collective-permute-done.4.refs_4_.refs_0_), channel_id=1, source_target_pairs={{0,32},{32,0},{1,33},{33,1},{2,34},{34,2},{3,35},{35,3},{4,36},{36... | collective-permute-start | bytes 1474568 | tf_op jit(solution)/shard_map/ppermute | solution.py:20
  34.4 21.1 %collective-permute-start.10 = (bf16[960,256]{1,0:T(8,128)(2,1)S(1)}, bf16[960,256]{1,0:T(8,128)(2,1)S(1)}, u32[]{:S(2)}, u32[]{:S(2)}) collective-permute-start(bf16[960,256]{1,0:T(8,128)(2,1)S(1)} %collective-permute-done.1.refs_1_), channel_id=1, source_target_pairs={{0,192},{64,0},{128,64},{192,128},{1,193},{65,1},{129,65},{193,129... | collective-permute-start | bytes 1474568 | tf_op jit(solution)/shard_map/ppermute | solution.py:20
  45.0 15.8 %collective-permute-start.9 = (bf16[960,256]{1,0:T(8,128)(2,1)S(1)}, bf16[960,256]{1,0:T(8,128)(2,1)S(1)}, u32[]{:S(2)}, u32[]{:S(2)}) collective-permute-start(bf16[960,256]{1,0:T(8,128)(2,1)S(1)} %collective-permute-done.1.refs_1_), channel_id=1, source_target_pairs={{0,64},{64,128},{128,192},{192,0},{1,65},{65,129},{129,193},{193,1... | collective-permute-start | bytes 1474568 | tf_op jit(solution)/shard_map/ppermute | solution.py:20
  46.0 21.3 %collective-permute-start.6 = (bf16[960,256]{1,0:T(8,128)(2,1)S(1)}, bf16[960,256]{1,0:T(8,128)(2,1)S(1)}, u32[]{:S(2)}, u32[]{:S(2)}) collective-permute-start(bf16[960,256]{1,0:T(8,128)(2,1)S(1)} %collective-permute-done.4.refs_4_.refs_0_), channel_id=1, source_target_pairs={{0,64},{64,128},{128,192},{192,0},{1,65},{65,129},{129,193},{193,1... | collective-permute-start | bytes 1474568 | tf_op jit(solution)/shard_map/ppermute | solution.py:20
  47.6 16.1 %collective-permute-start.15 = (bf16[480,256]{1,0:T(8,128)(2,1)S(1)}, bf16[480,256]{1,0:T(8,128)(2,1)S(1)}, u32[]{:S(2)}, u32[]{:S(2)}) collective-permute-start(bf16[480,256]{1,0:T(8,128)(2,1)S(1)} %get-tuple-element.37), channel_id=1, source_target_pairs={{0,192},{64,0},{128,64},{192,128},{1,193},{65,1},{129,65},{193,129... | collective-permute-start | bytes 737288 | tf_op jit(solution)/shard_map/ppermute | solution.py:20
  55.5 30.1 %copy-start.2 = (f32[80,128]{1,0:T(8,128)S(1)}, f32[80,128]{1,0:T(8,128)}, u32[]{:S(2)}) copy-start(f32[80,128]{1,0:T(8,128)} %param.8) | copy-start | bytes 122884
  55.5 11.8 %collective-permute-start.16 = (bf16[480,256]{1,0:T(8,128)(2,1)S(1)}, bf16[480,256]{1,0:T(8,128)(2,1)S(1)}, u32[]{:S(2)}, u32[]{:S(2)}) collective-permute-start(bf16[480,256]{1,0:T(8,128)(2,1)S(1)} %get-tuple-element.36), channel_id=1, source_target_pairs={{0,192},{64,0},{128,64},{192,128},{1,193},{65,1},{129,65},{193,129... | collective-permute-start | bytes 737288 | tf_op jit(solution)/shard_map/ppermute | solution.py:20
  60.7 26.6 %collective-permute-start.12 = (bf16[960,256]{1,0:T(8,128)(2,1)S(1)}, bf16[960,256]{1,0:T(8,128)(2,1)S(1)}, u32[]{:S(2)}, u32[]{:S(2)}) collective-permute-start(bf16[960,256]{1,0:T(8,128)(2,1)S(1)} %collective-permute-done.11.refs_2_), channel_id=1, source_target_pairs={{0,32},{32,0},{1,33},{33,1},{2,34},{34,2},{3,35},{35,3},{4,36},{36... | collective-permute-start | bytes 1474568 | tf_op jit(solution)/shard_map/ppermute | solution.py:20
  63.8 13.6 %collective-permute-start.17 = (bf16[480,256]{1,0:T(8,128)(2,1)S(1)}, bf16[480,256]{1,0:T(8,128)(2,1)S(1)}, u32[]{:S(2)}, u32[]{:S(2)}) collective-permute-start(bf16[480,256]{1,0:T(8,128)(2,1)S(1)} %collective-permute-done.15.refs_6_.refs_2_), channel_id=1, source_target_pairs={{0,32},{32,0},{1,33},{33,1},{2,34},{34,2},{3,35},{35,3},{4,36},{36... | collective-permute-start | bytes 737288 | tf_op jit(solution)/shard_map/ppermute | solution.py:20
  67.3 20.0 %collective-permute-start.13 = (bf16[960,256]{1,0:T(8,128)(2,1)S(1)}, bf16[960,256]{1,0:T(8,128)(2,1)S(1)}, u32[]{:S(2)}, u32[]{:S(2)}) collective-permute-start(bf16[960,256]{1,0:T(8,128)(2,1)S(1)} %collective-permute-done.5.refs_5_.refs_1_), channel_id=1, source_target_pairs={{0,64},{64,128},{128,192},{192,0},{1,65},{65,129},{129,193},{193,1... | collective-permute-start | bytes 1474568 | tf_op jit(solution)/shard_map/ppermute | solution.py:20
  67.3 20.0 %collective-permute-start.14 = (bf16[960,256]{1,0:T(8,128)(2,1)S(1)}, bf16[960,256]{1,0:T(8,128)(2,1)S(1)}, u32[]{:S(2)}, u32[]{:S(2)}) collective-permute-start(bf16[960,256]{1,0:T(8,128)(2,1)S(1)} %collective-permute-done.5.refs_5_.refs_1_), channel_id=1, source_target_pairs={{0,192},{64,0},{128,64},{192,128},{1,193},{65,1},{129,65},{193,129... | collective-permute-start | bytes 1474568 | tf_op jit(solution)/shard_map/ppermute | solution.py:20
  77.4 9.9 %collective-permute-start.18 = (bf16[480,256]{1,0:T(8,128)(2,1)S(1)}, bf16[480,256]{1,0:T(8,128)(2,1)S(1)}, u32[]{:S(2)}, u32[]{:S(2)}) collective-permute-start(bf16[480,256]{1,0:T(8,128)(2,1)S(1)} %collective-permute-done.16.refs_7_.refs_3_), channel_id=1, source_target_pairs={{0,32},{32,0},{1,33},{33,1},{2,34},{34,2},{3,35},{35,3},{4,36},{36... | collective-permute-start | bytes 737288 | tf_op jit(solution)/shard_map/ppermute | solution.py:20
  94.2 7.2 %copy-start.1 = (s32[192,192]{1,0:T(8,128)S(1)}, s32[192,192]{1,0:T(8,128)}, u32[]{:S(2)}) copy-start(s32[192,192]{1,0:T(8,128)} %mask.1) | copy-start | bytes 442372
  100.7 5.2 %collective-permute-start.20 = (f32[96,384]{1,0:T(8,128)S(1)}, f32[96,384]{1,0:T(8,128)S(1)}, u32[]{:S(2)}, u32[]{:S(2)}) collective-permute-start(f32[96,384]{1,0:T(8,128)S(1)} %partial_scores.1), channel_id=1, source_target_pairs={{0,1},{1,0},{2,3},{3,2},{4,5},{5,4},{6,7},{7,6},{8,9},{9,8},{10,11... | collective-permute-start | bytes 442376 | tf_op jit(solution)/shard_map/ppermute | solution.py:20
  101.6 1.3 collective-permute-start
  106.3 4.8 %collective-permute-start.21 = (f32[2,384]{1,0:T(2,128)S(1)}, f32[2,384]{1,0:T(2,128)S(1)}, u32[]{:S(2)}, u32[]{:S(2)}) collective-permute-start(f32[2,384]{1,0:T(2,128)S(1)} %fusion.16), channel_id=1, source_target_pairs={{0,6},{2,4},{4,2},{6,0},{8,14},{10,12},{12,10},{14,8},{16,22},{18,... | collective-permute-start | bytes 9224 | tf_op jit(solution)/shard_map/ppermute | solution.py:324
  108.2 4.5 %collective-permute-start.22 = (f32[2,384]{1,0:T(2,128)S(1)}, f32[2,384]{1,0:T(2,128)S(1)}, u32[]{:S(2)}, u32[]{:S(2)}) collective-permute-start(f32[2,384]{1,0:T(2,128)S(1)} %fusion.16), channel_id=1, source_target_pairs={{0,4},{2,6},{4,0},{6,2},{8,12},{10,14},{12,8},{14,10},{16,20},{18,... | collective-permute-start | bytes 9224 | tf_op jit(solution)/shard_map/ppermute | solution.py:324
  109.7 3.6 %collective-permute-start.23 = (f32[2,384]{1,0:T(2,128)S(1)}, f32[2,384]{1,0:T(2,128)S(1)}, u32[]{:S(2)}, u32[]{:S(2)}) collective-permute-start(f32[2,384]{1,0:T(2,128)S(1)} %fusion.16), channel_id=1, source_target_pairs={{0,2},{2,0},{4,6},{6,4},{8,10},{10,8},{12,14},{14,12},{16,18},{18,... | collective-permute-start | bytes 9224 | tf_op jit(solution)/shard_map/ppermute | solution.py:324
  113.3 10.9 %collective-permute-start.24 = (f32[2,384]{1,0:T(2,128)S(1)}, f32[2,384]{1,0:T(2,128)S(1)}, u32[]{:S(2)}, u32[]{:S(2)}) collective-permute-start(f32[2,384]{1,0:T(2,128)S(1)} %pad_maximum_fusion.3), channel_id=1, source_target_pairs={{0,28},{2,30},{4,24},{6,26},{8,20},{10,22},{12,16},{14,18},{16,12}... | collective-permute-start | bytes 9224 | tf_op jit(solution)/shard_map/ppermute | solution.py:324
  113.6 10.7 %collective-permute-start.25 = (f32[2,384]{1,0:T(2,128)S(1)}, f32[2,384]{1,0:T(2,128)S(1)}, u32[]{:S(2)}, u32[]{:S(2)}) collective-permute-start(f32[2,384]{1,0:T(2,128)S(1)} %pad_maximum_fusion.3), channel_id=1, source_target_pairs={{0,12},{2,14},{4,8},{6,10},{8,4},{10,6},{12,0},{14,2},{16,28},{18,... | collective-permute-start | bytes 9224 | tf_op jit(solution)/shard_map/ppermute | solution.py:324
  118.3 5.9 %collective-permute-start.26 = (f32[2,384]{1,0:T(2,128)S(1)}, f32[2,384]{1,0:T(2,128)S(1)}, u32[]{:S(2)}, u32[]{:S(2)}) collective-permute-start(f32[2,384]{1,0:T(2,128)S(1)} %pad_maximum_fusion.3), channel_id=1, source_target_pairs={{0,16},{2,18},{4,20},{6,22},{8,24},{10,26},{12,28},{14,30},{16,0},... | collective-permute-start | bytes 9224 | tf_op jit(solution)/shard_map/ppermute | solution.py:324
  131.2 5.3 %collective-permute-start.27 = (bf16[128,256]{1,0:T(8,128)(2,1)S(1)}, bf16[128,256]{1,0:T(8,128)(2,1)S(1)}, u32[]{:S(2)}, u32[]{:S(2)}) collective-permute-start(bf16[128,256]{1,0:T(8,128)(2,1)S(1)} %get-tuple-element.38), channel_id=1, source_target_pairs={{0,1},{1,0},{16,17},{17,16},{2,3},{3,2},{18,19},{19,18},{4,5},{5,4... | collective-permute-start | bytes 196616 | tf_op jit(solution)/shard_map/ppermute | solution.py:324
  132.1 4.4 %collective-permute-start.28 = (bf16[128,256]{1,0:T(8,128)(2,1)S(1)}, bf16[128,256]{1,0:T(8,128)(2,1)S(1)}, u32[]{:S(2)}, u32[]{:S(2)}) collective-permute-start(bf16[128,256]{1,0:T(8,128)(2,1)S(1)} %get-tuple-element.40), channel_id=1, source_target_pairs={{0,16},{1,17},{16,0},{17,1},{2,18},{3,19},{18,2},{19,3},{4,20},{5,... | collective-permute-start | bytes 196616 | tf_op jit(solution)/shard_map/ppermute | solution.py:324
  132.3 4.6 %collective-permute-start.29 = (bf16[128,256]{1,0:T(8,128)(2,1)S(1)}, bf16[128,256]{1,0:T(8,128)(2,1)S(1)}, u32[]{:S(2)}, u32[]{:S(2)}) collective-permute-start(bf16[128,256]{1,0:T(8,128)(2,1)S(1)} %get-tuple-element.39), channel_id=1, source_target_pairs={{0,17},{1,16},{16,1},{17,0},{2,19},{3,18},{18,3},{19,2},{4,21},{5,... | collective-permute-start | bytes 196616 | tf_op jit(solution)/shard_map/ppermute | solution.py:324
  137.6 19.7 %all-to-all-start = ((bf16[64,2,256]{2,1,0:T(2,128)(2,1)}), bf16[64,2,256]{2,1,0:T(2,128)(2,1)S(1)}, u32[]{:S(2)}, u32[]{:S(2)}) async-start(bf16[64,2,256]{2,1,0:T(2,128)(2,1)} %reshape.57), calls=%async_computation | async-start | bytes 131072 | tf_op jit(solution)/shard_map/all_to_all | solution.py:398
